TPU v7x, 128 devices: a whole 4x4x4 slice. The times are simulated.
128 devices in a mesh: cp: 64 (over x, z, y), hd: 2 (over core).
Axes of the slice: x: 4, y: 4, z: 4, core: 2. Of those that a mesh axis runs over, the one named last changes fastest.
Arguments:
- queries: bfloat16 [12288, 4096], P('cp', 'hd'), may hold values from -48 to 48
- keys: bfloat16 [12288, 1024], P('cp', 'hd'), may hold values from -48 to 48
- values: bfloat16 [12288, 1024], P('cp', 'hd'), may hold values from -6 to 6
- span_table: int32 [128], replicated, may hold values from 0 to 127, as said below
- doc_ids: int32 [12288], replicated, may hold values from 0 to 7, never falling along the last dimension, each value on 1 to 3072 neighbouring positions
- out_weight: bfloat16 [4096, 4096], P('hd'), may hold values from -0.09375 to 0.09375
Outputs:
- mixed: bfloat16 [12288, 4096], P(('cp', 'hd'))
Inputs may be any that keep to these rules, and one draw needn't show every extreme that they name: `span_table`: slots 2 j and 2 j + 1 hold two spans c and 127 - c, and every span is held once.
All inputs are finite; a program needn't handle non-finite values.
Results may differ from a plain program's by a relative error of at most 0.0095.
Values may be sent and summed in bfloat16 or wider, within the bound.
No kernel may reach another device: no remote copies, remote signals or barrier semaphores. Data moves between devices by JAX's collectives and lax.ppermute only.
A program may use at most 128 MiB of HBM per device.

v0:
```python
import jax
import jax.numpy as jnp
from jax import lax
from jax.experimental import pallas as pl
from jax.experimental.pallas import tpu as pltpu
from jax.sharding import Mesh, PartitionSpec as P

HEAD = 128
SPAN = 96
RING = 4
GROUP = 4
ROWS = GROUP * SPAN
DOCS = 8
LOW = -1e30
LOG2E = 1.4426950408889634
FACTOR = HEAD ** -0.5 * LOG2E
MAX_TASKS = 160

PHASES = (((0, 0), (0, 1)), ((1, 0), (1, 1), (3, 0), (3, 1)), ((2, 0), (2, 1)))
CHUNKS = (256, 512, 256)


def shift(value, axis, by):
    return lax.ppermute(value, axis, [(i, (i + by) % RING) for i in range(RING)])


def phase_kernel(phase, *refs):
    chunk = CHUNKS[phase]
    first_phase, last_phase = phase == 0, phase == 2
    order = PHASES[phase]
    refs = list(refs)

    def take(n):
        out = refs[:n]
        del refs[:n]
        return out

    coords, table, starts, rank = take(4)
    pieces = take(2 * len(order))
    if first_phase:
        q_parts = take(4)
    else:
        (q_all,) = take(1)
        take(2)
    if phase == 1:
        (weight,) = take(1)
    if first_phase:
        (q_all,) = take(1)
    best_all, acc_all = take(2)
    if last_phase:
        outs = take(8)
    if phase == 1:
        (weight_held,) = take(1)
        weight_copy = pltpu.make_async_copy(weight, weight_held, refs.pop())
        weight_copy.start()
    kv, low_all, high_all, s0, s1, p0, p1, f0, f1, task_span, task_first, task_upper = refs
    x, z, y, core = coords[0], coords[1], coords[2], coords[3]

    def slot_of(dx, dz, dy, half):
        cp = ((x + RING - dx) % RING) * 16 + ((z + RING - dz) % RING) * 4 + (y + RING - dy) % RING
        return 2 * cp + half

    for family in range(2):
        for index, (far, upper_block) in enumerate(order):
            ref = pieces[family * len(order) + index]
            for i in range(8):
                near = 2 * upper_block + i // 4
                dy = 2 * family + (i // 2) % 2
                dx, dz = (far, near) if family == 0 else (near, far)
                row = rank[table[slot_of(dx, dz, dy, i % 2)]] * SPAN
                kv[pl.ds(pl.multiple_of(row, SPAN), SPAN), :] = ref[i * SPAN : (i + 1) * SPAN, :]

    if first_phase:
        for s, ref in enumerate(q_parts):
            for half in range(2):
                for h in range(GROUP):
                    q_all[2 * s + half, h * SPAN : (h + 1) * SPAN, :] = ref[
                        half * SPAN : (half + 1) * SPAN, h * HEAD : (h + 1) * HEAD
                    ]
        best_all[...] = jnp.full(best_all.shape, LOW, jnp.float32)
        acc_all[...] = jnp.zeros(acc_all.shape, jnp.float32)

    doc_low = []
    for d in range(DOCS):
        span = starts[d] // SPAN
        doc_low.append(rank[span] * SPAN + (rank[span + 1] - rank[span]) * (starts[d] - span * SPAN))

    def plan(i, total):
        span = table[slot_of(0, 0, i // 2, i % 2)]
        row = lax.broadcasted_iota(jnp.int32, (SPAN, HEAD), 0)
        low = jnp.full((SPAN, HEAD), doc_low[0], jnp.int32)
        low_min = doc_low[0]
        for d in range(1, DOCS):
            low = jnp.where(row >= starts[d] - span * SPAN, doc_low[d], low)
            low_min = jnp.where(starts[d] <= span * SPAN, doc_low[d], low_min)
        low_all[i] = low
        base, top = rank[span] * SPAN, rank[span + 1] * SPAN
        high_all[i] = jnp.where(top > base, base + row, base - 1)

        def add(e, n):
            task_span[n] = i
            task_upper[n] = top - e * chunk
            task_first[n] = jnp.maximum(top - (e + 1) * chunk, 0)
            return n + 1

        return lax.fori_loop(0, (top - low_min + chunk - 1) // chunk, add, total)

    total = lax.fori_loop(0, 8, plan, 1)
    task_span[0] = 0
    task_first[0] = 0
    for extra in range(3):
        task_span[total + extra] = 0
        task_first[total + extra] = 0
        task_upper[total + extra] = 0

    p1[...] = jnp.zeros(p1.shape, jnp.bfloat16)
    f1[...] = jnp.ones(f1.shape, jnp.float32)
    ones = jnp.ones((chunk, HEAD), jnp.bfloat16)
    lanes = chunk // HEAD

    def score(t, out):
        k = kv[pl.ds(pl.multiple_of(task_first[t], 32), chunk), :HEAD]
        out[...] = lax.dot_general(
            q_all[task_span[t]], k, (((1,), (1,)), ((), ())), preferred_element_type=jnp.float32
        )

    def weigh(t, s_ref, p_ref, f_ref):
        i, k0 = task_span[t], task_first[t]
        low = low_all[i] - k0
        high = jnp.minimum(high_all[i], task_upper[t] - 1) - k0
        lane = lax.broadcasted_iota(jnp.int32, (SPAN, HEAD), 1)
        seen = [(lane >= low - g * HEAD) & (lane <= high - g * HEAD) for g in range(lanes)]
        for h in range(GROUP):
            at = slice(h * SPAN, (h + 1) * SPAN)
            s = [
                jnp.where(seen[g], s_ref[at, g * HEAD : (g + 1) * HEAD], 2 * LOW) for g in range(lanes)
            ]
            top = s[0]
            for g in range(1, lanes):
                top = jnp.maximum(top, s[g])
            best = best_all[i, at, :]
            new_best = jnp.maximum(best, jnp.max(top, axis=1, keepdims=True))
            best_all[i, at, :] = new_best
            f_ref[at, :] = jnp.exp2((best - new_best) * FACTOR)
            for g in range(lanes):
                p_ref[at, g * HEAD : (g + 1) * HEAD] = jnp.exp2((s[g] - new_best) * FACTOR).astype(
                    jnp.bfloat16
                )

    def accumulate(t, p_ref, f_ref):
        i, k0 = task_span[t], pl.multiple_of(task_first[t], 32)
        v = jnp.concatenate([kv[pl.ds(k0, chunk), HEAD:], ones], axis=1)
        part = jnp.dot(p_ref[...], v, preferred_element_type=jnp.float32)
        fade = f_ref[...]
        for half in range(2):
            cols = slice(half * HEAD, (half + 1) * HEAD)
            acc_all[i, :, cols] = acc_all[i, :, cols] * fade + part[:, cols]

    score(1, s0)

    def pair(j, _):
        t = 2 * j + 1
        accumulate(t - 1, p1, f1)
        score(t + 1, s1)
        weigh(t, s0, p0, f0)
        accumulate(t, p0, f0)
        score(t + 2, s0)
        weigh(t + 1, s1, p1, f1)
        return 0

    pairs = total // 2
    lax.fori_loop(0, pairs, pair, 0)
    accumulate(2 * pairs, p1, f1)

    if phase == 1:
        weight_copy.wait()
    if last_phase:
        for turn in range(2):
            half = 1 - core if turn == 0 else core
            for s in range(RING):
                i = 2 * s + half
                for h in range(GROUP):
                    at = slice(h * SPAN, (h + 1) * SPAN)
                    outs[4 * turn + s][:, h * HEAD : (h + 1) * HEAD] = (
                        acc_all[i, at, :HEAD] / acc_all[i, at, HEAD:]
                    ).astype(jnp.bfloat16)


def run_phase(phase, scalars, pieces, others, weight=None):
    smem = pl.BlockSpec(memory_space=pltpu.SMEM)
    vmem = pl.BlockSpec(memory_space=pltpu.VMEM)
    chunk = CHUNKS[phase]
    keys = sum(piece.shape[0] for piece in pieces)
    state = [((8, ROWS, HEAD), jnp.float32), ((8, ROWS, 2 * HEAD), jnp.float32)]
    far = [] if weight is None else [weight]
    held = [(w.shape, w.dtype) for w in far]
    if phase == 0:
        outs = [((8, ROWS, HEAD), jnp.bfloat16)] + state + held
        aliases = {}
    else:
        outs = state + held
        first = 4 + len(pieces) + 1
        aliases = {first: 0, first + 1: 1}
    if phase == 2:
        outs = outs + [((SPAN, GROUP * HEAD), jnp.bfloat16)] * 8
    scratch = [
        pltpu.VMEM((keys, 2 * HEAD), jnp.bfloat16),
        pltpu.VMEM((8, SPAN, HEAD), jnp.int32),
        pltpu.VMEM((8, SPAN, HEAD), jnp.int32),
        pltpu.VMEM((ROWS, chunk), jnp.float32),
        pltpu.VMEM((ROWS, chunk), jnp.float32),
        pltpu.VMEM((ROWS, chunk), jnp.bfloat16),
        pltpu.VMEM((ROWS, chunk), jnp.bfloat16),
        pltpu.VMEM((ROWS, HEAD), jnp.float32),
        pltpu.VMEM((ROWS, HEAD), jnp.float32),
        pltpu.SMEM((MAX_TASKS,), jnp.int32),
        pltpu.SMEM((MAX_TASKS,), jnp.int32),
        pltpu.SMEM((MAX_TASKS,), jnp.int32),
    ] + [pltpu.SemaphoreType.DMA] * len(far)
    share = len(pieces) / 16
    return pl.pallas_call(
        lambda *refs: phase_kernel(phase, *refs),
        out_shape=[jax.ShapeDtypeStruct(*o) for o in outs],
        in_specs=[smem] * 4
        + [vmem] * (len(pieces) + len(others))
        + [pl.BlockSpec(memory_space=pltpu.HBM)] * len(far),
        out_specs=[vmem] * len(outs),
        scratch_shapes=scratch,
        input_output_aliases=aliases,
        compiler_params=pltpu.CompilerParams(vmem_limit_bytes=16 * 1024 * 1024),
        cost_estimate=pl.CostEstimate(
            flops=int(8e9 * share), bytes_accessed=int(1e7 * share), transcendentals=int(1e7 * share)
        ),
    )(*scalars, *pieces, *others, *far)


def project_kernel(coords, o0, o1, o2, o3, w, out):
    y = coords[2]
    block = 512
    for n in range(w.shape[1] // block):
        cols = slice(n * block, (n + 1) * block)
        acc = None
        for s, ref in enumerate((o0, o1, o2, o3)):
            row = pl.multiple_of(((y + s) % RING) * 512, 512)
            part = jnp.dot(ref[...], w[pl.ds(row, 512), cols], preferred_element_type=jnp.float32)
            acc = part if acc is None else acc + part
        out[:, cols] = acc.astype(out.dtype)


def project(coords, o_parts, weight, dtype):
    smem = pl.BlockSpec(memory_space=pltpu.SMEM)
    vmem = pl.BlockSpec(memory_space=pltpu.VMEM)
    width = weight.shape[1]
    return pl.pallas_call(
        project_kernel,
        out_shape=jax.ShapeDtypeStruct((SPAN, width), dtype),
        in_specs=[smem] + [vmem] * 5,
        out_specs=vmem,
        compiler_params=pltpu.CompilerParams(vmem_limit_bytes=16 * 1024 * 1024),
        cost_estimate=pl.CostEstimate(
            flops=2 * SPAN * 2048 * width, bytes_accessed=2048 * width * 2, transcendentals=0
        ),
        name="project",
    )(coords, *o_parts, weight)


def layer(queries, keys, values, span_table, doc_ids, out_weight):
    rows = queries.shape[0]
    spans = span_table.shape[0]
    x, z, y, core = (lax.axis_index(a) for a in ("x", "z", "y", "hd"))
    coords = jnp.stack([x, z, y, core]).astype(jnp.int32)
    kv = jnp.concatenate([keys.reshape(rows, RING, HEAD), values.reshape(rows, RING, HEAD)], axis=2)
    kv = kv.transpose(1, 0, 2)
    part = [lax.dynamic_index_in_dim(kv, (y + s) % RING, 0, keepdims=False) for s in range(RING)]
    part = [part[0]] + [shift(part[s], "y", s) for s in range(1, RING)]
    low, high = jnp.concatenate(part[:2], 0), jnp.concatenate(part[2:], 0)

    q_part = [
        lax.dynamic_slice_in_dim(queries, ((y + s) % RING) * 512, 512, 1) for s in range(RING)
    ]
    q_part = [q_part[0]] + [shift(q_part[s], "y", s) for s in range(1, RING)]

    def gathered(block, near_axis, far_axis):
        near = [block] + [shift(block, near_axis, s) for s in range(1, RING)]
        first, second = jnp.concatenate(near[:2], 0), jnp.concatenate(near[2:], 0)
        ahead_first = shift(first, far_axis, 1)
        behind_second = shift(second, far_axis, -1)
        ahead_second = shift(second, far_axis, 1)
        behind_first = shift(first, far_axis, -1)
        far_first = shift(ahead_first, far_axis, 1)
        far_second = shift(behind_second, far_axis, -1)
        return [first, second], [ahead_first, ahead_second, behind_first, behind_second], [far_first, far_second]

    pieces = [a + b for a, b in zip(gathered(low, "z", "x"), gathered(high, "x", "z"))]

    docs = jnp.arange(DOCS, dtype=jnp.int32)
    starts = jnp.sum((doc_ids[None, :] < docs[:, None]).astype(jnp.int32), axis=1)
    slot = jnp.arange(spans, dtype=jnp.int32)
    cp = slot // 2
    dx, dz, dy = (x - cp // 16) % RING, (z - (cp // 4) % 4) % RING, (y - cp % 4) % RING
    far = jnp.where(dy < 2, dx, dz)
    phase_of = jnp.where(far == 0, 0, jnp.where(far == 2, 2, 1))
    before = span_table[None, :] < jnp.arange(spans + 8, dtype=jnp.int32)[:, None]
    ranks = [jnp.sum((before & (phase_of == p)[None, :]).astype(jnp.int32), axis=1) for p in range(3)]

    scalars = [coords, span_table, starts]
    q_all, best, acc = run_phase(0, scalars + [ranks[0]], pieces[0], q_part)
    best, acc, weight = run_phase(1, scalars + [ranks[1]], pieces[1], [q_all, best, acc], out_weight)
    o_part = run_phase(2, scalars + [ranks[2]], pieces[2], [q_all, best, acc])[2:]

    def returned(part):
        return [part[0]] + [shift(part[s], "y", -s) for s in range(1, RING)]

    theirs, ours = returned(o_part[:4]), returned(o_part[4:])
    sent = lax.ppermute(project(coords, theirs, weight, jnp.bfloat16), "hd", [(0, 1), (1, 0)])
    kept = project(coords, ours, weight, jnp.float32)
    return (kept + sent.astype(jnp.float32)).astype(jnp.bfloat16)


def solution(mesh):
    inner = Mesh(mesh.devices.reshape(RING, RING, RING, 2), ("x", "z", "y", "hd"))
    cp = ("x", "z", "y")
    return jax.shard_map(
        layer,
        mesh=inner,
        in_specs=(P(cp, "hd"), P(cp, "hd"), P(cp, "hd"), P(), P(), P("hd", None)),
        out_specs=P(cp + ("hd",), None),
        check_vma=False,
    )
```

profile of v0, /device:TPU:1, one launch (start us, length us, event | category | flops | bytes accessed | tf_op | source)
XLA Modules:
  0.0 113.6 jit_solution(10578536781273195917)
XLA Ops:
  0.0 0.9 copy-done
  1.0 1.0 bitcast_dynamic-update-slice_fusion
  2.0 3.8 %collective-permute-start.8 = (bf16[192,256]{1,0:T(8,128)(2,1)S(1)}, bf16[192,256]{1,0:T(8,128)(2,1)S(1)}, u32[]{:S(2)}, u32[]{:S(2)}) collective-permute-start(bf16[192,256]{1,0:T(8,128)(2,1)S(1)} %get-tuple-element.43), channel_id=1, source_target_pairs={{0,4},{2,6},{4,0},{6,2},{1,5},{3,7},{5,1},{7,3},{8,12},{10,14},{12... | collective-permute-start | bytes 294920 | tf_op jit(solution)/shard_map/ppermute | solution.py:24
  5.8 0.8 collective-permute-start.9
  6.6 0.7 collective-permute-start
  8.5 1.8 %collective-permute-done.9 = bf16[192,256]{1,0:T(8,128)(2,1)S(1)} collective-permute-done((bf16[192,256]{1,0:T(8,128)(2,1)S(1)}, bf16[192,256]{1,0:T(8,128)(2,1)S(1)}, u32[]{:S(2)}, u32[]{:S(2)}) %collective-permute-start.9) | collective-permute-done | bytes 98336 | tf_op jit(solution)/shard_map/ppermute | solution.py:24
  11.0 2.7 %collective-permute-start.13 = (bf16[384,256]{1,0:T(8,128)(2,1)S(1)}, bf16[384,256]{1,0:T(8,128)(2,1)S(1)}, u32[]{:S(2)}, u32[]{:S(2)}) collective-permute-start(bf16[384,256]{1,0:T(8,128)(2,1)S(1)} %get-tuple-element.46), channel_id=1, source_target_pairs={{0,64},{32,96},{64,0},{96,32},{1,65},{33,97},{65,1},{97,33},{2,66}... | collective-permute-start | bytes 589832 | tf_op jit(solution)/shard_map/ppermute | solution.py:24
  13.7 0.9 collective-permute-start.14
  15.3 3.7 %collective-permute-start.4 = (bf16[384,256]{1,0:T(8,128)(2,1)S(1)}, bf16[384,256]{1,0:T(8,128)(2,1)S(1)}, u32[]{:S(2)}, u32[]{:S(2)}) collective-permute-start(bf16[384,256]{1,0:T(8,128)(2,1)S(1)} %pad_maximum_fusion.1), channel_id=1, source_target_pairs={{0,16},{8,24},{16,0},{24,8},{1,17},{9,25},{17,1},{25,9},{2,18},{10... | collective-permute-start | bytes 589832 | tf_op jit(solution)/shard_map/ppermute | solution.py:24
  19.0 0.7 collective-permute-start.1
  19.7 2.0 %collective-permute-done.14 = bf16[384,256]{1,0:T(8,128)(2,1)S(1)} collective-permute-done((bf16[384,256]{1,0:T(8,128)(2,1)S(1)}, bf16[384,256]{1,0:T(8,128)(2,1)S(1)}, u32[]{:S(2)}, u32[]{:S(2)}) %collective-permute-start.14) | collective-permute-done | bytes 196640 | tf_op jit(solution)/shard_map/ppermute | solution.py:24
  21.8 3.8 %collective-permute-start.15 = (bf16[768,256]{1,0:T(8,128)(2,1)S(1)}, bf16[768,256]{1,0:T(8,128)(2,1)S(1)}, u32[]{:S(2)}, u32[]{:S(2)}) collective-permute-start(bf16[768,256]{1,0:T(8,128)(2,1)S(1)} %constant_dynamic-update-slice_fusion.7.refs_7_), channel_id=1, source_target_pairs={{0,24},{8,0},{16,8},{24,16},{1,25},{9,1},{17,9},{25,17},{2,26},{10... | collective-permute-start | bytes 1179656 | tf_op jit(solution)/shard_map/ppermute | solution.py:24
  25.6 1.5 %collective-permute-done.1 = bf16[384,256]{1,0:T(8,128)(2,1)S(1)} collective-permute-done((bf16[384,256]{1,0:T(8,128)(2,1)S(1)}, bf16[384,256]{1,0:T(8,128)(2,1)S(1)}, u32[]{:S(2)}, u32[]{:S(2)}) %collective-permute-start.1) | collective-permute-done | bytes 196640 | tf_op jit(solution)/shard_map/ppermute | solution.py:24
  27.1 2.7 %collective-permute-start.5 = (bf16[384,256]{1,0:T(8,128)(2,1)S(1)}, bf16[384,256]{1,0:T(8,128)(2,1)S(1)}, u32[]{:S(2)}, u32[]{:S(2)}) collective-permute-start(bf16[384,256]{1,0:T(8,128)(2,1)S(1)} %pad_maximum_fusion.1), channel_id=1, source_target_pairs={{0,24},{8,0},{16,8},{24,16},{1,25},{9,1},{17,9},{25,17},{2,26},{10... | collective-permute-start | bytes 589832 | tf_op jit(solution)/shard_map/ppermute | solution.py:24
  30.5 1.7 %collective-permute-start.18 = (bf16[192,512]{1,0:T(8,128)(2,1)S(1)}, bf16[192,512]{1,0:T(8,128)(2,1)S(1)}, u32[]{:S(2)}, u32[]{:S(2)}) collective-permute-start(bf16[192,512]{1,0:T(8,128)(2,1)S(1)} %get-tuple-element.41), channel_id=1, source_target_pairs={{0,4},{2,6},{4,0},{6,2},{1,5},{3,7},{5,1},{7,3},{8,12},{10,14},{12... | collective-permute-start | bytes 589832 | tf_op jit(solution)/shard_map/ppermute | solution.py:24
  32.2 2.3 %collective-permute-start.19 = (bf16[192,512]{1,0:T(8,128)(2,1)S(1)}, bf16[192,512]{1,0:T(8,128)(2,1)S(1)}, u32[]{:S(2)}, u32[]{:S(2)}) collective-permute-start(bf16[192,512]{1,0:T(8,128)(2,1)S(1)} %get-tuple-element.38), channel_id=1, source_target_pairs={{0,6},{2,0},{4,2},{6,4},{1,7},{3,1},{5,3},{7,5},{8,14},{10,8},{12,... | collective-permute-start | bytes 589832 | tf_op jit(solution)/shard_map/ppermute | solution.py:24
  34.5 0.7 constant_dynamic-update-slice_fusion.4.refs_6_
  35.2 2.1 %collective-permute-done.5 = bf16[384,256]{1,0:T(8,128)(2,1)S(1)} collective-permute-done((bf16[384,256]{1,0:T(8,128)(2,1)S(1)}, bf16[384,256]{1,0:T(8,128)(2,1)S(1)}, u32[]{:S(2)}, u32[]{:S(2)}) %collective-permute-start.5) | collective-permute-done | bytes 196640 | tf_op jit(solution)/shard_map/ppermute | solution.py:24
  37.4 0.7 constant_dynamic-update-slice_fusion.refs_5_
  38.7 2.7 %collective-permute-start.23 = (bf16[768,256]{1,0:T(8,128)(2,1)}, bf16[768,256]{1,0:T(8,128)(2,1)S(1)}, u32[]{:S(2)}, u32[]{:S(2)}) collective-permute-start(bf16[768,256]{1,0:T(8,128)(2,1)} %constant_dynamic-update-slice_fusion.4.refs_6_), channel_id=1, source_target_pairs={{0,24},{8,0},{16,8},{24,16},{1,25},{9,1},{17,9},{25,17},{2,26},{10... | collective-permute-start | bytes 1179656 | tf_op jit(solution)/shard_map/ppermute | solution.py:24
  42.1 3.3 %collective-permute-start.20 = (bf16[768,256]{1,0:T(8,128)(2,1)}, bf16[768,256]{1,0:T(8,128)(2,1)S(1)}, u32[]{:S(2)}, u32[]{:S(2)}) collective-permute-start(bf16[768,256]{1,0:T(8,128)(2,1)} %constant_dynamic-update-slice_fusion.refs_5_), channel_id=1, source_target_pairs={{0,32},{32,64},{64,96},{96,0},{1,33},{33,65},{65,97},{97,1},{2,34}... | collective-permute-start | bytes 1179656 | tf_op jit(solution)/shard_map/ppermute | solution.py:24
  45.4 0.8 collective-permute-start.6
  46.2 0.7 collective-permute-start.2
  47.1 4.7 %collective-permute-start.21 = (bf16[768,256]{1,0:T(8,128)(2,1)S(1)}, bf16[768,256]{1,0:T(8,128)(2,1)S(1)}, u32[]{:S(2)}, u32[]{:S(2)}) collective-permute-start(bf16[768,256]{1,0:T(8,128)(2,1)S(1)} %pad_maximum_fusion.refs_4_), channel_id=1, source_target_pairs={{0,96},{32,0},{64,32},{96,64},{1,97},{33,1},{65,33},{97,65},{2,98}... | collective-permute-start | bytes 1179656 | tf_op jit(solution)/shard_map/ppermute | solution.py:24
  51.8 1.0 convert_reduce_fusion.refs_2_
  52.9 1.3 %collective-permute-start.16 = (bf16[768,256]{1,0:T(8,128)(2,1)S(1)}, bf16[768,256]{1,0:T(8,128)(2,1)S(1)}, u32[]{:S(2)}, u32[]{:S(2)}) collective-permute-start(bf16[768,256]{1,0:T(8,128)(2,1)S(1)} %collective-permute-done.15.refs_11_), channel_id=1, source_target_pairs={{0,24},{8,0},{16,8},{24,16},{1,25},{9,1},{17,9},{25,17},{2,26},{10... | collective-permute-start | bytes 1179656 | tf_op jit(solution)/shard_map/ppermute | solution.py:24
  54.4 1.6 %collective-permute-start.7 = (bf16[768,256]{1,0:T(8,128)(2,1)S(1)}, bf16[768,256]{1,0:T(8,128)(2,1)S(1)}, u32[]{:S(2)}, u32[]{:S(2)}) collective-permute-start(bf16[768,256]{1,0:T(8,128)(2,1)S(1)} %collective-permute-done.6.refs_7_), channel_id=1, source_target_pairs={{0,96},{32,0},{64,32},{96,64},{1,97},{33,1},{65,33},{97,65},{2,98}... | collective-permute-start | bytes 1179656 | tf_op jit(solution)/shard_map/ppermute | solution.py:24
  56.0 6.0 %collective-permute-done.2.refs_4_ = bf16[768,256]{1,0:T(8,128)(2,1)S(1)} collective-permute-done((bf16[768,256]{1,0:T(8,128)(2,1)S(1)}, bf16[768,256]{1,0:T(8,128)(2,1)S(1)}, u32[]{:S(2)}, u32[]{:S(2)}) %collective-permute-start.2) | collective-permute-done | bytes 393248 | tf_op jit(solution)/shard_map/ppermute | solution.py:24
  62.6 1.0 copy-done.2
  63.6 0.9 copy-done.5
  64.6 0.9 copy-done.7
  65.5 0.9 copy-done.9
  66.4 5.5 %shard_map.64 = (bf16[8,384,128]{2,1,0:T(8,128)(2,1)S(1)}, f32[8,384,128]{2,1,0:T(8,128)S(1)}, f32[8,384,256]{2,1,0:T(8,128)S(1)}) custom-call(s32[4]{0:T(128)S(1)} %pad_add_fusion.refs_0_.coords, s32[128]{0:T(128)S(1)} %copy-done.3, s32[8]{0:T(128)S(1)} %convert_reduce_fusion.refs_2_, s32[136]{0:T(256)S(1)} %get-tuple-element.34.refs_3_, ...), custom_call_target="tpu_custom_call" | custom-call | flops 2000000000 | bytes 2500000 | tf_op jit(solution)/shard_map/pallas_call | solution.py:221
  72.0 6.6 %shard_map.65 = (f32[8,384,128]{2,1,0:T(8,128)S(1)}, f32[8,384,256]{2,1,0:T(8,128)S(1)}, bf16[2048,4096]{1,0:T(8,128)(2,1)S(1)}) custom-call(s32[4]{0:T(128)S(1)} %pad_add_fusion.refs_0_.coords, s32[128]{0:T(128)S(1)} %copy-done.3, s32[8]{0:T(128)S(1)} %convert_reduce_fusion.refs_2_, ...), custom_call_target="tpu_custom_call", output_to_operand_aliasing={{0}: (13, {}), {1}: (14, {})} | custom-call | flops 4000000000 | bytes 5000000 | tf_op jit(solution)/shard_map/pallas_call | solution.py:221
  78.6 4.4 %shard_map.66 = (f32[8,384,128]{2,1,0:T(8,128)S(1)}, f32[8,384,256]{2,1,0:T(8,128)S(1)}, bf16[96,512]{1,0:T(8,128)(2,1)S(1)}, bf16[96,512]{1,0:T(8,128)(2,1)S(1)...) custom-call(s32[4]{0:T(128)S(1)} %pad_add_fusion.refs_0_.coords, ...), custom_call_target="tpu_custom_call", output_to_operand_aliasing={{0}: (9, {}), {1}: (10, {})} | custom-call | flops 2000000000 | bytes 2500000 | tf_op jit(solution)/shard_map/pallas_call | solution.py:221
  83.0 3.8 %collective-permute-start.27 = (bf16[96,512]{1,0:T(8,128)(2,1)S(1)}, bf16[96,512]{1,0:T(8,128)(2,1)S(1)}, u32[]{:S(2)}, u32[]{:S(2)}) collective-permute-start(bf16[96,512]{1,0:T(8,128)(2,1)S(1)} %get-tuple-element.30), channel_id=1, source_target_pairs={{0,6},{2,0},{4,2},{6,4},{1,7},{3,1},{5,3},{7,5},{8,14},{10,8},{12,... | collective-permute-start | bytes 294920 | tf_op jit(solution)/shard_map/ppermute | solution.py:24
  86.8 0.9 collective-permute-start.28
  87.7 1.7 %collective-permute-done.27.o1 = bf16[96,512]{1,0:T(8,128)(2,1)S(1)} collective-permute-done((bf16[96,512]{1,0:T(8,128)(2,1)S(1)}, bf16[96,512]{1,0:T(8,128)(2,1)S(1)}, u32[]{:S(2)}, u32[]{:S(2)}) %collective-permute-start.27) | collective-permute-done | bytes 98336 | tf_op jit(solution)/shard_map/ppermute | solution.py:24
  89.4 2.4 %collective-permute-done.28.o2 = bf16[96,512]{1,0:T(8,128)(2,1)S(1)} collective-permute-done((bf16[96,512]{1,0:T(8,128)(2,1)S(1)}, bf16[96,512]{1,0:T(8,128)(2,1)S(1)}, u32[]{:S(2)}, u32[]{:S(2)}) %collective-permute-start.28) | collective-permute-done | bytes 98336 | tf_op jit(solution)/shard_map/ppermute | solution.py:24
  91.8 1.0 collective-permute-done.29.o3
  92.8 3.5 %project.3 = bf16[96,4096]{1,0:T(8,128)(2,1)S(1)} custom-call(s32[4]{0:T(128)S(1)} %pad_add_fusion.refs_0_.coords, bf16[96,512]{1,0:T(8,128)(2,1)S(1)} %get-tuple-element.29.o0, bf16[96,512]{1,0:T(8,128)(2,1)S(1)} %collective-permute-done.27.o1, bf16[96,512]{1,0:T(8,128)(2,1)S(1)} %collective-permute-done.28.o2, ...), custom_call_target="tpu_custom_call" | custom-call | flops 1610612736 | bytes 16777216 | tf_op jit(solution)/shard_map/project/pallas_call | solution.py:254
  96.4 4.2 %collective-permute-start.30 = (bf16[96,4096]{1,0:T(8,128)(2,1)S(1)}, bf16[96,4096]{1,0:T(8,128)(2,1)S(1)}, u32[]{:S(2)}, u32[]{:S(2)}) collective-permute-start(bf16[96,4096]{1,0:T(8,128)(2,1)S(1)} %project.3), channel_id=1, source_target_pairs={{0,1},{1,0},{2,3},{3,2},{4,5},{5,4},{6,7},{7,6},{8,9},{9,8},{10,11... | collective-permute-start | bytes 2359304 | tf_op jit(solution)/shard_map/ppermute | solution.py:315
  100.8 0.9 collective-permute-start.25
  102.3 2.6 %collective-permute-done.24.o1 = bf16[96,512]{1,0:T(8,128)(2,1)S(1)} collective-permute-done((bf16[96,512]{1,0:T(8,128)(2,1)S(1)}, bf16[96,512]{1,0:T(8,128)(2,1)S(1)}, u32[]{:S(2)}, u32[]{:S(2)}) %collective-permute-start.24) | collective-permute-done | bytes 98336 | tf_op jit(solution)/shard_map/ppermute | solution.py:24
  104.8 1.5 %collective-permute-done.25.o2 = bf16[96,512]{1,0:T(8,128)(2,1)S(1)} collective-permute-done((bf16[96,512]{1,0:T(8,128)(2,1)S(1)}, bf16[96,512]{1,0:T(8,128)(2,1)S(1)}, u32[]{:S(2)}, u32[]{:S(2)}) %collective-permute-start.25) | collective-permute-done | bytes 98336 | tf_op jit(solution)/shard_map/ppermute | solution.py:24
  106.3 2.8 %collective-permute-done.26.o3 = bf16[96,512]{1,0:T(8,128)(2,1)S(1)} collective-permute-done((bf16[96,512]{1,0:T(8,128)(2,1)S(1)}, bf16[96,512]{1,0:T(8,128)(2,1)S(1)}, u32[]{:S(2)}, u32[]{:S(2)}) %collective-permute-start.26) | collective-permute-done | bytes 98336 | tf_op jit(solution)/shard_map/ppermute | solution.py:24
  109.2 3.4 %project.2 = f32[96,4096]{1,0:T(8,128)S(1)} custom-call(s32[4]{0:T(128)S(1)} %pad_add_fusion.refs_0_.coords, bf16[96,512]{1,0:T(8,128)(2,1)S(1)} %get-tuple-element.24.o0, bf16[96,512]{1,0:T(8,128)(2,1)S(1)} %collective-permute-done.24.o1, bf16[96,512]{1,0:T(8,128)(2,1)S(1)} %collective-permute-done.25.o2, bf16[96,512]{1,0:T(8,128)(2,1)S(1)} %collective-permute-done.26.o3, ...), custom_call_target="tpu_custom_call" | custom-call | flops 1610612736 | bytes 16777216 | tf_op jit(solution)/shard_map/project/pallas_call | solution.py:254
  112.6 1.1 add_convert_fusion
  (60 shorter events, 6.8 us)
Async XLA Ops:
  0.0 0.9 copy-start
  0.0 7.3 %copy-start.10 = (bf16[192,2048]{1,0:T(8,128)(2,1)S(1)}, bf16[192,2048]{1,0:T(8,128)(2,1)}, u32[]{:S(2)}) copy-start(bf16[192,2048]{1,0:T(8,128)(2,1)} %param.6) | copy-start | bytes 2359300
  2.0 5.8 %collective-permute-start.8 = (bf16[192,256]{1,0:T(8,128)(2,1)S(1)}, bf16[192,256]{1,0:T(8,128)(2,1)S(1)}, u32[]{:S(2)}, u32[]{:S(2)}) collective-permute-start(bf16[192,256]{1,0:T(8,128)(2,1)S(1)} %get-tuple-element.43), channel_id=1, source_target_pairs={{0,4},{2,6},{4,0},{6,2},{1,5},{3,7},{5,1},{7,3},{8,12},{10,14},{12... | collective-permute-start | bytes 294920 | tf_op jit(solution)/shard_map/ppermute | solution.py:24
  5.8 4.4 %collective-permute-start.9 = (bf16[192,256]{1,0:T(8,128)(2,1)S(1)}, bf16[192,256]{1,0:T(8,128)(2,1)S(1)}, u32[]{:S(2)}, u32[]{:S(2)}) collective-permute-start(bf16[192,256]{1,0:T(8,128)(2,1)S(1)} %get-tuple-element.42), channel_id=1, source_target_pairs={{0,6},{2,0},{4,2},{6,4},{1,7},{3,1},{5,3},{7,5},{8,14},{10,8},{12,... | collective-permute-start | bytes 294920 | tf_op jit(solution)/shard_map/ppermute | solution.py:24
  6.6 8.6 %collective-permute-start = (bf16[192,256]{1,0:T(8,128)(2,1)S(1)}, bf16[192,256]{1,0:T(8,128)(2,1)S(1)}, u32[]{:S(2)}, u32[]{:S(2)}) collective-permute-start(bf16[192,256]{1,0:T(8,128)(2,1)S(1)} %get-tuple-element.44), channel_id=1, source_target_pairs={{0,2},{2,4},{4,6},{6,0},{1,3},{3,5},{5,7},{7,1},{8,10},{10,12},{12... | collective-permute-start | bytes 294920 | tf_op jit(solution)/shard_map/ppermute | solution.py:24
  7.4 23.1 %collective-permute-start.17 = (bf16[192,512]{1,0:T(8,128)(2,1)S(1)}, bf16[192,512]{1,0:T(8,128)(2,1)S(1)}, u32[]{:S(2)}, u32[]{:S(2)}) collective-permute-start(bf16[192,512]{1,0:T(8,128)(2,1)S(1)} %get-tuple-element.39), channel_id=1, source_target_pairs={{0,2},{2,4},{4,6},{6,0},{1,3},{3,5},{5,7},{7,1},{8,10},{10,12},{12... | collective-permute-start | bytes 589832 | tf_op jit(solution)/shard_map/ppermute | solution.py:24
  11.0 8.0 %collective-permute-start.13 = (bf16[384,256]{1,0:T(8,128)(2,1)S(1)}, bf16[384,256]{1,0:T(8,128)(2,1)S(1)}, u32[]{:S(2)}, u32[]{:S(2)}) collective-permute-start(bf16[384,256]{1,0:T(8,128)(2,1)S(1)} %get-tuple-element.46), channel_id=1, source_target_pairs={{0,64},{32,96},{64,0},{96,32},{1,65},{33,97},{65,1},{97,33},{2,66}... | collective-permute-start | bytes 589832 | tf_op jit(solution)/shard_map/ppermute | solution.py:24
  13.7 8.0 %collective-permute-start.14 = (bf16[384,256]{1,0:T(8,128)(2,1)S(1)}, bf16[384,256]{1,0:T(8,128)(2,1)S(1)}, u32[]{:S(2)}, u32[]{:S(2)}) collective-permute-start(bf16[384,256]{1,0:T(8,128)(2,1)S(1)} %get-tuple-element.46), channel_id=1, source_target_pairs={{0,96},{32,0},{64,32},{96,64},{1,97},{33,1},{65,33},{97,65},{2,98}... | collective-permute-start | bytes 589832 | tf_op jit(solution)/shard_map/ppermute | solution.py:24
  14.7 17.6 %collective-permute-start.10 = (bf16[384,256]{1,0:T(8,128)(2,1)S(1)}, bf16[384,256]{1,0:T(8,128)(2,1)S(1)}, u32[]{:S(2)}, u32[]{:S(2)}) collective-permute-start(bf16[384,256]{1,0:T(8,128)(2,1)S(1)} %get-tuple-element.46), channel_id=1, source_target_pairs={{0,32},{32,64},{64,96},{96,0},{1,33},{33,65},{65,97},{97,1},{2,34}... | collective-permute-start | bytes 589832 | tf_op jit(solution)/shard_map/ppermute | solution.py:24
  15.3 31.6 %copy-start.3 = (s32[128]{0:T(128)S(1)}, s32[128]{0:T(128)}, u32[]{:S(2)}) copy-start(s32[128]{0:T(128)} %refs_1_.5) | copy-start | bytes 1540
  15.3 11.8 %collective-permute-start.4 = (bf16[384,256]{1,0:T(8,128)(2,1)S(1)}, bf16[384,256]{1,0:T(8,128)(2,1)S(1)}, u32[]{:S(2)}, u32[]{:S(2)}) collective-permute-start(bf16[384,256]{1,0:T(8,128)(2,1)S(1)} %pad_maximum_fusion.1), channel_id=1, source_target_pairs={{0,16},{8,24},{16,0},{24,8},{1,17},{9,25},{17,1},{25,9},{2,18},{10... | collective-permute-start | bytes 589832 | tf_op jit(solution)/shard_map/ppermute | solution.py:24
  19.0 8.1 %collective-permute-start.1 = (bf16[384,256]{1,0:T(8,128)(2,1)S(1)}, bf16[384,256]{1,0:T(8,128)(2,1)S(1)}, u32[]{:S(2)}, u32[]{:S(2)}) collective-permute-start(bf16[384,256]{1,0:T(8,128)(2,1)S(1)} %pad_maximum_fusion.1), channel_id=1, source_target_pairs={{0,8},{8,16},{16,24},{24,0},{1,9},{9,17},{17,25},{25,1},{2,10},{10... | collective-permute-start | bytes 589832 | tf_op jit(solution)/shard_map/ppermute | solution.py:24
  21.8 24.4 %copy-start.1 = (bf16[768,256]{1,0:T(8,128)(2,1)}, bf16[768,256]{1,0:T(8,128)(2,1)S(1)}, u32[]{:S(2)}) copy-start(bf16[768,256]{1,0:T(8,128)(2,1)S(1)} %constant_dynamic-update-slice_fusion.7.refs_7_) | copy-start | bytes 1179652
  21.8 23.6 %collective-permute-start.15 = (bf16[768,256]{1,0:T(8,128)(2,1)S(1)}, bf16[768,256]{1,0:T(8,128)(2,1)S(1)}, u32[]{:S(2)}, u32[]{:S(2)}) collective-permute-start(bf16[768,256]{1,0:T(8,128)(2,1)S(1)} %constant_dynamic-update-slice_fusion.7.refs_7_), channel_id=1, source_target_pairs={{0,24},{8,0},{16,8},{24,16},{1,25},{9,1},{17,9},{25,17},{2,26},{10... | collective-permute-start | bytes 1179656 | tf_op jit(solution)/shard_map/ppermute | solution.py:24
  27.1 19.1 %collective-permute-start.22 = (bf16[768,256]{1,0:T(8,128)(2,1)S(1)}, bf16[768,256]{1,0:T(8,128)(2,1)S(1)}, u32[]{:S(2)}, u32[]{:S(2)}) collective-permute-start(bf16[768,256]{1,0:T(8,128)(2,1)S(1)} %constant_dynamic-update-slice_fusion.7.refs_7_), channel_id=1, source_target_pairs={{0,8},{8,16},{16,24},{24,0},{1,9},{9,17},{17,25},{25,1},{2,10},{10... | collective-permute-start | bytes 1179656 | tf_op jit(solution)/shard_map/ppermute | solution.py:24
  27.1 10.3 %collective-permute-start.5 = (bf16[384,256]{1,0:T(8,128)(2,1)S(1)}, bf16[384,256]{1,0:T(8,128)(2,1)S(1)}, u32[]{:S(2)}, u32[]{:S(2)}) collective-permute-start(bf16[384,256]{1,0:T(8,128)(2,1)S(1)} %pad_maximum_fusion.1), channel_id=1, source_target_pairs={{0,24},{8,0},{16,8},{24,16},{1,25},{9,1},{17,9},{25,17},{2,26},{10... | collective-permute-start | bytes 589832 | tf_op jit(solution)/shard_map/ppermute | solution.py:24
  30.5 10.9 %copy-start.4 = (bf16[192,512]{1,0:T(8,128)(2,1)}, bf16[192,512]{1,0:T(8,128)(2,1)S(1)}, u32[]{:S(2)}) copy-start(bf16[192,512]{1,0:T(8,128)(2,1)S(1)} %collective-permute-done.17.refs_9_) | copy-start | bytes 589828
  30.5 7.5 %collective-permute-start.18 = (bf16[192,512]{1,0:T(8,128)(2,1)S(1)}, bf16[192,512]{1,0:T(8,128)(2,1)S(1)}, u32[]{:S(2)}, u32[]{:S(2)}) collective-permute-start(bf16[192,512]{1,0:T(8,128)(2,1)S(1)} %get-tuple-element.41), channel_id=1, source_target_pairs={{0,4},{2,6},{4,0},{6,2},{1,5},{3,7},{5,1},{7,3},{8,12},{10,14},{12... | collective-permute-start | bytes 589832 | tf_op jit(solution)/shard_map/ppermute | solution.py:24
  32.2 9.2 %collective-permute-start.19 = (bf16[192,512]{1,0:T(8,128)(2,1)S(1)}, bf16[192,512]{1,0:T(8,128)(2,1)S(1)}, u32[]{:S(2)}, u32[]{:S(2)}) collective-permute-start(bf16[192,512]{1,0:T(8,128)(2,1)S(1)} %get-tuple-element.38), channel_id=1, source_target_pairs={{0,6},{2,0},{4,2},{6,4},{1,7},{3,1},{5,3},{7,5},{8,14},{10,8},{12,... | collective-permute-start | bytes 589832 | tf_op jit(solution)/shard_map/ppermute | solution.py:24
  37.4 9.7 %collective-permute-start.11 = (bf16[768,256]{1,0:T(8,128)(2,1)}, bf16[768,256]{1,0:T(8,128)(2,1)S(1)}, u32[]{:S(2)}, u32[]{:S(2)}) collective-permute-start(bf16[768,256]{1,0:T(8,128)(2,1)} %constant_dynamic-update-slice_fusion.4.refs_6_), channel_id=1, source_target_pairs={{0,8},{8,16},{16,24},{24,0},{1,9},{9,17},{17,25},{25,1},{2,10},{10... | collective-permute-start | bytes 1179656 | tf_op jit(solution)/shard_map/ppermute | solution.py:24
  38.1 0.7 copy-start.6
  38.7 14.1 %collective-permute-start.23 = (bf16[768,256]{1,0:T(8,128)(2,1)}, bf16[768,256]{1,0:T(8,128)(2,1)S(1)}, u32[]{:S(2)}, u32[]{:S(2)}) collective-permute-start(bf16[768,256]{1,0:T(8,128)(2,1)} %constant_dynamic-update-slice_fusion.4.refs_6_), channel_id=1, source_target_pairs={{0,24},{8,0},{16,8},{24,16},{1,25},{9,1},{17,9},{25,17},{2,26},{10... | collective-permute-start | bytes 1179656 | tf_op jit(solution)/shard_map/ppermute | solution.py:24
  41.4 0.7 copy-start.8
  42.1 12.0 %collective-permute-start.20 = (bf16[768,256]{1,0:T(8,128)(2,1)}, bf16[768,256]{1,0:T(8,128)(2,1)S(1)}, u32[]{:S(2)}, u32[]{:S(2)}) collective-permute-start(bf16[768,256]{1,0:T(8,128)(2,1)} %constant_dynamic-update-slice_fusion.refs_5_), channel_id=1, source_target_pairs={{0,32},{32,64},{64,96},{96,0},{1,33},{33,65},{65,97},{97,1},{2,34}... | collective-permute-start | bytes 1179656 | tf_op jit(solution)/shard_map/ppermute | solution.py:24
  45.4 9.0 %collective-permute-start.6 = (bf16[768,256]{1,0:T(8,128)(2,1)}, bf16[768,256]{1,0:T(8,128)(2,1)S(1)}, u32[]{:S(2)}, u32[]{:S(2)}) collective-permute-start(bf16[768,256]{1,0:T(8,128)(2,1)} %constant_dynamic-update-slice_fusion.refs_5_), channel_id=1, source_target_pairs={{0,96},{32,0},{64,32},{96,64},{1,97},{33,1},{65,33},{97,65},{2,98}... | collective-permute-start | bytes 1179656 | tf_op jit(solution)/shard_map/ppermute | solution.py:24
  46.2 15.8 %collective-permute-start.2 = (bf16[768,256]{1,0:T(8,128)(2,1)S(1)}, bf16[768,256]{1,0:T(8,128)(2,1)S(1)}, u32[]{:S(2)}, u32[]{:S(2)}) collective-permute-start(bf16[768,256]{1,0:T(8,128)(2,1)S(1)} %pad_maximum_fusion.refs_4_), channel_id=1, source_target_pairs={{0,32},{32,64},{64,96},{96,0},{1,33},{33,65},{65,97},{97,1},{2,34}... | collective-permute-start | bytes 1179656 | tf_op jit(solution)/shard_map/ppermute | solution.py:24
  47.1 24.9 %collective-permute-start.21 = (bf16[768,256]{1,0:T(8,128)(2,1)S(1)}, bf16[768,256]{1,0:T(8,128)(2,1)S(1)}, u32[]{:S(2)}, u32[]{:S(2)}) collective-permute-start(bf16[768,256]{1,0:T(8,128)(2,1)S(1)} %pad_maximum_fusion.refs_4_), channel_id=1, source_target_pairs={{0,96},{32,0},{64,32},{96,64},{1,97},{33,1},{65,33},{97,65},{2,98}... | collective-permute-start | bytes 1179656 | tf_op jit(solution)/shard_map/ppermute | solution.py:24
  52.9 25.7 %collective-permute-start.16 = (bf16[768,256]{1,0:T(8,128)(2,1)S(1)}, bf16[768,256]{1,0:T(8,128)(2,1)S(1)}, u32[]{:S(2)}, u32[]{:S(2)}) collective-permute-start(bf16[768,256]{1,0:T(8,128)(2,1)S(1)} %collective-permute-done.15.refs_11_), channel_id=1, source_target_pairs={{0,24},{8,0},{16,8},{24,16},{1,25},{9,1},{17,9},{25,17},{2,26},{10... | collective-permute-start | bytes 1179656 | tf_op jit(solution)/shard_map/ppermute | solution.py:24
  54.1 24.5 %collective-permute-start.12 = (bf16[768,256]{1,0:T(8,128)(2,1)S(1)}, bf16[768,256]{1,0:T(8,128)(2,1)S(1)}, u32[]{:S(2)}, u32[]{:S(2)}) collective-permute-start(bf16[768,256]{1,0:T(8,128)(2,1)S(1)} %collective-permute-done.11.refs_8_), channel_id=1, source_target_pairs={{0,8},{8,16},{16,24},{24,0},{1,9},{9,17},{17,25},{25,1},{2,10},{10... | collective-permute-start | bytes 1179656 | tf_op jit(solution)/shard_map/ppermute | solution.py:24
  54.4 24.2 %collective-permute-start.7 = (bf16[768,256]{1,0:T(8,128)(2,1)S(1)}, bf16[768,256]{1,0:T(8,128)(2,1)S(1)}, u32[]{:S(2)}, u32[]{:S(2)}) collective-permute-start(bf16[768,256]{1,0:T(8,128)(2,1)S(1)} %collective-permute-done.6.refs_7_), channel_id=1, source_target_pairs={{0,96},{32,0},{64,32},{96,64},{1,97},{33,1},{65,33},{97,65},{2,98}... | collective-permute-start | bytes 1179656 | tf_op jit(solution)/shard_map/ppermute | solution.py:24
  62.0 16.6 %collective-permute-start.3 = (bf16[768,256]{1,0:T(8,128)(2,1)S(1)}, bf16[768,256]{1,0:T(8,128)(2,1)S(1)}, u32[]{:S(2)}, u32[]{:S(2)}) collective-permute-start(bf16[768,256]{1,0:T(8,128)(2,1)S(1)} %collective-permute-done.2.refs_4_), channel_id=1, source_target_pairs={{0,32},{32,64},{64,96},{96,0},{1,33},{33,65},{65,97},{97,1},{2,34}... | collective-permute-start | bytes 1179656 | tf_op jit(solution)/shard_map/ppermute | solution.py:24
  62.6 1.0 copy-start.2
  63.6 0.9 copy-start.5
  64.6 0.9 copy-start.7
  65.5 0.9 copy-start.9
  83.0 6.4 %collective-permute-start.27 = (bf16[96,512]{1,0:T(8,128)(2,1)S(1)}, bf16[96,512]{1,0:T(8,128)(2,1)S(1)}, u32[]{:S(2)}, u32[]{:S(2)}) collective-permute-start(bf16[96,512]{1,0:T(8,128)(2,1)S(1)} %get-tuple-element.30), channel_id=1, source_target_pairs={{0,6},{2,0},{4,2},{6,4},{1,7},{3,1},{5,3},{7,5},{8,14},{10,8},{12,... | collective-permute-start | bytes 294920 | tf_op jit(solution)/shard_map/ppermute | solution.py:24
  86.8 5.0 %collective-permute-start.28 = (bf16[96,512]{1,0:T(8,128)(2,1)S(1)}, bf16[96,512]{1,0:T(8,128)(2,1)S(1)}, u32[]{:S(2)}, u32[]{:S(2)}) collective-permute-start(bf16[96,512]{1,0:T(8,128)(2,1)S(1)} %get-tuple-element.31), channel_id=1, source_target_pairs={{0,4},{2,6},{4,0},{6,2},{1,5},{3,7},{5,1},{7,3},{8,12},{10,14},{12... | collective-permute-start | bytes 294920 | tf_op jit(solution)/shard_map/ppermute | solution.py:24
  87.7 5.2 %collective-permute-start.29 = (bf16[96,512]{1,0:T(8,128)(2,1)S(1)}, bf16[96,512]{1,0:T(8,128)(2,1)S(1)}, u32[]{:S(2)}, u32[]{:S(2)}) collective-permute-start(bf16[96,512]{1,0:T(8,128)(2,1)S(1)} %get-tuple-element.32), channel_id=1, source_target_pairs={{0,2},{2,4},{4,6},{6,0},{1,3},{3,5},{5,7},{7,1},{8,10},{10,12},{12... | collective-permute-start | bytes 294920 | tf_op jit(solution)/shard_map/ppermute | solution.py:24
  96.4 16.2 %collective-permute-start.30 = (bf16[96,4096]{1,0:T(8,128)(2,1)S(1)}, bf16[96,4096]{1,0:T(8,128)(2,1)S(1)}, u32[]{:S(2)}, u32[]{:S(2)}) collective-permute-start(bf16[96,4096]{1,0:T(8,128)(2,1)S(1)} %project.3), channel_id=1, source_target_pairs={{0,1},{1,0},{2,3},{3,2},{4,5},{5,4},{6,7},{7,6},{8,9},{9,8},{10,11... | collective-permute-start | bytes 2359304 | tf_op jit(solution)/shard_map/ppermute | solution.py:315
  100.6 4.3 %collective-permute-start.24 = (bf16[96,512]{1,0:T(8,128)(2,1)S(1)}, bf16[96,512]{1,0:T(8,128)(2,1)S(1)}, u32[]{:S(2)}, u32[]{:S(2)}) collective-permute-start(bf16[96,512]{1,0:T(8,128)(2,1)S(1)} %get-tuple-element.25), channel_id=1, source_target_pairs={{0,6},{2,0},{4,2},{6,4},{1,7},{3,1},{5,3},{7,5},{8,14},{10,8},{12,... | collective-permute-start | bytes 294920 | tf_op jit(solution)/shard_map/ppermute | solution.py:24
  100.8 5.5 %collective-permute-start.25 = (bf16[96,512]{1,0:T(8,128)(2,1)S(1)}, bf16[96,512]{1,0:T(8,128)(2,1)S(1)}, u32[]{:S(2)}, u32[]{:S(2)}) collective-permute-start(bf16[96,512]{1,0:T(8,128)(2,1)S(1)} %get-tuple-element.26), channel_id=1, source_target_pairs={{0,4},{2,6},{4,0},{6,2},{1,5},{3,7},{5,1},{7,3},{8,12},{10,14},{12... | collective-permute-start | bytes 294920 | tf_op jit(solution)/shard_map/ppermute | solution.py:24
  101.7 7.5 %collective-permute-start.26 = (bf16[96,512]{1,0:T(8,128)(2,1)S(1)}, bf16[96,512]{1,0:T(8,128)(2,1)S(1)}, u32[]{:S(2)}, u32[]{:S(2)}) collective-permute-start(bf16[96,512]{1,0:T(8,128)(2,1)S(1)} %get-tuple-element.27), channel_id=1, source_target_pairs={{0,2},{2,4},{4,6},{6,0},{1,3},{3,5},{5,7},{7,1},{8,10},{10,12},{12... | collective-permute-start | bytes 294920 | tf_op jit(solution)/shard_map/ppermute | solution.py:24
where the time goes:
time: 115 us; the launch traced here: 114 us
  starting transfers between devices  51.5 us (45%)
  waiting for transfers between devices  25.5 us (22%)
  Pallas kernels  23.4 us (20%)
  local copies, waits for them, and re-layouts  10.6 us (9%)
  other arithmetic  2.44 us (2%)
    ppermute x30, starting transfers between devices, shift(): lax.ppermute(value, axis, [(i, (i + by) % RING) for i in range(RING)])  47.3 us
    ppermute x30, waiting for transfers between devices, shift(): lax.ppermute(value, axis, [(i, (i + by) % RING) for i in range(RING)])  25.5 us
    pallas_call x3, Pallas kernels, run_phase(): pl.pallas_call(lambda *refs: phase_kernel(phase, *refs), out_shape=[jax.S...  16.5 us
    unnamed x26, local copies, waits for them, and re-layouts  7.48 us
    pallas_call x2, Pallas kernels, project(): pl.pallas_call(project_kernel, out_shape=jax.ShapeDtypeStruct((SPAN, widt...  6.9 us
    ppermute x1, starting transfers between devices, layer(): lax.ppermute(project(coords, theirs, weight, jnp.bfloat16), 'hd', [(0, 1)...  4.2 us
  transfers between devices with their start and end apart: 31, of which 11 were waited for; matrix products, arithmetic and copies ran while one was open for 4% of the time, Pallas kernels for 14%

commit v1 on v0

--- a/solution.py
+++ b/solution.py
@@ -16,8 +16,8 @@
 FACTOR = HEAD ** -0.5 * LOG2E
 MAX_TASKS = 160
 
-PHASES = (((0, 0), (0, 1)), ((1, 0), (1, 1), (3, 0), (3, 1)), ((2, 0), (2, 1)))
-CHUNKS = (256, 512, 256)
+PHASES = (((0, 0), (0, 1)), ((1, 0), (3, 1)), ((1, 1), (3, 0)), ((2, 0), (2, 1)))
+CHUNKS = (256, 256, 256, 256)
 
 
 def shift(value, axis, by):
@@ -26,7 +26,7 @@
 
 def phase_kernel(phase, *refs):
     chunk = CHUNKS[phase]
-    first_phase, last_phase = phase == 0, phase == 2
+    first_phase, last_phase = phase == 0, phase == 3
     order = PHASES[phase]
     refs = list(refs)
 
@@ -201,7 +201,7 @@
         outs = state + held
         first = 4 + len(pieces) + 1
         aliases = {first: 0, first + 1: 1}
-    if phase == 2:
+    if phase == 3:
         outs = outs + [((SPAN, GROUP * HEAD), jnp.bfloat16)] * 8
     scratch = [
         pltpu.VMEM((keys, 2 * HEAD), jnp.bfloat16),
@@ -289,7 +289,7 @@
         behind_first = shift(first, far_axis, -1)
         far_first = shift(ahead_first, far_axis, 1)
         far_second = shift(behind_second, far_axis, -1)
-        return [first, second], [ahead_first, ahead_second, behind_first, behind_second], [far_first, far_second]
+        return [first, second], [ahead_first, behind_second], [ahead_second, behind_first], [far_first, far_second]
 
     pieces = [a + b for a, b in zip(gathered(low, "z", "x"), gathered(high, "x", "z"))]
 
@@ -298,15 +298,17 @@
     slot = jnp.arange(spans, dtype=jnp.int32)
     cp = slot // 2
     dx, dz, dy = (x - cp // 16) % RING, (z - (cp // 4) % 4) % RING, (y - cp % 4) % RING
-    far = jnp.where(dy < 2, dx, dz)
-    phase_of = jnp.where(far == 0, 0, jnp.where(far == 2, 2, 1))
+    far, near = jnp.where(dy < 2, dx, dz), jnp.where(dy < 2, dz, dx)
+    early = (far == 1) == (near < 2)
+    phase_of = jnp.where(far == 0, 0, jnp.where(far == 2, 3, jnp.where(early, 1, 2)))
     before = span_table[None, :] < jnp.arange(spans + 8, dtype=jnp.int32)[:, None]
-    ranks = [jnp.sum((before & (phase_of == p)[None, :]).astype(jnp.int32), axis=1) for p in range(3)]
+    ranks = [jnp.sum((before & (phase_of == p)[None, :]).astype(jnp.int32), axis=1) for p in range(4)]
 
     scalars = [coords, span_table, starts]
     q_all, best, acc = run_phase(0, scalars + [ranks[0]], pieces[0], q_part)
     best, acc, weight = run_phase(1, scalars + [ranks[1]], pieces[1], [q_all, best, acc], out_weight)
-    o_part = run_phase(2, scalars + [ranks[2]], pieces[2], [q_all, best, acc])[2:]
+    best, acc = run_phase(2, scalars + [ranks[2]], pieces[2], [q_all, best, acc])
+    o_part = run_phase(3, scalars + [ranks[3]], pieces[3], [q_all, best, acc])[2:]
 
     def returned(part):
         return [part[0]] + [shift(part[s], "y", -s) for s in range(1, RING)]

time: 115 us -> 121 us (1.052)
  waiting for transfers between devices: 25.5 us -> 32.8 us
  Pallas kernels: 23.4 us -> 27.5 us
  local copies, waits for them, and re-layouts: 10.6 us -> 6.98 us
  starting transfers between devices: 51.5 us -> 49.1 us
  other arithmetic: 2.44 us -> 3.67 us
    ppermute x30, waiting for transfers between devices: 25.5 us -> 32.8 us  [shift(): lax.ppermute(value, axis, [(i, (i + by) % RING) for i in range(RING)])]
    pallas_call x3 -> x4, Pallas kernels: 16.5 us -> 20.6 us  [run_phase(): pl.pallas_call(lambda *refs: phase_kernel(phase, *refs), out_shape=[jax.S...]
    ppermute x30, starting transfers between devices: 47.3 us -> 44.9 us  [shift(): lax.ppermute(value, axis, [(i, (i + by) % RING) for i in range(RING)])]
    unnamed x26 -> x22, local copies, waits for them, and re-layouts: 7.48 us -> 5.82 us
    concatenate x3, local copies, waits for them, and re-layouts: 1.4 us -> 0.04 us  [gathered(): first, second = (jnp.concatenate(near[:2], 0), jnp.concatenate(near[2:], 0))]
  transfers between devices with their start and end apart: 31 -> 31, of which waited for: 11 -> 13; matrix products, arithmetic and copies ran while one was open for 4% -> 2% of each run, Pallas kernels for 14% -> 16%
where the time goes in v1:
time: 121 us; the launch traced here: 120 us
  starting transfers between devices  49.1 us (41%)
  waiting for transfers between devices  32.8 us (27%)
  Pallas kernels  27.5 us (23%)
  local copies, waits for them, and re-layouts  6.98 us (6%)
  other arithmetic  3.67 us (3%)
    ppermute x30, starting transfers between devices, shift(): lax.ppermute(value, axis, [(i, (i + by) % RING) for i in range(RING)])  44.9 us
    ppermute x30, waiting for transfers between devices, shift(): lax.ppermute(value, axis, [(i, (i + by) % RING) for i in range(RING)])  32.8 us
    pallas_call x4, Pallas kernels, run_phase(): pl.pallas_call(lambda *refs: phase_kernel(phase, *refs), out_shape=[jax.S...  20.6 us
    pallas_call x2, Pallas kernels, project(): pl.pallas_call(project_kernel, out_shape=jax.ShapeDtypeStruct((SPAN, widt...  6.89 us
    unnamed x22, local copies, waits for them, and re-layouts  5.82 us
    ppermute x1, starting transfers between devices, layer(): lax.ppermute(project(coords, theirs, weight, jnp.bfloat16), 'hd', [(0, 1)...  4.16 us
  transfers between devices with their start and end apart: 31, of which 13 were waited for; matrix products, arithmetic and copies ran while one was open for 2% of the time, Pallas kernels for 16%

profile of v1, /device:TPU:1, one launch (start us, length us, event | category | flops | bytes accessed | tf_op | source)
XLA Modules:
  0.0 120.3 jit_solution(3559284089107950631)
XLA Ops:
  0.0 0.9 copy-done
  1.0 1.0 bitcast_dynamic-update-slice_fusion
  2.0 3.8 %collective-permute-start.8 = (bf16[192,256]{1,0:T(8,128)(2,1)S(1)}, bf16[192,256]{1,0:T(8,128)(2,1)S(1)}, u32[]{:S(2)}, u32[]{:S(2)}) collective-permute-start(bf16[192,256]{1,0:T(8,128)(2,1)S(1)} %get-tuple-element.48), channel_id=1, source_target_pairs={{0,4},{2,6},{4,0},{6,2},{1,5},{3,7},{5,1},{7,3},{8,12},{10,14},{12... | collective-permute-start | bytes 294920 | tf_op jit(solution)/shard_map/ppermute | solution.py:24
  5.8 0.8 collective-permute-start.9
  6.6 0.7 collective-permute-start
  7.9 2.4 %collective-permute-done.9 = bf16[192,256]{1,0:T(8,128)(2,1)S(1)} collective-permute-done((bf16[192,256]{1,0:T(8,128)(2,1)S(1)}, bf16[192,256]{1,0:T(8,128)(2,1)S(1)}, u32[]{:S(2)}, u32[]{:S(2)}) %collective-permute-start.9) | collective-permute-done | bytes 98336 | tf_op jit(solution)/shard_map/ppermute | solution.py:24
  10.3 2.8 %collective-permute-start.13 = (bf16[384,256]{1,0:T(8,128)(2,1)S(1)}, bf16[384,256]{1,0:T(8,128)(2,1)S(1)}, u32[]{:S(2)}, u32[]{:S(2)}) collective-permute-start(bf16[384,256]{1,0:T(8,128)(2,1)S(1)} %get-tuple-element.51), channel_id=1, source_target_pairs={{0,64},{32,96},{64,0},{96,32},{1,65},{33,97},{65,1},{97,33},{2,66}... | collective-permute-start | bytes 589832 | tf_op jit(solution)/shard_map/ppermute | solution.py:24
  13.2 0.9 collective-permute-start.14
  14.8 3.7 %collective-permute-start.4 = (bf16[384,256]{1,0:T(8,128)(2,1)S(1)}, bf16[384,256]{1,0:T(8,128)(2,1)S(1)}, u32[]{:S(2)}, u32[]{:S(2)}) collective-permute-start(bf16[384,256]{1,0:T(8,128)(2,1)S(1)} %pad_maximum_fusion.1), channel_id=1, source_target_pairs={{0,16},{8,24},{16,0},{24,8},{1,17},{9,25},{17,1},{25,9},{2,18},{10... | collective-permute-start | bytes 589832 | tf_op jit(solution)/shard_map/ppermute | solution.py:24
  18.9 1.0 collective-permute-start.1
  19.9 1.2 %collective-permute-done.14 = bf16[384,256]{1,0:T(8,128)(2,1)S(1)} collective-permute-done((bf16[384,256]{1,0:T(8,128)(2,1)S(1)}, bf16[384,256]{1,0:T(8,128)(2,1)S(1)}, u32[]{:S(2)}, u32[]{:S(2)}) %collective-permute-start.14) | collective-permute-done | bytes 196640 | tf_op jit(solution)/shard_map/ppermute | solution.py:24
  21.2 3.8 %collective-permute-start.15 = (bf16[768,256]{1,0:T(8,128)(2,1)S(1)}, bf16[768,256]{1,0:T(8,128)(2,1)S(1)}, u32[]{:S(2)}, u32[]{:S(2)}) collective-permute-start(bf16[768,256]{1,0:T(8,128)(2,1)S(1)} %constant_dynamic-update-slice_fusion.7.refs_7_), channel_id=1, source_target_pairs={{0,24},{8,0},{16,8},{24,16},{1,25},{9,1},{17,9},{25,17},{2,26},{10... | collective-permute-start | bytes 1179656 | tf_op jit(solution)/shard_map/ppermute | solution.py:24
  25.2 2.8 %collective-permute-start.17 = (bf16[192,512]{1,0:T(8,128)(2,1)S(1)}, bf16[192,512]{1,0:T(8,128)(2,1)S(1)}, u32[]{:S(2)}, u32[]{:S(2)}) collective-permute-start(bf16[192,512]{1,0:T(8,128)(2,1)S(1)} %get-tuple-element.44), channel_id=1, source_target_pairs={{0,2},{2,4},{4,6},{6,0},{1,3},{3,5},{5,7},{7,1},{8,10},{10,12},{12... | collective-permute-start | bytes 589832 | tf_op jit(solution)/shard_map/ppermute | solution.py:24
  28.0 2.6 %collective-permute-start.18 = (bf16[192,512]{1,0:T(8,128)(2,1)S(1)}, bf16[192,512]{1,0:T(8,128)(2,1)S(1)}, u32[]{:S(2)}, u32[]{:S(2)}) collective-permute-start(bf16[192,512]{1,0:T(8,128)(2,1)S(1)} %get-tuple-element.46), channel_id=1, source_target_pairs={{0,4},{2,6},{4,0},{6,2},{1,5},{3,7},{5,1},{7,3},{8,12},{10,14},{12... | collective-permute-start | bytes 589832 | tf_op jit(solution)/shard_map/ppermute | solution.py:24
  30.6 1.3 %collective-permute-start.19 = (bf16[192,512]{1,0:T(8,128)(2,1)S(1)}, bf16[192,512]{1,0:T(8,128)(2,1)S(1)}, u32[]{:S(2)}, u32[]{:S(2)}) collective-permute-start(bf16[192,512]{1,0:T(8,128)(2,1)S(1)} %get-tuple-element.43), channel_id=1, source_target_pairs={{0,6},{2,0},{4,2},{6,4},{1,7},{3,1},{5,3},{7,5},{8,14},{10,8},{12,... | collective-permute-start | bytes 589832 | tf_op jit(solution)/shard_map/ppermute | solution.py:24
  31.9 0.8 collective-permute-done.17.refs_9_
  32.8 0.7 copy-done.2
  33.4 4.1 %collective-permute-done.18.refs_10_ = bf16[192,512]{1,0:T(8,128)(2,1)S(1)} collective-permute-done((bf16[192,512]{1,0:T(8,128)(2,1)S(1)}, bf16[192,512]{1,0:T(8,128)(2,1)S(1)}, u32[]{:S(2)}, u32[]{:S(2)}) %collective-permute-start.18) | collective-permute-done | bytes 196640 | tf_op jit(solution)/shard_map/ppermute | solution.py:24
  37.6 0.7 copy-done.4
  38.2 2.4 %collective-permute-start.23 = (bf16[768,256]{1,0:T(8,128)(2,1)S(1)}, bf16[768,256]{1,0:T(8,128)(2,1)}, u32[]{:S(2)}, u32[]{:S(2)}) collective-permute-start(bf16[768,256]{1,0:T(8,128)(2,1)S(1)} %constant_dynamic-update-slice_fusion.4.refs_6_), channel_id=1, source_target_pairs={{0,24},{8,0},{16,8},{24,16},{1,25},{9,1},{17,9},{25,17},{2,26},{10... | collective-permute-start | bytes 1179656 | tf_op jit(solution)/shard_map/ppermute | solution.py:24
  40.6 0.7 copy-done.6
  41.3 4.8 %collective-permute-start.6 = (bf16[768,256]{1,0:T(8,128)(2,1)S(1)}, bf16[768,256]{1,0:T(8,128)(2,1)S(1)}, u32[]{:S(2)}, u32[]{:S(2)}) collective-permute-start(bf16[768,256]{1,0:T(8,128)(2,1)S(1)} %constant_dynamic-update-slice_fusion.refs_5_), channel_id=1, source_target_pairs={{0,96},{32,0},{64,32},{96,64},{1,97},{33,1},{65,33},{97,65},{2,98}... | collective-permute-start | bytes 1179656 | tf_op jit(solution)/shard_map/ppermute | solution.py:24
  46.9 0.9 convert_reduce_fusion.1
  47.8 1.0 convert_reduce_fusion.refs_2_
  48.8 3.6 %collective-permute-done.6.refs_5_ = bf16[768,256]{1,0:T(8,128)(2,1)S(1)} collective-permute-done((bf16[768,256]{1,0:T(8,128)(2,1)S(1)}, bf16[768,256]{1,0:T(8,128)(2,1)S(1)}, u32[]{:S(2)}, u32[]{:S(2)}) %collective-permute-start.6) | collective-permute-done | bytes 393248 | tf_op jit(solution)/shard_map/ppermute | solution.py:24
  52.4 3.4 %collective-permute-start.21 = (bf16[768,256]{1,0:T(8,128)(2,1)S(1)}, bf16[768,256]{1,0:T(8,128)(2,1)S(1)}, u32[]{:S(2)}, u32[]{:S(2)}) collective-permute-start(bf16[768,256]{1,0:T(8,128)(2,1)S(1)} %pad_maximum_fusion.refs_4_), channel_id=1, source_target_pairs={{0,96},{32,0},{64,32},{96,64},{1,97},{33,1},{65,33},{97,65},{2,98}... | collective-permute-start | bytes 1179656 | tf_op jit(solution)/shard_map/ppermute | solution.py:24
  55.8 8.1 %collective-permute-done.2.refs_4_ = bf16[768,256]{1,0:T(8,128)(2,1)S(1)} collective-permute-done((bf16[768,256]{1,0:T(8,128)(2,1)S(1)}, bf16[768,256]{1,0:T(8,128)(2,1)S(1)}, u32[]{:S(2)}, u32[]{:S(2)}) %collective-permute-start.2) | collective-permute-done | bytes 393248 | tf_op jit(solution)/shard_map/ppermute | solution.py:24
  64.2 1.2 collective-permute-start.12
  65.4 1.5 %collective-permute-start.3 = (bf16[768,256]{1,0:T(8,128)(2,1)S(1)}, bf16[768,256]{1,0:T(8,128)(2,1)S(1)}, u32[]{:S(2)}, u32[]{:S(2)}) collective-permute-start(bf16[768,256]{1,0:T(8,128)(2,1)S(1)} %collective-permute-done.2.refs_4_), channel_id=1, source_target_pairs={{0,32},{32,64},{64,96},{96,0},{1,33},{33,65},{65,97},{97,1},{2,34}... | collective-permute-start | bytes 1179656 | tf_op jit(solution)/shard_map/ppermute | solution.py:24
  66.9 0.9 copy-done.3
  67.8 0.9 copy-done.5
  68.7 0.9 copy-done.7
  69.6 5.0 %shard_map.64 = (bf16[8,384,128]{2,1,0:T(8,128)(2,1)S(1)}, f32[8,384,128]{2,1,0:T(8,128)S(1)}, f32[8,384,256]{2,1,0:T(8,128)S(1)}) custom-call(s32[4]{0:T(128)S(1)} %pad_add_fusion.refs_0_.coords, s32[128]{0:T(128)S(1)} %copy-done.1, s32[8]{0:T(128)S(1)} %convert_reduce_fusion.refs_2_, s32[136]{0:T(256)S(1)} %get-tuple-element.39.refs_3_, ...), custom_call_target="tpu_custom_call" | custom-call | flops 2000000000 | bytes 2500000 | tf_op jit(solution)/shard_map/pallas_call | solution.py:221
  74.6 6.5 %shard_map.65 = (f32[8,384,128]{2,1,0:T(8,128)S(1)}, f32[8,384,256]{2,1,0:T(8,128)S(1)}, bf16[2048,4096]{1,0:T(8,128)(2,1)S(1)}) custom-call(s32[4]{0:T(128)S(1)} %pad_add_fusion.refs_0_.coords, s32[128]{0:T(128)S(1)} %copy-done.1, s32[8]{0:T(128)S(1)} %convert_reduce_fusion.refs_2_, ...), custom_call_target="tpu_custom_call", output_to_operand_aliasing={{0}: (9, {}), {1}: (10, {})} | custom-call | flops 2000000000 | bytes 2500000 | tf_op jit(solution)/shard_map/pallas_call | solution.py:221
  81.1 4.8 %shard_map.66 = (f32[8,384,128]{2,1,0:T(8,128)S(1)}, f32[8,384,256]{2,1,0:T(8,128)S(1)}) custom-call(s32[4]{0:T(128)S(1)} %pad_add_fusion.refs_0_.coords, s32[128]{0:T(128)S(1)} %copy-done.1, s32[8]{0:T(128)S(1)} %convert_reduce_fusion.refs_2_, s32[136]{0:T(256)S(1)} %get-tuple-element.38.refs_3_, ...), custom_call_target="tpu_custom_call", output_to_operand_aliasing={{0}: (9, {}), {1}: (10, {})} | custom-call | flops 2000000000 | bytes 2500000 | tf_op jit(solution)/shard_map/pallas_call | solution.py:221
  86.0 4.4 %shard_map.67 = (f32[8,384,128]{2,1,0:T(8,128)S(1)}, f32[8,384,256]{2,1,0:T(8,128)S(1)}, bf16[96,512]{1,0:T(8,128)(2,1)S(1)}, bf16[96,512]{1,0:T(8,128)(2,1)S(1)...) custom-call(s32[4]{0:T(128)S(1)} %pad_add_fusion.refs_0_.coords, ...), custom_call_target="tpu_custom_call", output_to_operand_aliasing={{0}: (9, {}), {1}: (10, {})} | custom-call | flops 2000000000 | bytes 2500000 | tf_op jit(solution)/shard_map/pallas_call | solution.py:221
  90.3 2.1 %collective-permute-start.27 = (bf16[96,512]{1,0:T(8,128)(2,1)S(1)}, bf16[96,512]{1,0:T(8,128)(2,1)S(1)}, u32[]{:S(2)}, u32[]{:S(2)}) collective-permute-start(bf16[96,512]{1,0:T(8,128)(2,1)S(1)} %get-tuple-element.34), channel_id=1, source_target_pairs={{0,6},{2,0},{4,2},{6,4},{1,7},{3,1},{5,3},{7,5},{8,14},{10,8},{12,... | collective-permute-start | bytes 294920 | tf_op jit(solution)/shard_map/ppermute | solution.py:24
  92.4 2.0 %collective-permute-start.28 = (bf16[96,512]{1,0:T(8,128)(2,1)S(1)}, bf16[96,512]{1,0:T(8,128)(2,1)S(1)}, u32[]{:S(2)}, u32[]{:S(2)}) collective-permute-start(bf16[96,512]{1,0:T(8,128)(2,1)S(1)} %get-tuple-element.35), channel_id=1, source_target_pairs={{0,4},{2,6},{4,0},{6,2},{1,5},{3,7},{5,1},{7,3},{8,12},{10,14},{12... | collective-permute-start | bytes 294920 | tf_op jit(solution)/shard_map/ppermute | solution.py:24
  94.6 2.8 %collective-permute-done.28.o2 = bf16[96,512]{1,0:T(8,128)(2,1)S(1)} collective-permute-done((bf16[96,512]{1,0:T(8,128)(2,1)S(1)}, bf16[96,512]{1,0:T(8,128)(2,1)S(1)}, u32[]{:S(2)}, u32[]{:S(2)}) %collective-permute-start.28) | collective-permute-done | bytes 98336 | tf_op jit(solution)/shard_map/ppermute | solution.py:24
  97.4 1.7 %collective-permute-done.29.o3 = bf16[96,512]{1,0:T(8,128)(2,1)S(1)} collective-permute-done((bf16[96,512]{1,0:T(8,128)(2,1)S(1)}, bf16[96,512]{1,0:T(8,128)(2,1)S(1)}, u32[]{:S(2)}, u32[]{:S(2)}) %collective-permute-start.29) | collective-permute-done | bytes 98336 | tf_op jit(solution)/shard_map/ppermute | solution.py:24
  99.1 3.5 %project.3 = bf16[96,4096]{1,0:T(8,128)(2,1)S(1)} custom-call(s32[4]{0:T(128)S(1)} %pad_add_fusion.refs_0_.coords, bf16[96,512]{1,0:T(8,128)(2,1)S(1)} %get-tuple-element.33.o0, bf16[96,512]{1,0:T(8,128)(2,1)S(1)} %collective-permute-done.27.o1, bf16[96,512]{1,0:T(8,128)(2,1)S(1)} %collective-permute-done.28.o2, ...), custom_call_target="tpu_custom_call" | custom-call | flops 1610612736 | bytes 16777216 | tf_op jit(solution)/shard_map/project/pallas_call | solution.py:254
  102.6 4.2 %collective-permute-start.30 = (bf16[96,4096]{1,0:T(8,128)(2,1)S(1)}, bf16[96,4096]{1,0:T(8,128)(2,1)S(1)}, u32[]{:S(2)}, u32[]{:S(2)}) collective-permute-start(bf16[96,4096]{1,0:T(8,128)(2,1)S(1)} %project.3), channel_id=1, source_target_pairs={{0,1},{1,0},{2,3},{3,2},{4,5},{5,4},{6,7},{7,6},{8,9},{9,8},{10,11... | collective-permute-start | bytes 2359304 | tf_op jit(solution)/shard_map/ppermute | solution.py:317
  106.8 0.7 collective-permute-start.24
  108.5 2.5 %collective-permute-done.24.o1 = bf16[96,512]{1,0:T(8,128)(2,1)S(1)} collective-permute-done((bf16[96,512]{1,0:T(8,128)(2,1)S(1)}, bf16[96,512]{1,0:T(8,128)(2,1)S(1)}, u32[]{:S(2)}, u32[]{:S(2)}) %collective-permute-start.24) | collective-permute-done | bytes 98336 | tf_op jit(solution)/shard_map/ppermute | solution.py:24
  111.0 2.0 %collective-permute-done.25.o2 = bf16[96,512]{1,0:T(8,128)(2,1)S(1)} collective-permute-done((bf16[96,512]{1,0:T(8,128)(2,1)S(1)}, bf16[96,512]{1,0:T(8,128)(2,1)S(1)}, u32[]{:S(2)}, u32[]{:S(2)}) %collective-permute-start.25) | collective-permute-done | bytes 98336 | tf_op jit(solution)/shard_map/ppermute | solution.py:24
  113.0 2.8 %collective-permute-done.26.o3 = bf16[96,512]{1,0:T(8,128)(2,1)S(1)} collective-permute-done((bf16[96,512]{1,0:T(8,128)(2,1)S(1)}, bf16[96,512]{1,0:T(8,128)(2,1)S(1)}, u32[]{:S(2)}, u32[]{:S(2)}) %collective-permute-start.26) | collective-permute-done | bytes 98336 | tf_op jit(solution)/shard_map/ppermute | solution.py:24
  115.8 3.4 %project.2 = f32[96,4096]{1,0:T(8,128)S(1)} custom-call(s32[4]{0:T(128)S(1)} %pad_add_fusion.refs_0_.coords, bf16[96,512]{1,0:T(8,128)(2,1)S(1)} %get-tuple-element.28.o0, bf16[96,512]{1,0:T(8,128)(2,1)S(1)} %collective-permute-done.24.o1, bf16[96,512]{1,0:T(8,128)(2,1)S(1)} %collective-permute-done.25.o2, bf16[96,512]{1,0:T(8,128)(2,1)S(1)} %collective-permute-done.26.o3, ...), custom_call_target="tpu_custom_call" | custom-call | flops 1610612736 | bytes 16777216 | tf_op jit(solution)/shard_map/project/pallas_call | solution.py:254
  119.2 1.0 add_convert_fusion
  (57 shorter events, 4.4 us)
Async XLA Ops:
  0.0 0.9 copy-start
  0.0 13.1 %copy-start.8 = (bf16[192,2048]{1,0:T(8,128)(2,1)S(1)}, bf16[192,2048]{1,0:T(8,128)(2,1)}, u32[]{:S(2)}) copy-start(bf16[192,2048]{1,0:T(8,128)(2,1)} %param.6) | copy-start | bytes 2359300
  2.0 5.8 %collective-permute-start.8 = (bf16[192,256]{1,0:T(8,128)(2,1)S(1)}, bf16[192,256]{1,0:T(8,128)(2,1)S(1)}, u32[]{:S(2)}, u32[]{:S(2)}) collective-permute-start(bf16[192,256]{1,0:T(8,128)(2,1)S(1)} %get-tuple-element.48), channel_id=1, source_target_pairs={{0,4},{2,6},{4,0},{6,2},{1,5},{3,7},{5,1},{7,3},{8,12},{10,14},{12... | collective-permute-start | bytes 294920 | tf_op jit(solution)/shard_map/ppermute | solution.py:24
  5.8 4.4 %collective-permute-start.9 = (bf16[192,256]{1,0:T(8,128)(2,1)S(1)}, bf16[192,256]{1,0:T(8,128)(2,1)S(1)}, u32[]{:S(2)}, u32[]{:S(2)}) collective-permute-start(bf16[192,256]{1,0:T(8,128)(2,1)S(1)} %get-tuple-element.47), channel_id=1, source_target_pairs={{0,6},{2,0},{4,2},{6,4},{1,7},{3,1},{5,3},{7,5},{8,14},{10,8},{12,... | collective-permute-start | bytes 294920 | tf_op jit(solution)/shard_map/ppermute | solution.py:24
  6.6 8.1 %collective-permute-start = (bf16[192,256]{1,0:T(8,128)(2,1)S(1)}, bf16[192,256]{1,0:T(8,128)(2,1)S(1)}, u32[]{:S(2)}, u32[]{:S(2)}) collective-permute-start(bf16[192,256]{1,0:T(8,128)(2,1)S(1)} %get-tuple-element.49), channel_id=1, source_target_pairs={{0,2},{2,4},{4,6},{6,0},{1,3},{3,5},{5,7},{7,1},{8,10},{10,12},{12... | collective-permute-start | bytes 294920 | tf_op jit(solution)/shard_map/ppermute | solution.py:24
  10.3 8.6 %collective-permute-start.13 = (bf16[384,256]{1,0:T(8,128)(2,1)S(1)}, bf16[384,256]{1,0:T(8,128)(2,1)S(1)}, u32[]{:S(2)}, u32[]{:S(2)}) collective-permute-start(bf16[384,256]{1,0:T(8,128)(2,1)S(1)} %get-tuple-element.51), channel_id=1, source_target_pairs={{0,64},{32,96},{64,0},{96,32},{1,65},{33,97},{65,1},{97,33},{2,66}... | collective-permute-start | bytes 589832 | tf_op jit(solution)/shard_map/ppermute | solution.py:24
  13.2 7.9 %collective-permute-start.14 = (bf16[384,256]{1,0:T(8,128)(2,1)S(1)}, bf16[384,256]{1,0:T(8,128)(2,1)S(1)}, u32[]{:S(2)}, u32[]{:S(2)}) collective-permute-start(bf16[384,256]{1,0:T(8,128)(2,1)S(1)} %get-tuple-element.51), channel_id=1, source_target_pairs={{0,96},{32,0},{64,32},{96,64},{1,97},{33,1},{65,33},{97,65},{2,98}... | collective-permute-start | bytes 589832 | tf_op jit(solution)/shard_map/ppermute | solution.py:24
  14.1 10.9 %collective-permute-start.10 = (bf16[384,256]{1,0:T(8,128)(2,1)S(1)}, bf16[384,256]{1,0:T(8,128)(2,1)S(1)}, u32[]{:S(2)}, u32[]{:S(2)}) collective-permute-start(bf16[384,256]{1,0:T(8,128)(2,1)S(1)} %get-tuple-element.51), channel_id=1, source_target_pairs={{0,32},{32,64},{64,96},{96,0},{1,33},{33,65},{65,97},{97,1},{2,34}... | collective-permute-start | bytes 589832 | tf_op jit(solution)/shard_map/ppermute | solution.py:24
  14.8 32.1 %copy-start.1 = (s32[128]{0:T(128)S(1)}, s32[128]{0:T(128)}, u32[]{:S(2)}) copy-start(s32[128]{0:T(128)} %refs_1_.7) | copy-start | bytes 1540
  14.8 10.4 %collective-permute-start.4 = (bf16[384,256]{1,0:T(8,128)(2,1)S(1)}, bf16[384,256]{1,0:T(8,128)(2,1)S(1)}, u32[]{:S(2)}, u32[]{:S(2)}) collective-permute-start(bf16[384,256]{1,0:T(8,128)(2,1)S(1)} %pad_maximum_fusion.1), channel_id=1, source_target_pairs={{0,16},{8,24},{16,0},{24,8},{1,17},{9,25},{17,1},{25,9},{2,18},{10... | collective-permute-start | bytes 589832 | tf_op jit(solution)/shard_map/ppermute | solution.py:24
  18.5 9.5 %collective-permute-start.5 = (bf16[384,256]{1,0:T(8,128)(2,1)S(1)}, bf16[384,256]{1,0:T(8,128)(2,1)S(1)}, u32[]{:S(2)}, u32[]{:S(2)}) collective-permute-start(bf16[384,256]{1,0:T(8,128)(2,1)S(1)} %pad_maximum_fusion.1), channel_id=1, source_target_pairs={{0,24},{8,0},{16,8},{24,16},{1,25},{9,1},{17,9},{25,17},{2,26},{10... | collective-permute-start | bytes 589832 | tf_op jit(solution)/shard_map/ppermute | solution.py:24
  18.9 11.7 %collective-permute-start.1 = (bf16[384,256]{1,0:T(8,128)(2,1)S(1)}, bf16[384,256]{1,0:T(8,128)(2,1)S(1)}, u32[]{:S(2)}, u32[]{:S(2)}) collective-permute-start(bf16[384,256]{1,0:T(8,128)(2,1)S(1)} %pad_maximum_fusion.1), channel_id=1, source_target_pairs={{0,8},{8,16},{16,24},{24,0},{1,9},{9,17},{17,25},{25,1},{2,10},{10... | collective-permute-start | bytes 589832 | tf_op jit(solution)/shard_map/ppermute | solution.py:24
  21.2 24.9 %collective-permute-start.15 = (bf16[768,256]{1,0:T(8,128)(2,1)S(1)}, bf16[768,256]{1,0:T(8,128)(2,1)S(1)}, u32[]{:S(2)}, u32[]{:S(2)}) collective-permute-start(bf16[768,256]{1,0:T(8,128)(2,1)S(1)} %constant_dynamic-update-slice_fusion.7.refs_7_), channel_id=1, source_target_pairs={{0,24},{8,0},{16,8},{24,16},{1,25},{9,1},{17,9},{25,17},{2,26},{10... | collective-permute-start | bytes 1179656 | tf_op jit(solution)/shard_map/ppermute | solution.py:24
  25.0 21.1 %collective-permute-start.11 = (bf16[768,256]{1,0:T(8,128)(2,1)S(1)}, bf16[768,256]{1,0:T(8,128)(2,1)S(1)}, u32[]{:S(2)}, u32[]{:S(2)}) collective-permute-start(bf16[768,256]{1,0:T(8,128)(2,1)S(1)} %constant_dynamic-update-slice_fusion.4.refs_6_), channel_id=1, source_target_pairs={{0,8},{8,16},{16,24},{24,0},{1,9},{9,17},{17,25},{25,1},{2,10},{10... | collective-permute-start | bytes 1179656 | tf_op jit(solution)/shard_map/ppermute | solution.py:24
  25.2 7.6 %collective-permute-start.17 = (bf16[192,512]{1,0:T(8,128)(2,1)S(1)}, bf16[192,512]{1,0:T(8,128)(2,1)S(1)}, u32[]{:S(2)}, u32[]{:S(2)}) collective-permute-start(bf16[192,512]{1,0:T(8,128)(2,1)S(1)} %get-tuple-element.44), channel_id=1, source_target_pairs={{0,2},{2,4},{4,6},{6,0},{1,3},{3,5},{5,7},{7,1},{8,10},{10,12},{12... | collective-permute-start | bytes 589832 | tf_op jit(solution)/shard_map/ppermute | solution.py:24
  28.0 9.6 %collective-permute-start.18 = (bf16[192,512]{1,0:T(8,128)(2,1)S(1)}, bf16[192,512]{1,0:T(8,128)(2,1)S(1)}, u32[]{:S(2)}, u32[]{:S(2)}) collective-permute-start(bf16[192,512]{1,0:T(8,128)(2,1)S(1)} %get-tuple-element.46), channel_id=1, source_target_pairs={{0,4},{2,6},{4,0},{6,2},{1,5},{3,7},{5,1},{7,3},{8,12},{10,14},{12... | collective-permute-start | bytes 589832 | tf_op jit(solution)/shard_map/ppermute | solution.py:24
  30.6 10.0 %collective-permute-start.19 = (bf16[192,512]{1,0:T(8,128)(2,1)S(1)}, bf16[192,512]{1,0:T(8,128)(2,1)S(1)}, u32[]{:S(2)}, u32[]{:S(2)}) collective-permute-start(bf16[192,512]{1,0:T(8,128)(2,1)S(1)} %get-tuple-element.43), channel_id=1, source_target_pairs={{0,6},{2,0},{4,2},{6,4},{1,7},{3,1},{5,3},{7,5},{8,14},{10,8},{12,... | collective-permute-start | bytes 589832 | tf_op jit(solution)/shard_map/ppermute | solution.py:24
  32.8 0.7 copy-start.2
  33.4 30.8 %collective-permute-start.22 = (bf16[768,256]{1,0:T(8,128)(2,1)S(1)}, bf16[768,256]{1,0:T(8,128)(2,1)}, u32[]{:S(2)}, u32[]{:S(2)}) collective-permute-start(bf16[768,256]{1,0:T(8,128)(2,1)S(1)} %constant_dynamic-update-slice_fusion.7.refs_7_), channel_id=1, source_target_pairs={{0,8},{8,16},{16,24},{24,0},{1,9},{9,17},{17,25},{25,1},{2,10},{10... | collective-permute-start | bytes 1179656 | tf_op jit(solution)/shard_map/ppermute | solution.py:24
  37.6 0.7 copy-start.4
  38.2 27.1 %collective-permute-start.23 = (bf16[768,256]{1,0:T(8,128)(2,1)S(1)}, bf16[768,256]{1,0:T(8,128)(2,1)}, u32[]{:S(2)}, u32[]{:S(2)}) collective-permute-start(bf16[768,256]{1,0:T(8,128)(2,1)S(1)} %constant_dynamic-update-slice_fusion.4.refs_6_), channel_id=1, source_target_pairs={{0,24},{8,0},{16,8},{24,16},{1,25},{9,1},{17,9},{25,17},{2,26},{10... | collective-permute-start | bytes 1179656 | tf_op jit(solution)/shard_map/ppermute | solution.py:24
  40.6 0.7 copy-start.6
  41.3 11.1 %collective-permute-start.6 = (bf16[768,256]{1,0:T(8,128)(2,1)S(1)}, bf16[768,256]{1,0:T(8,128)(2,1)S(1)}, u32[]{:S(2)}, u32[]{:S(2)}) collective-permute-start(bf16[768,256]{1,0:T(8,128)(2,1)S(1)} %constant_dynamic-update-slice_fusion.refs_5_), channel_id=1, source_target_pairs={{0,96},{32,0},{64,32},{96,64},{1,97},{33,1},{65,33},{97,65},{2,98}... | collective-permute-start | bytes 1179656 | tf_op jit(solution)/shard_map/ppermute | solution.py:24
  46.1 19.3 %collective-permute-start.20 = (bf16[768,256]{1,0:T(8,128)(2,1)S(1)}, bf16[768,256]{1,0:T(8,128)(2,1)}, u32[]{:S(2)}, u32[]{:S(2)}) collective-permute-start(bf16[768,256]{1,0:T(8,128)(2,1)S(1)} %constant_dynamic-update-slice_fusion.refs_5_), channel_id=1, source_target_pairs={{0,32},{32,64},{64,96},{96,0},{1,33},{33,65},{65,97},{97,1},{2,34}... | collective-permute-start | bytes 1179656 | tf_op jit(solution)/shard_map/ppermute | solution.py:24
  46.1 17.8 %collective-permute-start.2 = (bf16[768,256]{1,0:T(8,128)(2,1)S(1)}, bf16[768,256]{1,0:T(8,128)(2,1)S(1)}, u32[]{:S(2)}, u32[]{:S(2)}) collective-permute-start(bf16[768,256]{1,0:T(8,128)(2,1)S(1)} %pad_maximum_fusion.refs_4_), channel_id=1, source_target_pairs={{0,32},{32,64},{64,96},{96,0},{1,33},{33,65},{65,97},{97,1},{2,34}... | collective-permute-start | bytes 1179656 | tf_op jit(solution)/shard_map/ppermute | solution.py:24
  52.4 28.8 %collective-permute-start.21 = (bf16[768,256]{1,0:T(8,128)(2,1)S(1)}, bf16[768,256]{1,0:T(8,128)(2,1)S(1)}, u32[]{:S(2)}, u32[]{:S(2)}) collective-permute-start(bf16[768,256]{1,0:T(8,128)(2,1)S(1)} %pad_maximum_fusion.refs_4_), channel_id=1, source_target_pairs={{0,96},{32,0},{64,32},{96,64},{1,97},{33,1},{65,33},{97,65},{2,98}... | collective-permute-start | bytes 1179656 | tf_op jit(solution)/shard_map/ppermute | solution.py:24
  63.9 22.0 %collective-permute-start.16 = (bf16[768,256]{1,0:T(8,128)(2,1)S(1)}, bf16[768,256]{1,0:T(8,128)(2,1)S(1)}, u32[]{:S(2)}, u32[]{:S(2)}) collective-permute-start(bf16[768,256]{1,0:T(8,128)(2,1)S(1)} %collective-permute-done.15.refs_7_), channel_id=1, source_target_pairs={{0,24},{8,0},{16,8},{24,16},{1,25},{9,1},{17,9},{25,17},{2,26},{10... | collective-permute-start | bytes 1179656 | tf_op jit(solution)/shard_map/ppermute | solution.py:24
  64.2 21.7 %collective-permute-start.12 = (bf16[768,256]{1,0:T(8,128)(2,1)S(1)}, bf16[768,256]{1,0:T(8,128)(2,1)S(1)}, u32[]{:S(2)}, u32[]{:S(2)}) collective-permute-start(bf16[768,256]{1,0:T(8,128)(2,1)S(1)} %collective-permute-done.11.refs_6_), channel_id=1, source_target_pairs={{0,8},{8,16},{16,24},{24,0},{1,9},{9,17},{17,25},{25,1},{2,10},{10... | collective-permute-start | bytes 1179656 | tf_op jit(solution)/shard_map/ppermute | solution.py:24
  65.4 20.6 %collective-permute-start.7 = (bf16[768,256]{1,0:T(8,128)(2,1)S(1)}, bf16[768,256]{1,0:T(8,128)(2,1)S(1)}, u32[]{:S(2)}, u32[]{:S(2)}) collective-permute-start(bf16[768,256]{1,0:T(8,128)(2,1)S(1)} %collective-permute-done.6.refs_5_), channel_id=1, source_target_pairs={{0,96},{32,0},{64,32},{96,64},{1,97},{33,1},{65,33},{97,65},{2,98}... | collective-permute-start | bytes 1179656 | tf_op jit(solution)/shard_map/ppermute | solution.py:24
  65.4 20.6 %collective-permute-start.3 = (bf16[768,256]{1,0:T(8,128)(2,1)S(1)}, bf16[768,256]{1,0:T(8,128)(2,1)S(1)}, u32[]{:S(2)}, u32[]{:S(2)}) collective-permute-start(bf16[768,256]{1,0:T(8,128)(2,1)S(1)} %collective-permute-done.2.refs_4_), channel_id=1, source_target_pairs={{0,32},{32,64},{64,96},{96,0},{1,33},{33,65},{65,97},{97,1},{2,34}... | collective-permute-start | bytes 1179656 | tf_op jit(solution)/shard_map/ppermute | solution.py:24
  66.9 0.9 copy-start.3
  67.8 0.9 copy-start.5
  68.7 0.9 copy-start.7
  90.3 4.3 %collective-permute-start.27 = (bf16[96,512]{1,0:T(8,128)(2,1)S(1)}, bf16[96,512]{1,0:T(8,128)(2,1)S(1)}, u32[]{:S(2)}, u32[]{:S(2)}) collective-permute-start(bf16[96,512]{1,0:T(8,128)(2,1)S(1)} %get-tuple-element.34), channel_id=1, source_target_pairs={{0,6},{2,0},{4,2},{6,4},{1,7},{3,1},{5,3},{7,5},{8,14},{10,8},{12,... | collective-permute-start | bytes 294920 | tf_op jit(solution)/shard_map/ppermute | solution.py:24
  92.4 5.0 %collective-permute-start.28 = (bf16[96,512]{1,0:T(8,128)(2,1)S(1)}, bf16[96,512]{1,0:T(8,128)(2,1)S(1)}, u32[]{:S(2)}, u32[]{:S(2)}) collective-permute-start(bf16[96,512]{1,0:T(8,128)(2,1)S(1)} %get-tuple-element.35), channel_id=1, source_target_pairs={{0,4},{2,6},{4,0},{6,2},{1,5},{3,7},{5,1},{7,3},{8,12},{10,14},{12... | collective-permute-start | bytes 294920 | tf_op jit(solution)/shard_map/ppermute | solution.py:24
  94.4 4.7 %collective-permute-start.29 = (bf16[96,512]{1,0:T(8,128)(2,1)S(1)}, bf16[96,512]{1,0:T(8,128)(2,1)S(1)}, u32[]{:S(2)}, u32[]{:S(2)}) collective-permute-start(bf16[96,512]{1,0:T(8,128)(2,1)S(1)} %get-tuple-element.36), channel_id=1, source_target_pairs={{0,2},{2,4},{4,6},{6,0},{1,3},{3,5},{5,7},{7,1},{8,10},{10,12},{12... | collective-permute-start | bytes 294920 | tf_op jit(solution)/shard_map/ppermute | solution.py:24
  102.6 16.6 %collective-permute-start.30 = (bf16[96,4096]{1,0:T(8,128)(2,1)S(1)}, bf16[96,4096]{1,0:T(8,128)(2,1)S(1)}, u32[]{:S(2)}, u32[]{:S(2)}) collective-permute-start(bf16[96,4096]{1,0:T(8,128)(2,1)S(1)} %project.3), channel_id=1, source_target_pairs={{0,1},{1,0},{2,3},{3,2},{4,5},{5,4},{6,7},{7,6},{8,9},{9,8},{10,11... | collective-permute-start | bytes 2359304 | tf_op jit(solution)/shard_map/ppermute | solution.py:317
  106.8 4.3 %collective-permute-start.24 = (bf16[96,512]{1,0:T(8,128)(2,1)S(1)}, bf16[96,512]{1,0:T(8,128)(2,1)S(1)}, u32[]{:S(2)}, u32[]{:S(2)}) collective-permute-start(bf16[96,512]{1,0:T(8,128)(2,1)S(1)} %get-tuple-element.29), channel_id=1, source_target_pairs={{0,6},{2,0},{4,2},{6,4},{1,7},{3,1},{5,3},{7,5},{8,14},{10,8},{12,... | collective-permute-start | bytes 294920 | tf_op jit(solution)/shard_map/ppermute | solution.py:24
  107.5 5.5 %collective-permute-start.25 = (bf16[96,512]{1,0:T(8,128)(2,1)S(1)}, bf16[96,512]{1,0:T(8,128)(2,1)S(1)}, u32[]{:S(2)}, u32[]{:S(2)}) collective-permute-start(bf16[96,512]{1,0:T(8,128)(2,1)S(1)} %get-tuple-element.30), channel_id=1, source_target_pairs={{0,4},{2,6},{4,0},{6,2},{1,5},{3,7},{5,1},{7,3},{8,12},{10,14},{12... | collective-permute-start | bytes 294920 | tf_op jit(solution)/shard_map/ppermute | solution.py:24
  108.2 7.7 %collective-permute-start.26 = (bf16[96,512]{1,0:T(8,128)(2,1)S(1)}, bf16[96,512]{1,0:T(8,128)(2,1)S(1)}, u32[]{:S(2)}, u32[]{:S(2)}) collective-permute-start(bf16[96,512]{1,0:T(8,128)(2,1)S(1)} %get-tuple-element.31), channel_id=1, source_target_pairs={{0,2},{2,4},{4,6},{6,0},{1,3},{3,5},{5,7},{7,1},{8,10},{10,12},{12... | collective-permute-start | bytes 294920 | tf_op jit(solution)/shard_map/ppermute | solution.py:24

commit v2 on v1

--- a/solution.py
+++ b/solution.py
@@ -42,14 +42,13 @@
     else:
         (q_all,) = take(1)
         take(2)
-    if phase == 1:
+    if first_phase:
         (weight,) = take(1)
-    if first_phase:
         (q_all,) = take(1)
     best_all, acc_all = take(2)
     if last_phase:
         outs = take(8)
-    if phase == 1:
+    if first_phase:
         (weight_held,) = take(1)
         weight_copy = pltpu.make_async_copy(weight, weight_held, refs.pop())
         weight_copy.start()
@@ -172,7 +171,7 @@
     lax.fori_loop(0, pairs, pair, 0)
     accumulate(2 * pairs, p1, f1)
 
-    if phase == 1:
+    if first_phase:
         weight_copy.wait()
     if last_phase:
         for turn in range(2):
@@ -305,8 +304,8 @@
     ranks = [jnp.sum((before & (phase_of == p)[None, :]).astype(jnp.int32), axis=1) for p in range(4)]
 
     scalars = [coords, span_table, starts]
-    q_all, best, acc = run_phase(0, scalars + [ranks[0]], pieces[0], q_part)
-    best, acc, weight = run_phase(1, scalars + [ranks[1]], pieces[1], [q_all, best, acc], out_weight)
+    q_all, best, acc, weight = run_phase(0, scalars + [ranks[0]], pieces[0], q_part, out_weight)
+    best, acc = run_phase(1, scalars + [ranks[1]], pieces[1], [q_all, best, acc])
     best, acc = run_phase(2, scalars + [ranks[2]], pieces[2], [q_all, best, acc])
     o_part = run_phase(3, scalars + [ranks[3]], pieces[3], [q_all, best, acc])[2:]
 

time: 121 us -> 117 us (0.967)
  local copies, waits for them, and re-layouts: 6.98 us -> 2.17 us
  waiting for transfers between devices: 32.8 us -> 34.1 us
    unnamed x22 -> x10, local copies, waits for them, and re-layouts: 5.82 us -> 1.01 us
    ppermute x30, waiting for transfers between devices: 32.8 us -> 34.1 us  [shift(): lax.ppermute(value, axis, [(i, (i + by) % RING) for i in range(RING)])]
  transfers between devices with their start and end apart: 31 -> 31, of which waited for: 13 -> 13; matrix products, arithmetic and copies ran while one was open for 2% -> 1% of each run, Pallas kernels for 16% -> 17%
where the time goes in v2:
time: 117 us; the launch traced here: 116 us
  starting transfers between devices  49.7 us (42%)
  waiting for transfers between devices  34.1 us (29%)
  Pallas kernels  27.3 us (23%)
  other arithmetic  2.48 us (2%)
  local copies, waits for them, and re-layouts  2.17 us (2%)
    ppermute x30, starting transfers between devices, shift(): lax.ppermute(value, axis, [(i, (i + by) % RING) for i in range(RING)])  45.6 us
    ppermute x30, waiting for transfers between devices, shift(): lax.ppermute(value, axis, [(i, (i + by) % RING) for i in range(RING)])  34.1 us
    pallas_call x4, Pallas kernels, run_phase(): pl.pallas_call(lambda *refs: phase_kernel(phase, *refs), out_shape=[jax.S...  20.4 us
    pallas_call x2, Pallas kernels, project(): pl.pallas_call(project_kernel, out_shape=jax.ShapeDtypeStruct((SPAN, widt...  6.89 us
    ppermute x1, starting transfers between devices, layer(): lax.ppermute(project(coords, theirs, weight, jnp.bfloat16), 'hd', [(0, 1)...  4.15 us
  transfers between devices with their start and end apart: 31, of which 13 were waited for; matrix products, arithmetic and copies ran while one was open for 1% of the time, Pallas kernels for 17%

profile of v2, /device:TPU:1, one launch (start us, length us, event | category | flops | bytes accessed | tf_op | source)
XLA Modules:
  0.0 116.1 jit_solution(7325103903458178202)
XLA Ops:
  0.0 0.9 copy-done
  1.0 1.0 bitcast_dynamic-update-slice_fusion
  2.0 3.8 %collective-permute-start.8 = (bf16[192,256]{1,0:T(8,128)(2,1)S(1)}, bf16[192,256]{1,0:T(8,128)(2,1)S(1)}, u32[]{:S(2)}, u32[]{:S(2)}) collective-permute-start(bf16[192,256]{1,0:T(8,128)(2,1)S(1)} %get-tuple-element.48), channel_id=1, source_target_pairs={{0,4},{2,6},{4,0},{6,2},{1,5},{3,7},{5,1},{7,3},{8,12},{10,14},{12... | collective-permute-start | bytes 294920 | tf_op jit(solution)/shard_map/ppermute | solution.py:24
  5.8 0.8 collective-permute-start.9
  6.6 0.7 collective-permute-start
  7.3 0.5 collective-permute-done.8
  7.9 2.4 %collective-permute-done.9 = bf16[192,256]{1,0:T(8,128)(2,1)S(1)} collective-permute-done((bf16[192,256]{1,0:T(8,128)(2,1)S(1)}, bf16[192,256]{1,0:T(8,128)(2,1)S(1)}, u32[]{:S(2)}, u32[]{:S(2)}) %collective-permute-start.9) | collective-permute-done | bytes 98336 | tf_op jit(solution)/shard_map/ppermute | solution.py:24
  10.3 2.8 %collective-permute-start.13 = (bf16[384,256]{1,0:T(8,128)(2,1)S(1)}, bf16[384,256]{1,0:T(8,128)(2,1)S(1)}, u32[]{:S(2)}, u32[]{:S(2)}) collective-permute-start(bf16[384,256]{1,0:T(8,128)(2,1)S(1)} %get-tuple-element.51), channel_id=1, source_target_pairs={{0,64},{32,96},{64,0},{96,32},{1,65},{33,97},{65,1},{97,33},{2,66}... | collective-permute-start | bytes 589832 | tf_op jit(solution)/shard_map/ppermute | solution.py:24
  13.2 0.9 collective-permute-start.14
  14.1 0.6 collective-permute-start.10
  14.8 3.7 %collective-permute-start.4 = (bf16[384,256]{1,0:T(8,128)(2,1)S(1)}, bf16[384,256]{1,0:T(8,128)(2,1)S(1)}, u32[]{:S(2)}, u32[]{:S(2)}) collective-permute-start(bf16[384,256]{1,0:T(8,128)(2,1)S(1)} %pad_maximum_fusion.1), channel_id=1, source_target_pairs={{0,16},{8,24},{16,0},{24,8},{1,17},{9,25},{17,1},{25,9},{2,18},{10... | collective-permute-start | bytes 589832 | tf_op jit(solution)/shard_map/ppermute | solution.py:24
  18.5 0.4 collective-permute-start.5
  18.9 1.0 collective-permute-start.1
  19.9 1.2 %collective-permute-done.14 = bf16[384,256]{1,0:T(8,128)(2,1)S(1)} collective-permute-done((bf16[384,256]{1,0:T(8,128)(2,1)S(1)}, bf16[384,256]{1,0:T(8,128)(2,1)S(1)}, u32[]{:S(2)}, u32[]{:S(2)}) %collective-permute-start.14) | collective-permute-done | bytes 196640 | tf_op jit(solution)/shard_map/ppermute | solution.py:24
  21.2 3.8 %collective-permute-start.15 = (bf16[768,256]{1,0:T(8,128)(2,1)S(1)}, bf16[768,256]{1,0:T(8,128)(2,1)S(1)}, u32[]{:S(2)}, u32[]{:S(2)}) collective-permute-start(bf16[768,256]{1,0:T(8,128)(2,1)S(1)} %constant_dynamic-update-slice_fusion.7.refs_7_), channel_id=1, source_target_pairs={{0,24},{8,0},{16,8},{24,16},{1,25},{9,1},{17,9},{25,17},{2,26},{10... | collective-permute-start | bytes 1179656 | tf_op jit(solution)/shard_map/ppermute | solution.py:24
  25.2 2.8 %collective-permute-start.17 = (bf16[192,512]{1,0:T(8,128)(2,1)S(1)}, bf16[192,512]{1,0:T(8,128)(2,1)S(1)}, u32[]{:S(2)}, u32[]{:S(2)}) collective-permute-start(bf16[192,512]{1,0:T(8,128)(2,1)S(1)} %get-tuple-element.44), channel_id=1, source_target_pairs={{0,2},{2,4},{4,6},{6,0},{1,3},{3,5},{5,7},{7,1},{8,10},{10,12},{12... | collective-permute-start | bytes 589832 | tf_op jit(solution)/shard_map/ppermute | solution.py:24
  28.0 2.6 %collective-permute-start.18 = (bf16[192,512]{1,0:T(8,128)(2,1)S(1)}, bf16[192,512]{1,0:T(8,128)(2,1)S(1)}, u32[]{:S(2)}, u32[]{:S(2)}) collective-permute-start(bf16[192,512]{1,0:T(8,128)(2,1)S(1)} %get-tuple-element.46), channel_id=1, source_target_pairs={{0,4},{2,6},{4,0},{6,2},{1,5},{3,7},{5,1},{7,3},{8,12},{10,14},{12... | collective-permute-start | bytes 589832 | tf_op jit(solution)/shard_map/ppermute | solution.py:24
  30.6 1.3 %collective-permute-start.19 = (bf16[192,512]{1,0:T(8,128)(2,1)S(1)}, bf16[192,512]{1,0:T(8,128)(2,1)S(1)}, u32[]{:S(2)}, u32[]{:S(2)}) collective-permute-start(bf16[192,512]{1,0:T(8,128)(2,1)S(1)} %get-tuple-element.43), channel_id=1, source_target_pairs={{0,6},{2,0},{4,2},{6,4},{1,7},{3,1},{5,3},{7,5},{8,14},{10,8},{12,... | collective-permute-start | bytes 589832 | tf_op jit(solution)/shard_map/ppermute | solution.py:24
  31.9 0.8 collective-permute-done.17.refs_9_
  32.8 4.8 %collective-permute-done.18.refs_10_ = bf16[192,512]{1,0:T(8,128)(2,1)S(1)} collective-permute-done((bf16[192,512]{1,0:T(8,128)(2,1)S(1)}, bf16[192,512]{1,0:T(8,128)(2,1)S(1)}, u32[]{:S(2)}, u32[]{:S(2)}) %collective-permute-start.18) | collective-permute-done | bytes 196640 | tf_op jit(solution)/shard_map/ppermute | solution.py:24
  37.6 2.4 %collective-permute-start.23 = (bf16[768,256]{1,0:T(8,128)(2,1)S(1)}, bf16[768,256]{1,0:T(8,128)(2,1)}, u32[]{:S(2)}, u32[]{:S(2)}) collective-permute-start(bf16[768,256]{1,0:T(8,128)(2,1)S(1)} %constant_dynamic-update-slice_fusion.4.refs_6_), channel_id=1, source_target_pairs={{0,24},{8,0},{16,8},{24,16},{1,25},{9,1},{17,9},{25,17},{2,26},{10... | collective-permute-start | bytes 1179656 | tf_op jit(solution)/shard_map/ppermute | solution.py:24
  40.0 4.8 %collective-permute-start.6 = (bf16[768,256]{1,0:T(8,128)(2,1)S(1)}, bf16[768,256]{1,0:T(8,128)(2,1)}, u32[]{:S(2)}, u32[]{:S(2)}) collective-permute-start(bf16[768,256]{1,0:T(8,128)(2,1)S(1)} %constant_dynamic-update-slice_fusion.refs_5_), channel_id=1, source_target_pairs={{0,96},{32,0},{64,32},{96,64},{1,97},{33,1},{65,33},{97,65},{2,98}... | collective-permute-start | bytes 1179656 | tf_op jit(solution)/shard_map/ppermute | solution.py:24
  44.7 0.2 collective-permute-start.2
  44.9 0.2 convert_reduce_fusion.1
  45.2 1.0 convert_reduce_fusion.refs_2_
  46.2 4.8 %collective-permute-done.6.refs_5_ = bf16[768,256]{1,0:T(8,128)(2,1)} collective-permute-done((bf16[768,256]{1,0:T(8,128)(2,1)S(1)}, bf16[768,256]{1,0:T(8,128)(2,1)}, u32[]{:S(2)}, u32[]{:S(2)}) %collective-permute-start.6) | collective-permute-done | bytes 393248 | tf_op jit(solution)/shard_map/ppermute | solution.py:24
  51.0 3.5 %collective-permute-start.21 = (bf16[768,256]{1,0:T(8,128)(2,1)S(1)}, bf16[768,256]{1,0:T(8,128)(2,1)S(1)}, u32[]{:S(2)}, u32[]{:S(2)}) collective-permute-start(bf16[768,256]{1,0:T(8,128)(2,1)S(1)} %pad_maximum_fusion.refs_4_), channel_id=1, source_target_pairs={{0,96},{32,0},{64,32},{96,64},{1,97},{33,1},{65,33},{97,65},{2,98}... | collective-permute-start | bytes 1179656 | tf_op jit(solution)/shard_map/ppermute | solution.py:24
  54.6 8.1 %collective-permute-done.2.refs_4_ = bf16[768,256]{1,0:T(8,128)(2,1)} collective-permute-done((bf16[768,256]{1,0:T(8,128)(2,1)S(1)}, bf16[768,256]{1,0:T(8,128)(2,1)}, u32[]{:S(2)}, u32[]{:S(2)}) %collective-permute-start.2) | collective-permute-done | bytes 393248 | tf_op jit(solution)/shard_map/ppermute | solution.py:24
  62.7 1.3 %collective-permute-start.16 = (bf16[768,256]{1,0:T(8,128)(2,1)S(1)}, bf16[768,256]{1,0:T(8,128)(2,1)S(1)}, u32[]{:S(2)}, u32[]{:S(2)}) collective-permute-start(bf16[768,256]{1,0:T(8,128)(2,1)S(1)} %collective-permute-done.15.refs_7_), channel_id=1, source_target_pairs={{0,24},{8,0},{16,8},{24,16},{1,25},{9,1},{17,9},{25,17},{2,26},{10... | collective-permute-start | bytes 1179656 | tf_op jit(solution)/shard_map/ppermute | solution.py:24
  64.2 1.5 %collective-permute-start.3 = (bf16[768,256]{1,0:T(8,128)(2,1)}, bf16[768,256]{1,0:T(8,128)(2,1)S(1)}, u32[]{:S(2)}, u32[]{:S(2)}) collective-permute-start(bf16[768,256]{1,0:T(8,128)(2,1)} %collective-permute-done.2.refs_4_), channel_id=1, source_target_pairs={{0,32},{32,64},{64,96},{96,0},{1,33},{33,65},{65,97},{97,1},{2,34}... | collective-permute-start | bytes 1179656 | tf_op jit(solution)/shard_map/ppermute | solution.py:24
  65.6 6.5 %shard_map.64 = (bf16[8,384,128]{2,1,0:T(8,128)(2,1)S(1)}, f32[8,384,128]{2,1,0:T(8,128)S(1)}, f32[8,384,256]{2,1,0:T(8,128)S(1)}, bf16[2048,4096]{1,0:T(8,128)(2,1)S(1)}) custom-call(s32[4]{0:T(128)S(1)} %pad_add_fusion.refs_0_.coords, s32[128]{0:T(128)S(1)} %copy-done.1, s32[8]{0:T(128)S(1)} %convert_reduce_fusion.refs_2_, ...), custom_call_target="tpu_custom_call" | custom-call | flops 2000000000 | bytes 2500000 | tf_op jit(solution)/shard_map/pallas_call | solution.py:220
  72.1 4.6 %shard_map.65 = (f32[8,384,128]{2,1,0:T(8,128)S(1)}, f32[8,384,256]{2,1,0:T(8,128)S(1)}) custom-call(s32[4]{0:T(128)S(1)} %pad_add_fusion.refs_0_.coords, s32[128]{0:T(128)S(1)} %copy-done.1, s32[8]{0:T(128)S(1)} %convert_reduce_fusion.refs_2_, s32[136]{0:T(256)S(1)} %get-tuple-element.37.refs_3_, ...), custom_call_target="tpu_custom_call", output_to_operand_aliasing={{0}: (9, {}), {1}: (10, {})} | custom-call | flops 2000000000 | bytes 2500000 | tf_op jit(solution)/shard_map/pallas_call | solution.py:220
  76.7 4.9 %shard_map.66 = (f32[8,384,128]{2,1,0:T(8,128)S(1)}, f32[8,384,256]{2,1,0:T(8,128)S(1)}) custom-call(s32[4]{0:T(128)S(1)} %pad_add_fusion.refs_0_.coords, s32[128]{0:T(128)S(1)} %copy-done.1, s32[8]{0:T(128)S(1)} %convert_reduce_fusion.refs_2_, s32[136]{0:T(256)S(1)} %get-tuple-element.38.refs_3_, ...), custom_call_target="tpu_custom_call", output_to_operand_aliasing={{0}: (9, {}), {1}: (10, {})} | custom-call | flops 2000000000 | bytes 2500000 | tf_op jit(solution)/shard_map/pallas_call | solution.py:220
  81.6 4.5 %shard_map.67 = (f32[8,384,128]{2,1,0:T(8,128)S(1)}, f32[8,384,256]{2,1,0:T(8,128)S(1)}, bf16[96,512]{1,0:T(8,128)(2,1)S(1)}, bf16[96,512]{1,0:T(8,128)(2,1)S(1)...) custom-call(s32[4]{0:T(128)S(1)} %pad_add_fusion.refs_0_.coords, ...), custom_call_target="tpu_custom_call", output_to_operand_aliasing={{0}: (9, {}), {1}: (10, {})} | custom-call | flops 2000000000 | bytes 2500000 | tf_op jit(solution)/shard_map/pallas_call | solution.py:220
  86.1 2.7 %collective-permute-start.27 = (bf16[96,512]{1,0:T(8,128)(2,1)S(1)}, bf16[96,512]{1,0:T(8,128)(2,1)S(1)}, u32[]{:S(2)}, u32[]{:S(2)}) collective-permute-start(bf16[96,512]{1,0:T(8,128)(2,1)S(1)} %get-tuple-element.34), channel_id=1, source_target_pairs={{0,6},{2,0},{4,2},{6,4},{1,7},{3,1},{5,3},{7,5},{8,14},{10,8},{12,... | collective-permute-start | bytes 294920 | tf_op jit(solution)/shard_map/ppermute | solution.py:24
  88.8 2.1 %collective-permute-start.28 = (bf16[96,512]{1,0:T(8,128)(2,1)S(1)}, bf16[96,512]{1,0:T(8,128)(2,1)S(1)}, u32[]{:S(2)}, u32[]{:S(2)}) collective-permute-start(bf16[96,512]{1,0:T(8,128)(2,1)S(1)} %get-tuple-element.35), channel_id=1, source_target_pairs={{0,4},{2,6},{4,0},{6,2},{1,5},{3,7},{5,1},{7,3},{8,12},{10,14},{12... | collective-permute-start | bytes 294920 | tf_op jit(solution)/shard_map/ppermute | solution.py:24
  90.9 0.2 collective-permute-done.27.o1
  91.1 2.7 %collective-permute-done.28.o2 = bf16[96,512]{1,0:T(8,128)(2,1)S(1)} collective-permute-done((bf16[96,512]{1,0:T(8,128)(2,1)S(1)}, bf16[96,512]{1,0:T(8,128)(2,1)S(1)}, u32[]{:S(2)}, u32[]{:S(2)}) %collective-permute-start.28) | collective-permute-done | bytes 98336 | tf_op jit(solution)/shard_map/ppermute | solution.py:24
  93.8 1.8 %collective-permute-done.29.o3 = bf16[96,512]{1,0:T(8,128)(2,1)S(1)} collective-permute-done((bf16[96,512]{1,0:T(8,128)(2,1)S(1)}, bf16[96,512]{1,0:T(8,128)(2,1)S(1)}, u32[]{:S(2)}, u32[]{:S(2)}) %collective-permute-start.29) | collective-permute-done | bytes 98336 | tf_op jit(solution)/shard_map/ppermute | solution.py:24
  95.5 3.5 %project.3 = bf16[96,4096]{1,0:T(8,128)(2,1)S(1)} custom-call(s32[4]{0:T(128)S(1)} %pad_add_fusion.refs_0_.coords, bf16[96,512]{1,0:T(8,128)(2,1)S(1)} %get-tuple-element.33.o0, bf16[96,512]{1,0:T(8,128)(2,1)S(1)} %collective-permute-done.27.o1, bf16[96,512]{1,0:T(8,128)(2,1)S(1)} %collective-permute-done.28.o2, ...), custom_call_target="tpu_custom_call" | custom-call | flops 1610612736 | bytes 16777216 | tf_op jit(solution)/shard_map/project/pallas_call | solution.py:253
  99.1 4.1 %collective-permute-start.30 = (bf16[96,4096]{1,0:T(8,128)(2,1)S(1)}, bf16[96,4096]{1,0:T(8,128)(2,1)S(1)}, u32[]{:S(2)}, u32[]{:S(2)}) collective-permute-start(bf16[96,4096]{1,0:T(8,128)(2,1)S(1)} %project.3), channel_id=1, source_target_pairs={{0,1},{1,0},{2,3},{3,2},{4,5},{5,4},{6,7},{7,6},{8,9},{9,8},{10,11... | collective-permute-start | bytes 2359304 | tf_op jit(solution)/shard_map/ppermute | solution.py:316
  103.3 1.3 %collective-permute-start.25 = (bf16[96,512]{1,0:T(8,128)(2,1)S(1)}, bf16[96,512]{1,0:T(8,128)(2,1)S(1)}, u32[]{:S(2)}, u32[]{:S(2)}) collective-permute-start(bf16[96,512]{1,0:T(8,128)(2,1)S(1)} %get-tuple-element.30), channel_id=1, source_target_pairs={{0,4},{2,6},{4,0},{6,2},{1,5},{3,7},{5,1},{7,3},{8,12},{10,14},{12... | collective-permute-start | bytes 294920 | tf_op jit(solution)/shard_map/ppermute | solution.py:24
  104.6 0.3 collective-permute-start.26
  104.9 2.6 %collective-permute-done.24.o1 = bf16[96,512]{1,0:T(8,128)(2,1)S(1)} collective-permute-done((bf16[96,512]{1,0:T(8,128)(2,1)S(1)}, bf16[96,512]{1,0:T(8,128)(2,1)S(1)}, u32[]{:S(2)}, u32[]{:S(2)}) %collective-permute-start.24) | collective-permute-done | bytes 98336 | tf_op jit(solution)/shard_map/ppermute | solution.py:24
  107.5 1.3 %collective-permute-done.25.o2 = bf16[96,512]{1,0:T(8,128)(2,1)S(1)} collective-permute-done((bf16[96,512]{1,0:T(8,128)(2,1)S(1)}, bf16[96,512]{1,0:T(8,128)(2,1)S(1)}, u32[]{:S(2)}, u32[]{:S(2)}) %collective-permute-start.25) | collective-permute-done | bytes 98336 | tf_op jit(solution)/shard_map/ppermute | solution.py:24
  108.8 2.8 %collective-permute-done.26.o3 = bf16[96,512]{1,0:T(8,128)(2,1)S(1)} collective-permute-done((bf16[96,512]{1,0:T(8,128)(2,1)S(1)}, bf16[96,512]{1,0:T(8,128)(2,1)S(1)}, u32[]{:S(2)}, u32[]{:S(2)}) %collective-permute-start.26) | collective-permute-done | bytes 98336 | tf_op jit(solution)/shard_map/ppermute | solution.py:24
  111.6 3.4 %project.2 = f32[96,4096]{1,0:T(8,128)S(1)} custom-call(s32[4]{0:T(128)S(1)} %pad_add_fusion.refs_0_.coords, bf16[96,512]{1,0:T(8,128)(2,1)S(1)} %get-tuple-element.28.o0, bf16[96,512]{1,0:T(8,128)(2,1)S(1)} %collective-permute-done.24.o1, bf16[96,512]{1,0:T(8,128)(2,1)S(1)} %collective-permute-done.25.o2, bf16[96,512]{1,0:T(8,128)(2,1)S(1)} %collective-permute-done.26.o3, ...), custom_call_target="tpu_custom_call" | custom-call | flops 1610612736 | bytes 16777216 | tf_op jit(solution)/shard_map/project/pallas_call | solution.py:253
  115.0 1.1 add_convert_fusion
  (45 shorter events, 0.8 us)
Async XLA Ops:
  0.0 0.9 copy-start
  0.0 13.1 %copy-start.2 = (bf16[192,2048]{1,0:T(8,128)(2,1)S(1)}, bf16[192,2048]{1,0:T(8,128)(2,1)}, u32[]{:S(2)}) copy-start(bf16[192,2048]{1,0:T(8,128)(2,1)} %param.6) | copy-start | bytes 2359300
  2.0 5.8 %collective-permute-start.8 = (bf16[192,256]{1,0:T(8,128)(2,1)S(1)}, bf16[192,256]{1,0:T(8,128)(2,1)S(1)}, u32[]{:S(2)}, u32[]{:S(2)}) collective-permute-start(bf16[192,256]{1,0:T(8,128)(2,1)S(1)} %get-tuple-element.48), channel_id=1, source_target_pairs={{0,4},{2,6},{4,0},{6,2},{1,5},{3,7},{5,1},{7,3},{8,12},{10,14},{12... | collective-permute-start | bytes 294920 | tf_op jit(solution)/shard_map/ppermute | solution.py:24
  5.8 4.4 %collective-permute-start.9 = (bf16[192,256]{1,0:T(8,128)(2,1)S(1)}, bf16[192,256]{1,0:T(8,128)(2,1)S(1)}, u32[]{:S(2)}, u32[]{:S(2)}) collective-permute-start(bf16[192,256]{1,0:T(8,128)(2,1)S(1)} %get-tuple-element.47), channel_id=1, source_target_pairs={{0,6},{2,0},{4,2},{6,4},{1,7},{3,1},{5,3},{7,5},{8,14},{10,8},{12,... | collective-permute-start | bytes 294920 | tf_op jit(solution)/shard_map/ppermute | solution.py:24
  6.6 8.1 %collective-permute-start = (bf16[192,256]{1,0:T(8,128)(2,1)S(1)}, bf16[192,256]{1,0:T(8,128)(2,1)S(1)}, u32[]{:S(2)}, u32[]{:S(2)}) collective-permute-start(bf16[192,256]{1,0:T(8,128)(2,1)S(1)} %get-tuple-element.49), channel_id=1, source_target_pairs={{0,2},{2,4},{4,6},{6,0},{1,3},{3,5},{5,7},{7,1},{8,10},{10,12},{12... | collective-permute-start | bytes 294920 | tf_op jit(solution)/shard_map/ppermute | solution.py:24
  10.3 8.6 %collective-permute-start.13 = (bf16[384,256]{1,0:T(8,128)(2,1)S(1)}, bf16[384,256]{1,0:T(8,128)(2,1)S(1)}, u32[]{:S(2)}, u32[]{:S(2)}) collective-permute-start(bf16[384,256]{1,0:T(8,128)(2,1)S(1)} %get-tuple-element.51), channel_id=1, source_target_pairs={{0,64},{32,96},{64,0},{96,32},{1,65},{33,97},{65,1},{97,33},{2,66}... | collective-permute-start | bytes 589832 | tf_op jit(solution)/shard_map/ppermute | solution.py:24
  13.2 7.9 %collective-permute-start.14 = (bf16[384,256]{1,0:T(8,128)(2,1)S(1)}, bf16[384,256]{1,0:T(8,128)(2,1)S(1)}, u32[]{:S(2)}, u32[]{:S(2)}) collective-permute-start(bf16[384,256]{1,0:T(8,128)(2,1)S(1)} %get-tuple-element.51), channel_id=1, source_target_pairs={{0,96},{32,0},{64,32},{96,64},{1,97},{33,1},{65,33},{97,65},{2,98}... | collective-permute-start | bytes 589832 | tf_op jit(solution)/shard_map/ppermute | solution.py:24
  14.1 10.9 %collective-permute-start.10 = (bf16[384,256]{1,0:T(8,128)(2,1)S(1)}, bf16[384,256]{1,0:T(8,128)(2,1)S(1)}, u32[]{:S(2)}, u32[]{:S(2)}) collective-permute-start(bf16[384,256]{1,0:T(8,128)(2,1)S(1)} %get-tuple-element.51), channel_id=1, source_target_pairs={{0,32},{32,64},{64,96},{96,0},{1,33},{33,65},{65,97},{97,1},{2,34}... | collective-permute-start | bytes 589832 | tf_op jit(solution)/shard_map/ppermute | solution.py:24
  14.8 30.2 %copy-start.1 = (s32[128]{0:T(128)S(1)}, s32[128]{0:T(128)}, u32[]{:S(2)}) copy-start(s32[128]{0:T(128)} %refs_1_.7) | copy-start | bytes 1540
  14.8 10.4 %collective-permute-start.4 = (bf16[384,256]{1,0:T(8,128)(2,1)S(1)}, bf16[384,256]{1,0:T(8,128)(2,1)S(1)}, u32[]{:S(2)}, u32[]{:S(2)}) collective-permute-start(bf16[384,256]{1,0:T(8,128)(2,1)S(1)} %pad_maximum_fusion.1), channel_id=1, source_target_pairs={{0,16},{8,24},{16,0},{24,8},{1,17},{9,25},{17,1},{25,9},{2,18},{10... | collective-permute-start | bytes 589832 | tf_op jit(solution)/shard_map/ppermute | solution.py:24
  18.5 9.5 %collective-permute-start.5 = (bf16[384,256]{1,0:T(8,128)(2,1)S(1)}, bf16[384,256]{1,0:T(8,128)(2,1)S(1)}, u32[]{:S(2)}, u32[]{:S(2)}) collective-permute-start(bf16[384,256]{1,0:T(8,128)(2,1)S(1)} %pad_maximum_fusion.1), channel_id=1, source_target_pairs={{0,24},{8,0},{16,8},{24,16},{1,25},{9,1},{17,9},{25,17},{2,26},{10... | collective-permute-start | bytes 589832 | tf_op jit(solution)/shard_map/ppermute | solution.py:24
  18.9 11.7 %collective-permute-start.1 = (bf16[384,256]{1,0:T(8,128)(2,1)S(1)}, bf16[384,256]{1,0:T(8,128)(2,1)S(1)}, u32[]{:S(2)}, u32[]{:S(2)}) collective-permute-start(bf16[384,256]{1,0:T(8,128)(2,1)S(1)} %pad_maximum_fusion.1), channel_id=1, source_target_pairs={{0,8},{8,16},{16,24},{24,0},{1,9},{9,17},{17,25},{25,1},{2,10},{10... | collective-permute-start | bytes 589832 | tf_op jit(solution)/shard_map/ppermute | solution.py:24
  21.2 23.5 %collective-permute-start.15 = (bf16[768,256]{1,0:T(8,128)(2,1)S(1)}, bf16[768,256]{1,0:T(8,128)(2,1)S(1)}, u32[]{:S(2)}, u32[]{:S(2)}) collective-permute-start(bf16[768,256]{1,0:T(8,128)(2,1)S(1)} %constant_dynamic-update-slice_fusion.7.refs_7_), channel_id=1, source_target_pairs={{0,24},{8,0},{16,8},{24,16},{1,25},{9,1},{17,9},{25,17},{2,26},{10... | collective-permute-start | bytes 1179656 | tf_op jit(solution)/shard_map/ppermute | solution.py:24
  25.0 19.7 %collective-permute-start.11 = (bf16[768,256]{1,0:T(8,128)(2,1)S(1)}, bf16[768,256]{1,0:T(8,128)(2,1)S(1)}, u32[]{:S(2)}, u32[]{:S(2)}) collective-permute-start(bf16[768,256]{1,0:T(8,128)(2,1)S(1)} %constant_dynamic-update-slice_fusion.4.refs_6_), channel_id=1, source_target_pairs={{0,8},{8,16},{16,24},{24,0},{1,9},{9,17},{17,25},{25,1},{2,10},{10... | collective-permute-start | bytes 1179656 | tf_op jit(solution)/shard_map/ppermute | solution.py:24
  25.2 7.6 %collective-permute-start.17 = (bf16[192,512]{1,0:T(8,128)(2,1)S(1)}, bf16[192,512]{1,0:T(8,128)(2,1)S(1)}, u32[]{:S(2)}, u32[]{:S(2)}) collective-permute-start(bf16[192,512]{1,0:T(8,128)(2,1)S(1)} %get-tuple-element.44), channel_id=1, source_target_pairs={{0,2},{2,4},{4,6},{6,0},{1,3},{3,5},{5,7},{7,1},{8,10},{10,12},{12... | collective-permute-start | bytes 589832 | tf_op jit(solution)/shard_map/ppermute | solution.py:24
  28.0 9.6 %collective-permute-start.18 = (bf16[192,512]{1,0:T(8,128)(2,1)S(1)}, bf16[192,512]{1,0:T(8,128)(2,1)S(1)}, u32[]{:S(2)}, u32[]{:S(2)}) collective-permute-start(bf16[192,512]{1,0:T(8,128)(2,1)S(1)} %get-tuple-element.46), channel_id=1, source_target_pairs={{0,4},{2,6},{4,0},{6,2},{1,5},{3,7},{5,1},{7,3},{8,12},{10,14},{12... | collective-permute-start | bytes 589832 | tf_op jit(solution)/shard_map/ppermute | solution.py:24
  30.6 9.4 %collective-permute-start.19 = (bf16[192,512]{1,0:T(8,128)(2,1)S(1)}, bf16[192,512]{1,0:T(8,128)(2,1)S(1)}, u32[]{:S(2)}, u32[]{:S(2)}) collective-permute-start(bf16[192,512]{1,0:T(8,128)(2,1)S(1)} %get-tuple-element.43), channel_id=1, source_target_pairs={{0,6},{2,0},{4,2},{6,4},{1,7},{3,1},{5,3},{7,5},{8,14},{10,8},{12,... | collective-permute-start | bytes 589832 | tf_op jit(solution)/shard_map/ppermute | solution.py:24
  32.8 31.2 %collective-permute-start.22 = (bf16[768,256]{1,0:T(8,128)(2,1)S(1)}, bf16[768,256]{1,0:T(8,128)(2,1)}, u32[]{:S(2)}, u32[]{:S(2)}) collective-permute-start(bf16[768,256]{1,0:T(8,128)(2,1)S(1)} %constant_dynamic-update-slice_fusion.7.refs_7_), channel_id=1, source_target_pairs={{0,8},{8,16},{16,24},{24,0},{1,9},{9,17},{17,25},{25,1},{2,10},{10... | collective-permute-start | bytes 1179656 | tf_op jit(solution)/shard_map/ppermute | solution.py:24
  37.6 26.6 %collective-permute-start.23 = (bf16[768,256]{1,0:T(8,128)(2,1)S(1)}, bf16[768,256]{1,0:T(8,128)(2,1)}, u32[]{:S(2)}, u32[]{:S(2)}) collective-permute-start(bf16[768,256]{1,0:T(8,128)(2,1)S(1)} %constant_dynamic-update-slice_fusion.4.refs_6_), channel_id=1, source_target_pairs={{0,24},{8,0},{16,8},{24,16},{1,25},{9,1},{17,9},{25,17},{2,26},{10... | collective-permute-start | bytes 1179656 | tf_op jit(solution)/shard_map/ppermute | solution.py:24
  40.0 11.1 %collective-permute-start.6 = (bf16[768,256]{1,0:T(8,128)(2,1)S(1)}, bf16[768,256]{1,0:T(8,128)(2,1)}, u32[]{:S(2)}, u32[]{:S(2)}) collective-permute-start(bf16[768,256]{1,0:T(8,128)(2,1)S(1)} %constant_dynamic-update-slice_fusion.refs_5_), channel_id=1, source_target_pairs={{0,96},{32,0},{64,32},{96,64},{1,97},{33,1},{65,33},{97,65},{2,98}... | collective-permute-start | bytes 1179656 | tf_op jit(solution)/shard_map/ppermute | solution.py:24
  44.7 19.4 %collective-permute-start.20 = (bf16[768,256]{1,0:T(8,128)(2,1)S(1)}, bf16[768,256]{1,0:T(8,128)(2,1)}, u32[]{:S(2)}, u32[]{:S(2)}) collective-permute-start(bf16[768,256]{1,0:T(8,128)(2,1)S(1)} %constant_dynamic-update-slice_fusion.refs_5_), channel_id=1, source_target_pairs={{0,32},{32,64},{64,96},{96,0},{1,33},{33,65},{65,97},{97,1},{2,34}... | collective-permute-start | bytes 1179656 | tf_op jit(solution)/shard_map/ppermute | solution.py:24
  44.7 17.9 %collective-permute-start.2 = (bf16[768,256]{1,0:T(8,128)(2,1)S(1)}, bf16[768,256]{1,0:T(8,128)(2,1)}, u32[]{:S(2)}, u32[]{:S(2)}) collective-permute-start(bf16[768,256]{1,0:T(8,128)(2,1)S(1)} %pad_maximum_fusion.refs_4_), channel_id=1, source_target_pairs={{0,32},{32,64},{64,96},{96,0},{1,33},{33,65},{65,97},{97,1},{2,34}... | collective-permute-start | bytes 1179656 | tf_op jit(solution)/shard_map/ppermute | solution.py:24
  51.0 25.6 %collective-permute-start.21 = (bf16[768,256]{1,0:T(8,128)(2,1)S(1)}, bf16[768,256]{1,0:T(8,128)(2,1)S(1)}, u32[]{:S(2)}, u32[]{:S(2)}) collective-permute-start(bf16[768,256]{1,0:T(8,128)(2,1)S(1)} %pad_maximum_fusion.refs_4_), channel_id=1, source_target_pairs={{0,96},{32,0},{64,32},{96,64},{1,97},{33,1},{65,33},{97,65},{2,98}... | collective-permute-start | bytes 1179656 | tf_op jit(solution)/shard_map/ppermute | solution.py:24
  62.7 18.9 %collective-permute-start.16 = (bf16[768,256]{1,0:T(8,128)(2,1)S(1)}, bf16[768,256]{1,0:T(8,128)(2,1)S(1)}, u32[]{:S(2)}, u32[]{:S(2)}) collective-permute-start(bf16[768,256]{1,0:T(8,128)(2,1)S(1)} %collective-permute-done.15.refs_7_), channel_id=1, source_target_pairs={{0,24},{8,0},{16,8},{24,16},{1,25},{9,1},{17,9},{25,17},{2,26},{10... | collective-permute-start | bytes 1179656 | tf_op jit(solution)/shard_map/ppermute | solution.py:24
  64.0 17.6 %collective-permute-start.12 = (bf16[768,256]{1,0:T(8,128)(2,1)S(1)}, bf16[768,256]{1,0:T(8,128)(2,1)S(1)}, u32[]{:S(2)}, u32[]{:S(2)}) collective-permute-start(bf16[768,256]{1,0:T(8,128)(2,1)S(1)} %collective-permute-done.11.refs_6_), channel_id=1, source_target_pairs={{0,8},{8,16},{16,24},{24,0},{1,9},{9,17},{17,25},{25,1},{2,10},{10... | collective-permute-start | bytes 1179656 | tf_op jit(solution)/shard_map/ppermute | solution.py:24
  64.1 17.5 %collective-permute-start.7 = (bf16[768,256]{1,0:T(8,128)(2,1)}, bf16[768,256]{1,0:T(8,128)(2,1)S(1)}, u32[]{:S(2)}, u32[]{:S(2)}) collective-permute-start(bf16[768,256]{1,0:T(8,128)(2,1)} %collective-permute-done.6.refs_5_), channel_id=1, source_target_pairs={{0,96},{32,0},{64,32},{96,64},{1,97},{33,1},{65,33},{97,65},{2,98}... | collective-permute-start | bytes 1179656 | tf_op jit(solution)/shard_map/ppermute | solution.py:24
  64.2 17.5 %collective-permute-start.3 = (bf16[768,256]{1,0:T(8,128)(2,1)}, bf16[768,256]{1,0:T(8,128)(2,1)S(1)}, u32[]{:S(2)}, u32[]{:S(2)}) collective-permute-start(bf16[768,256]{1,0:T(8,128)(2,1)} %collective-permute-done.2.refs_4_), channel_id=1, source_target_pairs={{0,32},{32,64},{64,96},{96,0},{1,33},{33,65},{65,97},{97,1},{2,34}... | collective-permute-start | bytes 1179656 | tf_op jit(solution)/shard_map/ppermute | solution.py:24
  86.1 4.9 %collective-permute-start.27 = (bf16[96,512]{1,0:T(8,128)(2,1)S(1)}, bf16[96,512]{1,0:T(8,128)(2,1)S(1)}, u32[]{:S(2)}, u32[]{:S(2)}) collective-permute-start(bf16[96,512]{1,0:T(8,128)(2,1)S(1)} %get-tuple-element.34), channel_id=1, source_target_pairs={{0,6},{2,0},{4,2},{6,4},{1,7},{3,1},{5,3},{7,5},{8,14},{10,8},{12,... | collective-permute-start | bytes 294920 | tf_op jit(solution)/shard_map/ppermute | solution.py:24
  88.8 5.0 %collective-permute-start.28 = (bf16[96,512]{1,0:T(8,128)(2,1)S(1)}, bf16[96,512]{1,0:T(8,128)(2,1)S(1)}, u32[]{:S(2)}, u32[]{:S(2)}) collective-permute-start(bf16[96,512]{1,0:T(8,128)(2,1)S(1)} %get-tuple-element.35), channel_id=1, source_target_pairs={{0,4},{2,6},{4,0},{6,2},{1,5},{3,7},{5,1},{7,3},{8,12},{10,14},{12... | collective-permute-start | bytes 294920 | tf_op jit(solution)/shard_map/ppermute | solution.py:24
  90.9 4.7 %collective-permute-start.29 = (bf16[96,512]{1,0:T(8,128)(2,1)S(1)}, bf16[96,512]{1,0:T(8,128)(2,1)S(1)}, u32[]{:S(2)}, u32[]{:S(2)}) collective-permute-start(bf16[96,512]{1,0:T(8,128)(2,1)S(1)} %get-tuple-element.36), channel_id=1, source_target_pairs={{0,2},{2,4},{4,6},{6,0},{1,3},{3,5},{5,7},{7,1},{8,10},{10,12},{12... | collective-permute-start | bytes 294920 | tf_op jit(solution)/shard_map/ppermute | solution.py:24
  99.1 15.9 %collective-permute-start.30 = (bf16[96,4096]{1,0:T(8,128)(2,1)S(1)}, bf16[96,4096]{1,0:T(8,128)(2,1)S(1)}, u32[]{:S(2)}, u32[]{:S(2)}) collective-permute-start(bf16[96,4096]{1,0:T(8,128)(2,1)S(1)} %project.3), channel_id=1, source_target_pairs={{0,1},{1,0},{2,3},{3,2},{4,5},{5,4},{6,7},{7,6},{8,9},{9,8},{10,11... | collective-permute-start | bytes 2359304 | tf_op jit(solution)/shard_map/ppermute | solution.py:316
  103.2 4.3 %collective-permute-start.24 = (bf16[96,512]{1,0:T(8,128)(2,1)S(1)}, bf16[96,512]{1,0:T(8,128)(2,1)S(1)}, u32[]{:S(2)}, u32[]{:S(2)}) collective-permute-start(bf16[96,512]{1,0:T(8,128)(2,1)S(1)} %get-tuple-element.29), channel_id=1, source_target_pairs={{0,6},{2,0},{4,2},{6,4},{1,7},{3,1},{5,3},{7,5},{8,14},{10,8},{12,... | collective-permute-start | bytes 294920 | tf_op jit(solution)/shard_map/ppermute | solution.py:24
  103.3 5.5 %collective-permute-start.25 = (bf16[96,512]{1,0:T(8,128)(2,1)S(1)}, bf16[96,512]{1,0:T(8,128)(2,1)S(1)}, u32[]{:S(2)}, u32[]{:S(2)}) collective-permute-start(bf16[96,512]{1,0:T(8,128)(2,1)S(1)} %get-tuple-element.30), channel_id=1, source_target_pairs={{0,4},{2,6},{4,0},{6,2},{1,5},{3,7},{5,1},{7,3},{8,12},{10,14},{12... | collective-permute-start | bytes 294920 | tf_op jit(solution)/shard_map/ppermute | solution.py:24
  104.6 7.0 %collective-permute-start.26 = (bf16[96,512]{1,0:T(8,128)(2,1)S(1)}, bf16[96,512]{1,0:T(8,128)(2,1)S(1)}, u32[]{:S(2)}, u32[]{:S(2)}) collective-permute-start(bf16[96,512]{1,0:T(8,128)(2,1)S(1)} %get-tuple-element.31), channel_id=1, source_target_pairs={{0,2},{2,4},{4,6},{6,0},{1,3},{3,5},{5,7},{7,1},{8,10},{10,12},{12... | collective-permute-start | bytes 294920 | tf_op jit(solution)/shard_map/ppermute | solution.py:24

commit v3 on v0

--- a/solution.py
+++ b/solution.py
@@ -42,14 +42,13 @@
     else:
         (q_all,) = take(1)
         take(2)
-    if phase == 1:
+    if first_phase:
         (weight,) = take(1)
-    if first_phase:
         (q_all,) = take(1)
     best_all, acc_all = take(2)
     if last_phase:
         outs = take(8)
-    if phase == 1:
+    if first_phase:
         (weight_held,) = take(1)
         weight_copy = pltpu.make_async_copy(weight, weight_held, refs.pop())
         weight_copy.start()
@@ -172,7 +171,7 @@
     lax.fori_loop(0, pairs, pair, 0)
     accumulate(2 * pairs, p1, f1)
 
-    if phase == 1:
+    if first_phase:
         weight_copy.wait()
     if last_phase:
         for turn in range(2):
@@ -304,8 +303,8 @@
     ranks = [jnp.sum((before & (phase_of == p)[None, :]).astype(jnp.int32), axis=1) for p in range(3)]
 
     scalars = [coords, span_table, starts]
-    q_all, best, acc = run_phase(0, scalars + [ranks[0]], pieces[0], q_part)
-    best, acc, weight = run_phase(1, scalars + [ranks[1]], pieces[1], [q_all, best, acc], out_weight)
+    q_all, best, acc, weight = run_phase(0, scalars + [ranks[0]], pieces[0], q_part, out_weight)
+    best, acc = run_phase(1, scalars + [ranks[1]], pieces[1], [q_all, best, acc])
     o_part = run_phase(2, scalars + [ranks[2]], pieces[2], [q_all, best, acc])[2:]
 
     def returned(part):

time: 115 us -> 110 us (0.957)
  local copies, waits for them, and re-layouts: 10.6 us -> 2.91 us
  waiting for transfers between devices: 25.5 us -> 28 us
    unnamed x26 -> x12, local copies, waits for them, and re-layouts: 7.48 us -> 1.01 us
    ppermute x30, waiting for transfers between devices: 25.5 us -> 28 us  [shift(): lax.ppermute(value, axis, [(i, (i + by) % RING) for i in range(RING)])]
    concatenate x3, local copies, waits for them, and re-layouts: 1.4 us -> 0.04 us  [gathered(): first, second = (jnp.concatenate(near[:2], 0), jnp.concatenate(near[2:], 0))]
  transfers between devices with their start and end apart: 31 -> 31, of which waited for: 11 -> 12; matrix products, arithmetic and copies ran while one was open for 4% -> 2% of each run, Pallas kernels for 14% -> 15%
where the time goes in v3:
time: 110 us; the launch traced here: 109 us
  starting transfers between devices  50.7 us (46%)
  waiting for transfers between devices  28 us (25%)
  Pallas kernels  24.4 us (22%)
  local copies, waits for them, and re-layouts  2.91 us (3%)
  other arithmetic  2.43 us (2%)
    ppermute x30, starting transfers between devices, shift(): lax.ppermute(value, axis, [(i, (i + by) % RING) for i in range(RING)])  46.5 us
    ppermute x30, waiting for transfers between devices, shift(): lax.ppermute(value, axis, [(i, (i + by) % RING) for i in range(RING)])  28 us
    pallas_call x3, Pallas kernels, run_phase(): pl.pallas_call(lambda *refs: phase_kernel(phase, *refs), out_shape=[jax.S...  17.5 us
    pallas_call x2, Pallas kernels, project(): pl.pallas_call(project_kernel, out_shape=jax.ShapeDtypeStruct((SPAN, widt...  6.9 us
    ppermute x1, starting transfers between devices, layer(): lax.ppermute(project(coords, theirs, weight, jnp.bfloat16), 'hd', [(0, 1)...  4.19 us
  transfers between devices with their start and end apart: 31, of which 12 were waited for; matrix products, arithmetic and copies ran while one was open for 2% of the time, Pallas kernels for 15%

profile of v3, /device:TPU:1, one launch (start us, length us, event | category | flops | bytes accessed | tf_op | source)
XLA Modules:
  0.0 108.7 jit_solution(13058824968212162096)
XLA Ops:
  0.0 0.9 copy-done
  1.0 1.0 bitcast_dynamic-update-slice_fusion
  2.0 3.8 %collective-permute-start.8 = (bf16[192,256]{1,0:T(8,128)(2,1)S(1)}, bf16[192,256]{1,0:T(8,128)(2,1)S(1)}, u32[]{:S(2)}, u32[]{:S(2)}) collective-permute-start(bf16[192,256]{1,0:T(8,128)(2,1)S(1)} %get-tuple-element.43), channel_id=1, source_target_pairs={{0,4},{2,6},{4,0},{6,2},{1,5},{3,7},{5,1},{7,3},{8,12},{10,14},{12... | collective-permute-start | bytes 294920 | tf_op jit(solution)/shard_map/ppermute | solution.py:24
  5.8 0.8 collective-permute-start.9
  6.6 0.7 collective-permute-start
  7.3 0.8 constant_dynamic-slice_fusion
  8.1 0.4 collective-permute-start.17
  8.5 1.8 %collective-permute-done.9 = bf16[192,256]{1,0:T(8,128)(2,1)S(1)} collective-permute-done((bf16[192,256]{1,0:T(8,128)(2,1)S(1)}, bf16[192,256]{1,0:T(8,128)(2,1)S(1)}, u32[]{:S(2)}, u32[]{:S(2)}) %collective-permute-start.9) | collective-permute-done | bytes 98336 | tf_op jit(solution)/shard_map/ppermute | solution.py:24
  10.3 2.8 %collective-permute-start.13 = (bf16[384,256]{1,0:T(8,128)(2,1)S(1)}, bf16[384,256]{1,0:T(8,128)(2,1)S(1)}, u32[]{:S(2)}, u32[]{:S(2)}) collective-permute-start(bf16[384,256]{1,0:T(8,128)(2,1)S(1)} %get-tuple-element.46), channel_id=1, source_target_pairs={{0,64},{32,96},{64,0},{96,32},{1,65},{33,97},{65,1},{97,33},{2,66}... | collective-permute-start | bytes 589832 | tf_op jit(solution)/shard_map/ppermute | solution.py:24
  13.2 0.9 collective-permute-start.14
  14.1 0.6 collective-permute-start.10
  14.7 3.7 %collective-permute-start.4 = (bf16[384,256]{1,0:T(8,128)(2,1)S(1)}, bf16[384,256]{1,0:T(8,128)(2,1)S(1)}, u32[]{:S(2)}, u32[]{:S(2)}) collective-permute-start(bf16[384,256]{1,0:T(8,128)(2,1)S(1)} %pad_maximum_fusion.1), channel_id=1, source_target_pairs={{0,16},{8,24},{16,0},{24,8},{1,17},{9,25},{17,1},{25,9},{2,18},{10... | collective-permute-start | bytes 589832 | tf_op jit(solution)/shard_map/ppermute | solution.py:24
  18.4 0.7 collective-permute-start.1
  19.2 2.0 %collective-permute-done.14 = bf16[384,256]{1,0:T(8,128)(2,1)S(1)} collective-permute-done((bf16[384,256]{1,0:T(8,128)(2,1)S(1)}, bf16[384,256]{1,0:T(8,128)(2,1)S(1)}, u32[]{:S(2)}, u32[]{:S(2)}) %collective-permute-start.14) | collective-permute-done | bytes 196640 | tf_op jit(solution)/shard_map/ppermute | solution.py:24
  21.2 3.8 %collective-permute-start.15 = (bf16[768,256]{1,0:T(8,128)(2,1)S(1)}, bf16[768,256]{1,0:T(8,128)(2,1)S(1)}, u32[]{:S(2)}, u32[]{:S(2)}) collective-permute-start(bf16[768,256]{1,0:T(8,128)(2,1)S(1)} %constant_dynamic-update-slice_fusion.7.refs_7_), channel_id=1, source_target_pairs={{0,24},{8,0},{16,8},{24,16},{1,25},{9,1},{17,9},{25,17},{2,26},{10... | collective-permute-start | bytes 1179656 | tf_op jit(solution)/shard_map/ppermute | solution.py:24
  25.0 1.5 %collective-permute-done.1 = bf16[384,256]{1,0:T(8,128)(2,1)S(1)} collective-permute-done((bf16[384,256]{1,0:T(8,128)(2,1)S(1)}, bf16[384,256]{1,0:T(8,128)(2,1)S(1)}, u32[]{:S(2)}, u32[]{:S(2)}) %collective-permute-start.1) | collective-permute-done | bytes 196640 | tf_op jit(solution)/shard_map/ppermute | solution.py:24
  26.5 2.7 %collective-permute-start.5 = (bf16[384,256]{1,0:T(8,128)(2,1)S(1)}, bf16[384,256]{1,0:T(8,128)(2,1)S(1)}, u32[]{:S(2)}, u32[]{:S(2)}) collective-permute-start(bf16[384,256]{1,0:T(8,128)(2,1)S(1)} %pad_maximum_fusion.1), channel_id=1, source_target_pairs={{0,24},{8,0},{16,8},{24,16},{1,25},{9,1},{17,9},{25,17},{2,26},{10... | collective-permute-start | bytes 589832 | tf_op jit(solution)/shard_map/ppermute | solution.py:24
  29.3 1.8 %collective-permute-start.18 = (bf16[192,512]{1,0:T(8,128)(2,1)S(1)}, bf16[192,512]{1,0:T(8,128)(2,1)S(1)}, u32[]{:S(2)}, u32[]{:S(2)}) collective-permute-start(bf16[192,512]{1,0:T(8,128)(2,1)S(1)} %copy-done.3), channel_id=1, source_target_pairs={{0,4},{2,6},{4,0},{6,2},{1,5},{3,7},{5,1},{7,3},{8,12},{10,14},{12... | collective-permute-start | bytes 589832 | tf_op jit(solution)/shard_map/ppermute | solution.py:24
  31.2 2.2 %collective-permute-start.19 = (bf16[192,512]{1,0:T(8,128)(2,1)S(1)}, bf16[192,512]{1,0:T(8,128)(2,1)S(1)}, u32[]{:S(2)}, u32[]{:S(2)}) collective-permute-start(bf16[192,512]{1,0:T(8,128)(2,1)S(1)} %get-tuple-element.38), channel_id=1, source_target_pairs={{0,6},{2,0},{4,2},{6,4},{1,7},{3,1},{5,3},{7,5},{8,14},{10,8},{12,... | collective-permute-start | bytes 589832 | tf_op jit(solution)/shard_map/ppermute | solution.py:24
  33.4 3.4 %collective-permute-done.5 = bf16[384,256]{1,0:T(8,128)(2,1)S(1)} collective-permute-done((bf16[384,256]{1,0:T(8,128)(2,1)S(1)}, bf16[384,256]{1,0:T(8,128)(2,1)S(1)}, u32[]{:S(2)}, u32[]{:S(2)}) %collective-permute-start.5) | collective-permute-done | bytes 196640 | tf_op jit(solution)/shard_map/ppermute | solution.py:24
  36.8 2.7 %collective-permute-start.23 = (bf16[768,256]{1,0:T(8,128)(2,1)S(1)}, bf16[768,256]{1,0:T(8,128)(2,1)}, u32[]{:S(2)}, u32[]{:S(2)}) collective-permute-start(bf16[768,256]{1,0:T(8,128)(2,1)S(1)} %constant_dynamic-update-slice_fusion.4.refs_6_), channel_id=1, source_target_pairs={{0,24},{8,0},{16,8},{24,16},{1,25},{9,1},{17,9},{25,17},{2,26},{10... | collective-permute-start | bytes 1179656 | tf_op jit(solution)/shard_map/ppermute | solution.py:24
  39.6 3.3 %collective-permute-start.20 = (bf16[768,256]{1,0:T(8,128)(2,1)S(1)}, bf16[768,256]{1,0:T(8,128)(2,1)}, u32[]{:S(2)}, u32[]{:S(2)}) collective-permute-start(bf16[768,256]{1,0:T(8,128)(2,1)S(1)} %constant_dynamic-update-slice_fusion.refs_5_), channel_id=1, source_target_pairs={{0,32},{32,64},{64,96},{96,0},{1,33},{33,65},{65,97},{97,1},{2,34}... | collective-permute-start | bytes 1179656 | tf_op jit(solution)/shard_map/ppermute | solution.py:24
  42.8 0.8 collective-permute-start.6
  43.7 0.6 collective-permute-start.2
  44.5 1.8 %collective-permute-done.11.refs_8_ = bf16[768,256]{1,0:T(8,128)(2,1)} collective-permute-done((bf16[768,256]{1,0:T(8,128)(2,1)S(1)}, bf16[768,256]{1,0:T(8,128)(2,1)}, u32[]{:S(2)}, u32[]{:S(2)}) %collective-permute-start.11) | collective-permute-done | bytes 393248 | tf_op jit(solution)/shard_map/ppermute | solution.py:24
  46.3 4.8 %collective-permute-start.21 = (bf16[768,256]{1,0:T(8,128)(2,1)S(1)}, bf16[768,256]{1,0:T(8,128)(2,1)S(1)}, u32[]{:S(2)}, u32[]{:S(2)}) collective-permute-start(bf16[768,256]{1,0:T(8,128)(2,1)S(1)} %pad_maximum_fusion.refs_4_), channel_id=1, source_target_pairs={{0,96},{32,0},{64,32},{96,64},{1,97},{33,1},{65,33},{97,65},{2,98}... | collective-permute-start | bytes 1179656 | tf_op jit(solution)/shard_map/ppermute | solution.py:24
  51.2 1.0 convert_reduce_fusion.refs_2_
  52.2 1.3 %collective-permute-start.16 = (bf16[768,256]{1,0:T(8,128)(2,1)S(1)}, bf16[768,256]{1,0:T(8,128)(2,1)S(1)}, u32[]{:S(2)}, u32[]{:S(2)}) collective-permute-start(bf16[768,256]{1,0:T(8,128)(2,1)S(1)} %collective-permute-done.15.refs_11_), channel_id=1, source_target_pairs={{0,24},{8,0},{16,8},{24,16},{1,25},{9,1},{17,9},{25,17},{2,26},{10... | collective-permute-start | bytes 1179656 | tf_op jit(solution)/shard_map/ppermute | solution.py:24
  53.7 5.5 %collective-permute-done.2.refs_4_ = bf16[768,256]{1,0:T(8,128)(2,1)} collective-permute-done((bf16[768,256]{1,0:T(8,128)(2,1)S(1)}, bf16[768,256]{1,0:T(8,128)(2,1)}, u32[]{:S(2)}, u32[]{:S(2)}) %collective-permute-start.2) | collective-permute-done | bytes 393248 | tf_op jit(solution)/shard_map/ppermute | solution.py:24
  59.2 0.8 collective-permute-start.3
  60.0 6.5 %shard_map.64 = (bf16[8,384,128]{2,1,0:T(8,128)(2,1)S(1)}, f32[8,384,128]{2,1,0:T(8,128)S(1)}, f32[8,384,256]{2,1,0:T(8,128)S(1)}, bf16[2048,4096]{1,0:T(8,128)(2,1)S(1)}) custom-call(s32[4]{0:T(128)S(1)} %pad_add_fusion.refs_0_.coords, s32[128]{0:T(128)S(1)} %copy-done.1, s32[8]{0:T(128)S(1)} %convert_reduce_fusion.refs_2_, ...), custom_call_target="tpu_custom_call" | custom-call | flops 2000000000 | bytes 2500000 | tf_op jit(solution)/shard_map/pallas_call | solution.py:220
  66.5 6.6 %shard_map.65 = (f32[8,384,128]{2,1,0:T(8,128)S(1)}, f32[8,384,256]{2,1,0:T(8,128)S(1)}) custom-call(s32[4]{0:T(128)S(1)} %pad_add_fusion.refs_0_.coords, s32[128]{0:T(128)S(1)} %copy-done.1, s32[8]{0:T(128)S(1)} %convert_reduce_fusion.refs_2_, s32[136]{0:T(256)S(1)} %get-tuple-element.33.refs_3_, ...), custom_call_target="tpu_custom_call", output_to_operand_aliasing={{0}: (13, {}), {1}: (14, {})} | custom-call | flops 4000000000 | bytes 5000000 | tf_op jit(solution)/shard_map/pallas_call | solution.py:220
  73.1 4.5 %shard_map.66 = (f32[8,384,128]{2,1,0:T(8,128)S(1)}, f32[8,384,256]{2,1,0:T(8,128)S(1)}, bf16[96,512]{1,0:T(8,128)(2,1)S(1)}, bf16[96,512]{1,0:T(8,128)(2,1)S(1)...) custom-call(s32[4]{0:T(128)S(1)} %pad_add_fusion.refs_0_.coords, ...), custom_call_target="tpu_custom_call", output_to_operand_aliasing={{0}: (9, {}), {1}: (10, {})} | custom-call | flops 2000000000 | bytes 2500000 | tf_op jit(solution)/shard_map/pallas_call | solution.py:220
  77.6 4.3 %collective-permute-start.27 = (bf16[96,512]{1,0:T(8,128)(2,1)S(1)}, bf16[96,512]{1,0:T(8,128)(2,1)S(1)}, u32[]{:S(2)}, u32[]{:S(2)}) collective-permute-start(bf16[96,512]{1,0:T(8,128)(2,1)S(1)} %get-tuple-element.30), channel_id=1, source_target_pairs={{0,6},{2,0},{4,2},{6,4},{1,7},{3,1},{5,3},{7,5},{8,14},{10,8},{12,... | collective-permute-start | bytes 294920 | tf_op jit(solution)/shard_map/ppermute | solution.py:24
  81.9 0.9 collective-permute-start.28
  82.8 1.7 %collective-permute-done.27.o1 = bf16[96,512]{1,0:T(8,128)(2,1)S(1)} collective-permute-done((bf16[96,512]{1,0:T(8,128)(2,1)S(1)}, bf16[96,512]{1,0:T(8,128)(2,1)S(1)}, u32[]{:S(2)}, u32[]{:S(2)}) %collective-permute-start.27) | collective-permute-done | bytes 98336 | tf_op jit(solution)/shard_map/ppermute | solution.py:24
  84.5 2.4 %collective-permute-done.28.o2 = bf16[96,512]{1,0:T(8,128)(2,1)S(1)} collective-permute-done((bf16[96,512]{1,0:T(8,128)(2,1)S(1)}, bf16[96,512]{1,0:T(8,128)(2,1)S(1)}, u32[]{:S(2)}, u32[]{:S(2)}) %collective-permute-start.28) | collective-permute-done | bytes 98336 | tf_op jit(solution)/shard_map/ppermute | solution.py:24
  86.9 1.0 collective-permute-done.29.o3
  87.9 3.5 %project.3 = bf16[96,4096]{1,0:T(8,128)(2,1)S(1)} custom-call(s32[4]{0:T(128)S(1)} %pad_add_fusion.refs_0_.coords, bf16[96,512]{1,0:T(8,128)(2,1)S(1)} %get-tuple-element.29.o0, bf16[96,512]{1,0:T(8,128)(2,1)S(1)} %collective-permute-done.27.o1, bf16[96,512]{1,0:T(8,128)(2,1)S(1)} %collective-permute-done.28.o2, ...), custom_call_target="tpu_custom_call" | custom-call | flops 1610612736 | bytes 16777216 | tf_op jit(solution)/shard_map/project/pallas_call | solution.py:253
  91.4 4.2 %collective-permute-start.30 = (bf16[96,4096]{1,0:T(8,128)(2,1)S(1)}, bf16[96,4096]{1,0:T(8,128)(2,1)S(1)}, u32[]{:S(2)}, u32[]{:S(2)}) collective-permute-start(bf16[96,4096]{1,0:T(8,128)(2,1)S(1)} %project.3), channel_id=1, source_target_pairs={{0,1},{1,0},{2,3},{3,2},{4,5},{5,4},{6,7},{7,6},{8,9},{9,8},{10,11... | collective-permute-start | bytes 2359304 | tf_op jit(solution)/shard_map/ppermute | solution.py:314
  95.6 0.3 collective-permute-start.24
  95.9 0.8 collective-permute-start.25
  96.7 0.6 collective-permute-start.26
  97.3 2.6 %collective-permute-done.24.o1 = bf16[96,512]{1,0:T(8,128)(2,1)S(1)} collective-permute-done((bf16[96,512]{1,0:T(8,128)(2,1)S(1)}, bf16[96,512]{1,0:T(8,128)(2,1)S(1)}, u32[]{:S(2)}, u32[]{:S(2)}) %collective-permute-start.24) | collective-permute-done | bytes 98336 | tf_op jit(solution)/shard_map/ppermute | solution.py:24
  99.9 1.5 %collective-permute-done.25.o2 = bf16[96,512]{1,0:T(8,128)(2,1)S(1)} collective-permute-done((bf16[96,512]{1,0:T(8,128)(2,1)S(1)}, bf16[96,512]{1,0:T(8,128)(2,1)S(1)}, u32[]{:S(2)}, u32[]{:S(2)}) %collective-permute-start.25) | collective-permute-done | bytes 98336 | tf_op jit(solution)/shard_map/ppermute | solution.py:24
  101.4 2.8 %collective-permute-done.26.o3 = bf16[96,512]{1,0:T(8,128)(2,1)S(1)} collective-permute-done((bf16[96,512]{1,0:T(8,128)(2,1)S(1)}, bf16[96,512]{1,0:T(8,128)(2,1)S(1)}, u32[]{:S(2)}, u32[]{:S(2)}) %collective-permute-start.26) | collective-permute-done | bytes 98336 | tf_op jit(solution)/shard_map/ppermute | solution.py:24
  104.2 3.4 %project.2 = f32[96,4096]{1,0:T(8,128)S(1)} custom-call(s32[4]{0:T(128)S(1)} %pad_add_fusion.refs_0_.coords, bf16[96,512]{1,0:T(8,128)(2,1)S(1)} %get-tuple-element.24.o0, bf16[96,512]{1,0:T(8,128)(2,1)S(1)} %collective-permute-done.24.o1, bf16[96,512]{1,0:T(8,128)(2,1)S(1)} %collective-permute-done.25.o2, bf16[96,512]{1,0:T(8,128)(2,1)S(1)} %collective-permute-done.26.o3, ...), custom_call_target="tpu_custom_call" | custom-call | flops 1610612736 | bytes 16777216 | tf_op jit(solution)/shard_map/project/pallas_call | solution.py:253
  107.6 1.1 add_convert_fusion
  (46 shorter events, 0.9 us)
Async XLA Ops:
  0.0 0.9 copy-start
  0.0 7.3 %copy-start.2 = (bf16[192,2048]{1,0:T(8,128)(2,1)S(1)}, bf16[192,2048]{1,0:T(8,128)(2,1)}, u32[]{:S(2)}) copy-start(bf16[192,2048]{1,0:T(8,128)(2,1)} %param.6) | copy-start | bytes 2359300
  2.0 6.5 %collective-permute-start.8 = (bf16[192,256]{1,0:T(8,128)(2,1)S(1)}, bf16[192,256]{1,0:T(8,128)(2,1)S(1)}, u32[]{:S(2)}, u32[]{:S(2)}) collective-permute-start(bf16[192,256]{1,0:T(8,128)(2,1)S(1)} %get-tuple-element.43), channel_id=1, source_target_pairs={{0,4},{2,6},{4,0},{6,2},{1,5},{3,7},{5,1},{7,3},{8,12},{10,14},{12... | collective-permute-start | bytes 294920 | tf_op jit(solution)/shard_map/ppermute | solution.py:24
  5.8 4.4 %collective-permute-start.9 = (bf16[192,256]{1,0:T(8,128)(2,1)S(1)}, bf16[192,256]{1,0:T(8,128)(2,1)S(1)}, u32[]{:S(2)}, u32[]{:S(2)}) collective-permute-start(bf16[192,256]{1,0:T(8,128)(2,1)S(1)} %get-tuple-element.42), channel_id=1, source_target_pairs={{0,6},{2,0},{4,2},{6,4},{1,7},{3,1},{5,3},{7,5},{8,14},{10,8},{12,... | collective-permute-start | bytes 294920 | tf_op jit(solution)/shard_map/ppermute | solution.py:24
  6.6 8.1 %collective-permute-start = (bf16[192,256]{1,0:T(8,128)(2,1)S(1)}, bf16[192,256]{1,0:T(8,128)(2,1)S(1)}, u32[]{:S(2)}, u32[]{:S(2)}) collective-permute-start(bf16[192,256]{1,0:T(8,128)(2,1)S(1)} %get-tuple-element.44), channel_id=1, source_target_pairs={{0,2},{2,4},{4,6},{6,0},{1,3},{3,5},{5,7},{7,1},{8,10},{10,12},{12... | collective-permute-start | bytes 294920 | tf_op jit(solution)/shard_map/ppermute | solution.py:24
  8.1 21.2 %collective-permute-start.17 = (bf16[192,512]{1,0:T(8,128)(2,1)}, bf16[192,512]{1,0:T(8,128)(2,1)S(1)}, u32[]{:S(2)}, u32[]{:S(2)}) collective-permute-start(bf16[192,512]{1,0:T(8,128)(2,1)} %get-tuple-element.39), channel_id=1, source_target_pairs={{0,2},{2,4},{4,6},{6,0},{1,3},{3,5},{5,7},{7,1},{8,10},{10,12},{12... | collective-permute-start | bytes 589832 | tf_op jit(solution)/shard_map/ppermute | solution.py:24
  8.5 20.8 %copy-start.3 = (bf16[192,512]{1,0:T(8,128)(2,1)S(1)}, bf16[192,512]{1,0:T(8,128)(2,1)}, u32[]{:S(2)}) copy-start(bf16[192,512]{1,0:T(8,128)(2,1)} %get-tuple-element.41) | copy-start | bytes 589828
  10.3 8.1 %collective-permute-start.13 = (bf16[384,256]{1,0:T(8,128)(2,1)S(1)}, bf16[384,256]{1,0:T(8,128)(2,1)S(1)}, u32[]{:S(2)}, u32[]{:S(2)}) collective-permute-start(bf16[384,256]{1,0:T(8,128)(2,1)S(1)} %get-tuple-element.46), channel_id=1, source_target_pairs={{0,64},{32,96},{64,0},{96,32},{1,65},{33,97},{65,1},{97,33},{2,66}... | collective-permute-start | bytes 589832 | tf_op jit(solution)/shard_map/ppermute | solution.py:24
  13.2 8.0 %collective-permute-start.14 = (bf16[384,256]{1,0:T(8,128)(2,1)S(1)}, bf16[384,256]{1,0:T(8,128)(2,1)S(1)}, u32[]{:S(2)}, u32[]{:S(2)}) collective-permute-start(bf16[384,256]{1,0:T(8,128)(2,1)S(1)} %get-tuple-element.46), channel_id=1, source_target_pairs={{0,96},{32,0},{64,32},{96,64},{1,97},{33,1},{65,33},{97,65},{2,98}... | collective-permute-start | bytes 589832 | tf_op jit(solution)/shard_map/ppermute | solution.py:24
  14.1 17.1 %collective-permute-start.10 = (bf16[384,256]{1,0:T(8,128)(2,1)S(1)}, bf16[384,256]{1,0:T(8,128)(2,1)S(1)}, u32[]{:S(2)}, u32[]{:S(2)}) collective-permute-start(bf16[384,256]{1,0:T(8,128)(2,1)S(1)} %get-tuple-element.46), channel_id=1, source_target_pairs={{0,32},{32,64},{64,96},{96,0},{1,33},{33,65},{65,97},{97,1},{2,34}... | collective-permute-start | bytes 589832 | tf_op jit(solution)/shard_map/ppermute | solution.py:24
  14.7 29.6 %copy-start.1 = (s32[128]{0:T(128)S(1)}, s32[128]{0:T(128)}, u32[]{:S(2)}) copy-start(s32[128]{0:T(128)} %refs_1_.5) | copy-start | bytes 1540
  14.7 11.8 %collective-permute-start.4 = (bf16[384,256]{1,0:T(8,128)(2,1)S(1)}, bf16[384,256]{1,0:T(8,128)(2,1)S(1)}, u32[]{:S(2)}, u32[]{:S(2)}) collective-permute-start(bf16[384,256]{1,0:T(8,128)(2,1)S(1)} %pad_maximum_fusion.1), channel_id=1, source_target_pairs={{0,16},{8,24},{16,0},{24,8},{1,17},{9,25},{17,1},{25,9},{2,18},{10... | collective-permute-start | bytes 589832 | tf_op jit(solution)/shard_map/ppermute | solution.py:24
  18.4 8.1 %collective-permute-start.1 = (bf16[384,256]{1,0:T(8,128)(2,1)S(1)}, bf16[384,256]{1,0:T(8,128)(2,1)S(1)}, u32[]{:S(2)}, u32[]{:S(2)}) collective-permute-start(bf16[384,256]{1,0:T(8,128)(2,1)S(1)} %pad_maximum_fusion.1), channel_id=1, source_target_pairs={{0,8},{8,16},{16,24},{24,0},{1,9},{9,17},{17,25},{25,1},{2,10},{10... | collective-permute-start | bytes 589832 | tf_op jit(solution)/shard_map/ppermute | solution.py:24
  21.2 21.6 %collective-permute-start.15 = (bf16[768,256]{1,0:T(8,128)(2,1)S(1)}, bf16[768,256]{1,0:T(8,128)(2,1)S(1)}, u32[]{:S(2)}, u32[]{:S(2)}) collective-permute-start(bf16[768,256]{1,0:T(8,128)(2,1)S(1)} %constant_dynamic-update-slice_fusion.7.refs_7_), channel_id=1, source_target_pairs={{0,24},{8,0},{16,8},{24,16},{1,25},{9,1},{17,9},{25,17},{2,26},{10... | collective-permute-start | bytes 1179656 | tf_op jit(solution)/shard_map/ppermute | solution.py:24
  26.5 17.2 %collective-permute-start.22 = (bf16[768,256]{1,0:T(8,128)(2,1)S(1)}, bf16[768,256]{1,0:T(8,128)(2,1)S(1)}, u32[]{:S(2)}, u32[]{:S(2)}) collective-permute-start(bf16[768,256]{1,0:T(8,128)(2,1)S(1)} %constant_dynamic-update-slice_fusion.7.refs_7_), channel_id=1, source_target_pairs={{0,8},{8,16},{16,24},{24,0},{1,9},{9,17},{17,25},{25,1},{2,10},{10... | collective-permute-start | bytes 1179656 | tf_op jit(solution)/shard_map/ppermute | solution.py:24
  26.5 10.3 %collective-permute-start.5 = (bf16[384,256]{1,0:T(8,128)(2,1)S(1)}, bf16[384,256]{1,0:T(8,128)(2,1)S(1)}, u32[]{:S(2)}, u32[]{:S(2)}) collective-permute-start(bf16[384,256]{1,0:T(8,128)(2,1)S(1)} %pad_maximum_fusion.1), channel_id=1, source_target_pairs={{0,24},{8,0},{16,8},{24,16},{1,25},{9,1},{17,9},{25,17},{2,26},{10... | collective-permute-start | bytes 589832 | tf_op jit(solution)/shard_map/ppermute | solution.py:24
  29.3 7.5 %collective-permute-start.18 = (bf16[192,512]{1,0:T(8,128)(2,1)S(1)}, bf16[192,512]{1,0:T(8,128)(2,1)S(1)}, u32[]{:S(2)}, u32[]{:S(2)}) collective-permute-start(bf16[192,512]{1,0:T(8,128)(2,1)S(1)} %copy-done.3), channel_id=1, source_target_pairs={{0,4},{2,6},{4,0},{6,2},{1,5},{3,7},{5,1},{7,3},{8,12},{10,14},{12... | collective-permute-start | bytes 589832 | tf_op jit(solution)/shard_map/ppermute | solution.py:24
  31.2 8.4 %collective-permute-start.19 = (bf16[192,512]{1,0:T(8,128)(2,1)S(1)}, bf16[192,512]{1,0:T(8,128)(2,1)S(1)}, u32[]{:S(2)}, u32[]{:S(2)}) collective-permute-start(bf16[192,512]{1,0:T(8,128)(2,1)S(1)} %get-tuple-element.38), channel_id=1, source_target_pairs={{0,6},{2,0},{4,2},{6,4},{1,7},{3,1},{5,3},{7,5},{8,14},{10,8},{12,... | collective-permute-start | bytes 589832 | tf_op jit(solution)/shard_map/ppermute | solution.py:24
  36.8 9.5 %collective-permute-start.11 = (bf16[768,256]{1,0:T(8,128)(2,1)S(1)}, bf16[768,256]{1,0:T(8,128)(2,1)}, u32[]{:S(2)}, u32[]{:S(2)}) collective-permute-start(bf16[768,256]{1,0:T(8,128)(2,1)S(1)} %constant_dynamic-update-slice_fusion.4.refs_6_), channel_id=1, source_target_pairs={{0,8},{8,16},{16,24},{24,0},{1,9},{9,17},{17,25},{25,1},{2,10},{10... | collective-permute-start | bytes 1179656 | tf_op jit(solution)/shard_map/ppermute | solution.py:24
  36.8 15.4 %collective-permute-start.23 = (bf16[768,256]{1,0:T(8,128)(2,1)S(1)}, bf16[768,256]{1,0:T(8,128)(2,1)}, u32[]{:S(2)}, u32[]{:S(2)}) collective-permute-start(bf16[768,256]{1,0:T(8,128)(2,1)S(1)} %constant_dynamic-update-slice_fusion.4.refs_6_), channel_id=1, source_target_pairs={{0,24},{8,0},{16,8},{24,16},{1,25},{9,1},{17,9},{25,17},{2,26},{10... | collective-permute-start | bytes 1179656 | tf_op jit(solution)/shard_map/ppermute | solution.py:24
  39.6 13.9 %collective-permute-start.20 = (bf16[768,256]{1,0:T(8,128)(2,1)S(1)}, bf16[768,256]{1,0:T(8,128)(2,1)}, u32[]{:S(2)}, u32[]{:S(2)}) collective-permute-start(bf16[768,256]{1,0:T(8,128)(2,1)S(1)} %constant_dynamic-update-slice_fusion.refs_5_), channel_id=1, source_target_pairs={{0,32},{32,64},{64,96},{96,0},{1,33},{33,65},{65,97},{97,1},{2,34}... | collective-permute-start | bytes 1179656 | tf_op jit(solution)/shard_map/ppermute | solution.py:24
  42.8 10.9 %collective-permute-start.6 = (bf16[768,256]{1,0:T(8,128)(2,1)S(1)}, bf16[768,256]{1,0:T(8,128)(2,1)}, u32[]{:S(2)}, u32[]{:S(2)}) collective-permute-start(bf16[768,256]{1,0:T(8,128)(2,1)S(1)} %constant_dynamic-update-slice_fusion.refs_5_), channel_id=1, source_target_pairs={{0,96},{32,0},{64,32},{96,64},{1,97},{33,1},{65,33},{97,65},{2,98}... | collective-permute-start | bytes 1179656 | tf_op jit(solution)/shard_map/ppermute | solution.py:24
  43.7 15.5 %collective-permute-start.2 = (bf16[768,256]{1,0:T(8,128)(2,1)S(1)}, bf16[768,256]{1,0:T(8,128)(2,1)}, u32[]{:S(2)}, u32[]{:S(2)}) collective-permute-start(bf16[768,256]{1,0:T(8,128)(2,1)S(1)} %pad_maximum_fusion.refs_4_), channel_id=1, source_target_pairs={{0,32},{32,64},{64,96},{96,0},{1,33},{33,65},{65,97},{97,1},{2,34}... | collective-permute-start | bytes 1179656 | tf_op jit(solution)/shard_map/ppermute | solution.py:24
  46.3 20.2 %collective-permute-start.21 = (bf16[768,256]{1,0:T(8,128)(2,1)S(1)}, bf16[768,256]{1,0:T(8,128)(2,1)S(1)}, u32[]{:S(2)}, u32[]{:S(2)}) collective-permute-start(bf16[768,256]{1,0:T(8,128)(2,1)S(1)} %pad_maximum_fusion.refs_4_), channel_id=1, source_target_pairs={{0,96},{32,0},{64,32},{96,64},{1,97},{33,1},{65,33},{97,65},{2,98}... | collective-permute-start | bytes 1179656 | tf_op jit(solution)/shard_map/ppermute | solution.py:24
  52.2 20.9 %collective-permute-start.16 = (bf16[768,256]{1,0:T(8,128)(2,1)S(1)}, bf16[768,256]{1,0:T(8,128)(2,1)S(1)}, u32[]{:S(2)}, u32[]{:S(2)}) collective-permute-start(bf16[768,256]{1,0:T(8,128)(2,1)S(1)} %collective-permute-done.15.refs_11_), channel_id=1, source_target_pairs={{0,24},{8,0},{16,8},{24,16},{1,25},{9,1},{17,9},{25,17},{2,26},{10... | collective-permute-start | bytes 1179656 | tf_op jit(solution)/shard_map/ppermute | solution.py:24
  53.4 19.7 %collective-permute-start.12 = (bf16[768,256]{1,0:T(8,128)(2,1)}, bf16[768,256]{1,0:T(8,128)(2,1)S(1)}, u32[]{:S(2)}, u32[]{:S(2)}) collective-permute-start(bf16[768,256]{1,0:T(8,128)(2,1)} %collective-permute-done.11.refs_8_), channel_id=1, source_target_pairs={{0,8},{8,16},{16,24},{24,0},{1,9},{9,17},{17,25},{25,1},{2,10},{10... | collective-permute-start | bytes 1179656 | tf_op jit(solution)/shard_map/ppermute | solution.py:24
  53.7 19.4 %collective-permute-start.7 = (bf16[768,256]{1,0:T(8,128)(2,1)}, bf16[768,256]{1,0:T(8,128)(2,1)S(1)}, u32[]{:S(2)}, u32[]{:S(2)}) collective-permute-start(bf16[768,256]{1,0:T(8,128)(2,1)} %collective-permute-done.6.refs_7_), channel_id=1, source_target_pairs={{0,96},{32,0},{64,32},{96,64},{1,97},{33,1},{65,33},{97,65},{2,98}... | collective-permute-start | bytes 1179656 | tf_op jit(solution)/shard_map/ppermute | solution.py:24
  59.2 13.9 %collective-permute-start.3 = (bf16[768,256]{1,0:T(8,128)(2,1)}, bf16[768,256]{1,0:T(8,128)(2,1)S(1)}, u32[]{:S(2)}, u32[]{:S(2)}) collective-permute-start(bf16[768,256]{1,0:T(8,128)(2,1)} %collective-permute-done.2.refs_4_), channel_id=1, source_target_pairs={{0,32},{32,64},{64,96},{96,0},{1,33},{33,65},{65,97},{97,1},{2,34}... | collective-permute-start | bytes 1179656 | tf_op jit(solution)/shard_map/ppermute | solution.py:24
  77.6 6.9 %collective-permute-start.27 = (bf16[96,512]{1,0:T(8,128)(2,1)S(1)}, bf16[96,512]{1,0:T(8,128)(2,1)S(1)}, u32[]{:S(2)}, u32[]{:S(2)}) collective-permute-start(bf16[96,512]{1,0:T(8,128)(2,1)S(1)} %get-tuple-element.30), channel_id=1, source_target_pairs={{0,6},{2,0},{4,2},{6,4},{1,7},{3,1},{5,3},{7,5},{8,14},{10,8},{12,... | collective-permute-start | bytes 294920 | tf_op jit(solution)/shard_map/ppermute | solution.py:24
  81.9 5.0 %collective-permute-start.28 = (bf16[96,512]{1,0:T(8,128)(2,1)S(1)}, bf16[96,512]{1,0:T(8,128)(2,1)S(1)}, u32[]{:S(2)}, u32[]{:S(2)}) collective-permute-start(bf16[96,512]{1,0:T(8,128)(2,1)S(1)} %get-tuple-element.31), channel_id=1, source_target_pairs={{0,4},{2,6},{4,0},{6,2},{1,5},{3,7},{5,1},{7,3},{8,12},{10,14},{12... | collective-permute-start | bytes 294920 | tf_op jit(solution)/shard_map/ppermute | solution.py:24
  82.8 5.1 %collective-permute-start.29 = (bf16[96,512]{1,0:T(8,128)(2,1)S(1)}, bf16[96,512]{1,0:T(8,128)(2,1)S(1)}, u32[]{:S(2)}, u32[]{:S(2)}) collective-permute-start(bf16[96,512]{1,0:T(8,128)(2,1)S(1)} %get-tuple-element.32), channel_id=1, source_target_pairs={{0,2},{2,4},{4,6},{6,0},{1,3},{3,5},{5,7},{7,1},{8,10},{10,12},{12... | collective-permute-start | bytes 294920 | tf_op jit(solution)/shard_map/ppermute | solution.py:24
  91.4 16.2 %collective-permute-start.30 = (bf16[96,4096]{1,0:T(8,128)(2,1)S(1)}, bf16[96,4096]{1,0:T(8,128)(2,1)S(1)}, u32[]{:S(2)}, u32[]{:S(2)}) collective-permute-start(bf16[96,4096]{1,0:T(8,128)(2,1)S(1)} %project.3), channel_id=1, source_target_pairs={{0,1},{1,0},{2,3},{3,2},{4,5},{5,4},{6,7},{7,6},{8,9},{9,8},{10,11... | collective-permute-start | bytes 2359304 | tf_op jit(solution)/shard_map/ppermute | solution.py:314
  95.6 4.3 %collective-permute-start.24 = (bf16[96,512]{1,0:T(8,128)(2,1)S(1)}, bf16[96,512]{1,0:T(8,128)(2,1)S(1)}, u32[]{:S(2)}, u32[]{:S(2)}) collective-permute-start(bf16[96,512]{1,0:T(8,128)(2,1)S(1)} %get-tuple-element.25), channel_id=1, source_target_pairs={{0,6},{2,0},{4,2},{6,4},{1,7},{3,1},{5,3},{7,5},{8,14},{10,8},{12,... | collective-permute-start | bytes 294920 | tf_op jit(solution)/shard_map/ppermute | solution.py:24
  95.9 5.5 %collective-permute-start.25 = (bf16[96,512]{1,0:T(8,128)(2,1)S(1)}, bf16[96,512]{1,0:T(8,128)(2,1)S(1)}, u32[]{:S(2)}, u32[]{:S(2)}) collective-permute-start(bf16[96,512]{1,0:T(8,128)(2,1)S(1)} %get-tuple-element.26), channel_id=1, source_target_pairs={{0,4},{2,6},{4,0},{6,2},{1,5},{3,7},{5,1},{7,3},{8,12},{10,14},{12... | collective-permute-start | bytes 294920 | tf_op jit(solution)/shard_map/ppermute | solution.py:24
  96.7 7.5 %collective-permute-start.26 = (bf16[96,512]{1,0:T(8,128)(2,1)S(1)}, bf16[96,512]{1,0:T(8,128)(2,1)S(1)}, u32[]{:S(2)}, u32[]{:S(2)}) collective-permute-start(bf16[96,512]{1,0:T(8,128)(2,1)S(1)} %get-tuple-element.27), channel_id=1, source_target_pairs={{0,2},{2,4},{4,6},{6,0},{1,3},{3,5},{5,7},{7,1},{8,10},{10,12},{12... | collective-permute-start | bytes 294920 | tf_op jit(solution)/shard_map/ppermute | solution.py:24

commit v4 on v3

--- a/solution.py
+++ b/solution.py
@@ -15,6 +15,7 @@
 LOG2E = 1.4426950408889634
 FACTOR = HEAD ** -0.5 * LOG2E
 MAX_TASKS = 160
+TILE = 16
 
 PHASES = (((0, 0), (0, 1)), ((1, 0), (1, 1), (3, 0), (3, 1)), ((2, 0), (2, 1)))
 CHUNKS = (256, 512, 256)
@@ -47,7 +48,7 @@
         (q_all,) = take(1)
     best_all, acc_all = take(2)
     if last_phase:
-        outs = take(8)
+        outs = take(7)
     if first_phase:
         (weight_held,) = take(1)
         weight_copy = pltpu.make_async_copy(weight, weight_held, refs.pop())
@@ -73,9 +74,12 @@
         for s, ref in enumerate(q_parts):
             for half in range(2):
                 for h in range(GROUP):
-                    q_all[2 * s + half, h * SPAN : (h + 1) * SPAN, :] = ref[
-                        half * SPAN : (half + 1) * SPAN, h * HEAD : (h + 1) * HEAD
-                    ]
+                    scaled = ref[half * SPAN : (half + 1) * SPAN, h * HEAD : (h + 1) * HEAD]
+                    scaled = scaled.astype(jnp.float32) * FACTOR
+                    main = scaled.astype(jnp.bfloat16)
+                    rest = (scaled - main.astype(jnp.float32)).astype(jnp.bfloat16)
+                    q_all[2 * s + half, h * SPAN : (h + 1) * SPAN, :HEAD] = main
+                    q_all[2 * s + half, h * SPAN : (h + 1) * SPAN, HEAD:] = rest
         best_all[...] = jnp.full(best_all.shape, LOW, jnp.float32)
         acc_all[...] = jnp.zeros(acc_all.shape, jnp.float32)
 
@@ -120,29 +124,31 @@
     def score(t, out):
         k = kv[pl.ds(pl.multiple_of(task_first[t], 32), chunk), :HEAD]
         out[...] = lax.dot_general(
-            q_all[task_span[t]], k, (((1,), (1,)), ((), ())), preferred_element_type=jnp.float32
+            q_all[task_span[t]], jnp.concatenate([k, k], axis=1), (((1,), (1,)), ((), ())), preferred_element_type=jnp.float32
         )
 
     def weigh(t, s_ref, p_ref, f_ref):
         i, k0 = task_span[t], task_first[t]
-        low = low_all[i] - k0
-        high = jnp.minimum(high_all[i], task_upper[t] - 1) - k0
-        lane = lax.broadcasted_iota(jnp.int32, (SPAN, HEAD), 1)
-        seen = [(lane >= low - g * HEAD) & (lane <= high - g * HEAD) for g in range(lanes)]
-        for h in range(GROUP):
-            at = slice(h * SPAN, (h + 1) * SPAN)
-            s = [
-                jnp.where(seen[g], s_ref[at, g * HEAD : (g + 1) * HEAD], 2 * LOW) for g in range(lanes)
-            ]
-            top = s[0]
-            for g in range(1, lanes):
-                top = jnp.maximum(top, s[g])
-            best = best_all[i, at, :]
-            new_best = jnp.maximum(best, jnp.max(top, axis=1, keepdims=True))
-            best_all[i, at, :] = new_best
-            f_ref[at, :] = jnp.exp2((best - new_best) * FACTOR)
-            for g in range(lanes):
-                p_ref[at, g * HEAD : (g + 1) * HEAD] = jnp.exp2((s[g] - new_best) * FACTOR).astype(
+        last = task_upper[t] - 1
+        lane = lax.broadcasted_iota(jnp.int32, (TILE, HEAD), 1)
+        for r in range(0, SPAN, TILE):
+            low = low_all[i, r : r + TILE, :] - k0
+            high = jnp.minimum(high_all[i, r : r + TILE, :], last) - k0
+            seen = [(lane + g * HEAD >= low) & (lane + g * HEAD <= high) for g in range(lanes)]
+            for h in range(GROUP):
+                at = slice(h * SPAN + r, h * SPAN + r + TILE)
+                s = [
+                    jnp.where(seen[g], s_ref[at, g * HEAD : (g + 1) * HEAD], 2 * LOW)
+                    for g in range(lanes)
+                ]
+                top = s[0]
+                for g in range(1, lanes):
+                    top = jnp.maximum(top, s[g])
+                best = best_all[i, at, :]
+                new_best = jnp.maximum(best, jnp.max(top, axis=1, keepdims=True))
+                best_all[i, at, :] = new_best
+                f_ref[at, :] = jnp.exp2(best - new_best)
+                p_ref[at, :] = jnp.concatenate([jnp.exp2(x - new_best) for x in s], axis=1).astype(
                     jnp.bfloat16
                 )
 
@@ -178,9 +184,11 @@
             half = 1 - core if turn == 0 else core
             for s in range(RING):
                 i = 2 * s + half
+                out = outs[6] if s == 2 else outs[3 * turn + min(s, 2)]
+                first = turn * SPAN if s == 2 else 0
                 for h in range(GROUP):
                     at = slice(h * SPAN, (h + 1) * SPAN)
-                    outs[4 * turn + s][:, h * HEAD : (h + 1) * HEAD] = (
+                    out[first : first + SPAN, h * HEAD : (h + 1) * HEAD] = (
                         acc_all[i, at, :HEAD] / acc_all[i, at, HEAD:]
                     ).astype(jnp.bfloat16)
 
@@ -194,14 +202,15 @@
     far = [] if weight is None else [weight]
     held = [(w.shape, w.dtype) for w in far]
     if phase == 0:
-        outs = [((8, ROWS, HEAD), jnp.bfloat16)] + state + held
+        outs = [((8, ROWS, 2 * HEAD), jnp.bfloat16)] + state + held
         aliases = {}
     else:
         outs = state + held
         first = 4 + len(pieces) + 1
         aliases = {first: 0, first + 1: 1}
     if phase == 2:
-        outs = outs + [((SPAN, GROUP * HEAD), jnp.bfloat16)] * 8
+        part = ((SPAN, GROUP * HEAD), jnp.bfloat16)
+        outs = outs + [part] * 6 + [((2 * SPAN, GROUP * HEAD), jnp.bfloat16)]
     scratch = [
         pltpu.VMEM((keys, 2 * HEAD), jnp.bfloat16),
         pltpu.VMEM((8, SPAN, HEAD), jnp.int32),
@@ -233,7 +242,7 @@
     )(*scalars, *pieces, *others, *far)
 
 
-def project_kernel(coords, o0, o1, o2, o3, w, out):
+def project_kernel(turn, coords, o0, o1, o2, o3, w, out):
     y = coords[2]
     block = 512
     for n in range(w.shape[1] // block):
@@ -241,17 +250,18 @@
         acc = None
         for s, ref in enumerate((o0, o1, o2, o3)):
             row = pl.multiple_of(((y + s) % RING) * 512, 512)
-            part = jnp.dot(ref[...], w[pl.ds(row, 512), cols], preferred_element_type=jnp.float32)
+            rows = ref[turn * SPAN : (turn + 1) * SPAN, :] if s == 2 else ref[...]
+            part = jnp.dot(rows, w[pl.ds(row, 512), cols], preferred_element_type=jnp.float32)
             acc = part if acc is None else acc + part
         out[:, cols] = acc.astype(out.dtype)
 
 
-def project(coords, o_parts, weight, dtype):
+def project(turn, coords, o_parts, weight, dtype):
     smem = pl.BlockSpec(memory_space=pltpu.SMEM)
     vmem = pl.BlockSpec(memory_space=pltpu.VMEM)
     width = weight.shape[1]
     return pl.pallas_call(
-        project_kernel,
+        lambda *refs: project_kernel(turn, *refs),
         out_shape=jax.ShapeDtypeStruct((SPAN, width), dtype),
         in_specs=[smem] + [vmem] * 5,
         out_specs=vmem,
@@ -308,11 +318,13 @@
     o_part = run_phase(2, scalars + [ranks[2]], pieces[2], [q_all, best, acc])[2:]
 
     def returned(part):
-        return [part[0]] + [shift(part[s], "y", -s) for s in range(1, RING)]
-
-    theirs, ours = returned(o_part[:4]), returned(o_part[4:])
-    sent = lax.ppermute(project(coords, theirs, weight, jnp.bfloat16), "hd", [(0, 1), (1, 0)])
-    kept = project(coords, ours, weight, jnp.float32)
+        return [part[0], shift(part[1], "y", -1), both, shift(part[2], "y", 1)]
+
+    both = shift(o_part[6], "y", -2)
+    theirs, ours = returned(o_part[:3]), returned(o_part[3:6])
+    sent = project(0, coords, theirs, weight, jnp.bfloat16)
+    sent = lax.ppermute(sent, "hd", [(0, 1), (1, 0)])
+    kept = project(1, coords, ours, weight, jnp.float32)
     return (kept + sent.astype(jnp.float32)).astype(jnp.bfloat16)
 
 

time: 110 us -> 107 us (0.973)
  waiting for transfers between devices: 28 us -> 25.9 us
    ppermute x30 -> x29, waiting for transfers between devices: 28 us -> 25.9 us  [shift(): lax.ppermute(value, axis, [(i, (i + by) % RING) for i in range(RING)])]
    ppermute x30 -> x29, starting transfers between devices: 46.5 us -> 46.9 us  [shift(): lax.ppermute(value, axis, [(i, (i + by) % RING) for i in range(RING)])]
  transfers between devices with their start and end apart: 31 -> 30, of which waited for: 12 -> 10; matrix products, arithmetic and copies ran while one was open for 2% -> 2% of each run, Pallas kernels for 15% -> 15%
where the time goes in v4:
time: 107 us; the launch traced here: 106 us
  starting transfers between devices  50.2 us (47%)
  waiting for transfers between devices  25.9 us (24%)
  Pallas kernels  24.1 us (23%)
  local copies, waits for them, and re-layouts  2.91 us (3%)
  other arithmetic  2.44 us (2%)
    ppermute x29, starting transfers between devices, shift(): lax.ppermute(value, axis, [(i, (i + by) % RING) for i in range(RING)])  46.9 us
    ppermute x29, waiting for transfers between devices, shift(): lax.ppermute(value, axis, [(i, (i + by) % RING) for i in range(RING)])  25.9 us
    pallas_call x3, Pallas kernels, run_phase(): pl.pallas_call(lambda *refs: phase_kernel(phase, *refs), out_shape=[jax.S...  17.4 us
    pallas_call x2, Pallas kernels, project(): pl.pallas_call(lambda *refs: project_kernel(turn, *refs), out_shape=jax.S...  6.75 us
    ppermute x1, starting transfers between devices, layer(): sent = lax.ppermute(sent, 'hd', [(0, 1), (1, 0)])  3.31 us
  transfers between devices with their start and end apart: 30, of which 10 were waited for; matrix products, arithmetic and copies ran while one was open for 2% of the time, Pallas kernels for 15%

profile of v4, /device:TPU:1, one launch (start us, length us, event | category | flops | bytes accessed | tf_op | source)
XLA Modules:
  0.0 105.8 jit_solution(6773104234250068696)
XLA Ops:
  0.0 0.9 copy-done
  1.0 1.0 bitcast_dynamic-update-slice_fusion
  2.0 3.8 %collective-permute-start.8 = (bf16[192,256]{1,0:T(8,128)(2,1)S(1)}, bf16[192,256]{1,0:T(8,128)(2,1)S(1)}, u32[]{:S(2)}, u32[]{:S(2)}) collective-permute-start(bf16[192,256]{1,0:T(8,128)(2,1)S(1)} %get-tuple-element.41), channel_id=1, source_target_pairs={{0,4},{2,6},{4,0},{6,2},{1,5},{3,7},{5,1},{7,3},{8,12},{10,14},{12... | collective-permute-start | bytes 294920 | tf_op jit(solution)/shard_map/ppermute | solution.py:25
  5.8 0.8 collective-permute-start.9
  6.6 0.7 collective-permute-start
  7.3 0.8 constant_dynamic-slice_fusion
  8.1 0.4 collective-permute-start.17
  8.5 1.7 %collective-permute-done.9 = bf16[192,256]{1,0:T(8,128)(2,1)S(1)} collective-permute-done((bf16[192,256]{1,0:T(8,128)(2,1)S(1)}, bf16[192,256]{1,0:T(8,128)(2,1)S(1)}, u32[]{:S(2)}, u32[]{:S(2)}) %collective-permute-start.9) | collective-permute-done | bytes 98336 | tf_op jit(solution)/shard_map/ppermute | solution.py:25
  10.3 2.8 %collective-permute-start.13 = (bf16[384,256]{1,0:T(8,128)(2,1)S(1)}, bf16[384,256]{1,0:T(8,128)(2,1)S(1)}, u32[]{:S(2)}, u32[]{:S(2)}) collective-permute-start(bf16[384,256]{1,0:T(8,128)(2,1)S(1)} %get-tuple-element.44), channel_id=1, source_target_pairs={{0,64},{32,96},{64,0},{96,32},{1,65},{33,97},{65,1},{97,33},{2,66}... | collective-permute-start | bytes 589832 | tf_op jit(solution)/shard_map/ppermute | solution.py:25
  13.2 0.9 collective-permute-start.14
  14.1 0.6 collective-permute-start.10
  14.7 3.7 %collective-permute-start.4 = (bf16[384,256]{1,0:T(8,128)(2,1)S(1)}, bf16[384,256]{1,0:T(8,128)(2,1)S(1)}, u32[]{:S(2)}, u32[]{:S(2)}) collective-permute-start(bf16[384,256]{1,0:T(8,128)(2,1)S(1)} %pad_maximum_fusion.1), channel_id=1, source_target_pairs={{0,16},{8,24},{16,0},{24,8},{1,17},{9,25},{17,1},{25,9},{2,18},{10... | collective-permute-start | bytes 589832 | tf_op jit(solution)/shard_map/ppermute | solution.py:25
  18.4 0.7 collective-permute-start.1
  19.2 2.0 %collective-permute-done.14 = bf16[384,256]{1,0:T(8,128)(2,1)S(1)} collective-permute-done((bf16[384,256]{1,0:T(8,128)(2,1)S(1)}, bf16[384,256]{1,0:T(8,128)(2,1)S(1)}, u32[]{:S(2)}, u32[]{:S(2)}) %collective-permute-start.14) | collective-permute-done | bytes 196640 | tf_op jit(solution)/shard_map/ppermute | solution.py:25
  21.2 3.8 %collective-permute-start.15 = (bf16[768,256]{1,0:T(8,128)(2,1)S(1)}, bf16[768,256]{1,0:T(8,128)(2,1)S(1)}, u32[]{:S(2)}, u32[]{:S(2)}) collective-permute-start(bf16[768,256]{1,0:T(8,128)(2,1)S(1)} %constant_dynamic-update-slice_fusion.7.refs_7_), channel_id=1, source_target_pairs={{0,24},{8,0},{16,8},{24,16},{1,25},{9,1},{17,9},{25,17},{2,26},{10... | collective-permute-start | bytes 1179656 | tf_op jit(solution)/shard_map/ppermute | solution.py:25
  25.0 1.5 %collective-permute-done.1 = bf16[384,256]{1,0:T(8,128)(2,1)S(1)} collective-permute-done((bf16[384,256]{1,0:T(8,128)(2,1)S(1)}, bf16[384,256]{1,0:T(8,128)(2,1)S(1)}, u32[]{:S(2)}, u32[]{:S(2)}) %collective-permute-start.1) | collective-permute-done | bytes 196640 | tf_op jit(solution)/shard_map/ppermute | solution.py:25
  26.5 2.7 %collective-permute-start.5 = (bf16[384,256]{1,0:T(8,128)(2,1)S(1)}, bf16[384,256]{1,0:T(8,128)(2,1)S(1)}, u32[]{:S(2)}, u32[]{:S(2)}) collective-permute-start(bf16[384,256]{1,0:T(8,128)(2,1)S(1)} %pad_maximum_fusion.1), channel_id=1, source_target_pairs={{0,24},{8,0},{16,8},{24,16},{1,25},{9,1},{17,9},{25,17},{2,26},{10... | collective-permute-start | bytes 589832 | tf_op jit(solution)/shard_map/ppermute | solution.py:25
  29.3 1.8 %collective-permute-start.18 = (bf16[192,512]{1,0:T(8,128)(2,1)S(1)}, bf16[192,512]{1,0:T(8,128)(2,1)S(1)}, u32[]{:S(2)}, u32[]{:S(2)}) collective-permute-start(bf16[192,512]{1,0:T(8,128)(2,1)S(1)} %copy-done.3), channel_id=1, source_target_pairs={{0,4},{2,6},{4,0},{6,2},{1,5},{3,7},{5,1},{7,3},{8,12},{10,14},{12... | collective-permute-start | bytes 589832 | tf_op jit(solution)/shard_map/ppermute | solution.py:25
  31.2 2.2 %collective-permute-start.19 = (bf16[192,512]{1,0:T(8,128)(2,1)S(1)}, bf16[192,512]{1,0:T(8,128)(2,1)S(1)}, u32[]{:S(2)}, u32[]{:S(2)}) collective-permute-start(bf16[192,512]{1,0:T(8,128)(2,1)S(1)} %get-tuple-element.36), channel_id=1, source_target_pairs={{0,6},{2,0},{4,2},{6,4},{1,7},{3,1},{5,3},{7,5},{8,14},{10,8},{12,... | collective-permute-start | bytes 589832 | tf_op jit(solution)/shard_map/ppermute | solution.py:25
  33.4 3.4 %collective-permute-done.5 = bf16[384,256]{1,0:T(8,128)(2,1)S(1)} collective-permute-done((bf16[384,256]{1,0:T(8,128)(2,1)S(1)}, bf16[384,256]{1,0:T(8,128)(2,1)S(1)}, u32[]{:S(2)}, u32[]{:S(2)}) %collective-permute-start.5) | collective-permute-done | bytes 196640 | tf_op jit(solution)/shard_map/ppermute | solution.py:25
  36.8 2.7 %collective-permute-start.23 = (bf16[768,256]{1,0:T(8,128)(2,1)S(1)}, bf16[768,256]{1,0:T(8,128)(2,1)}, u32[]{:S(2)}, u32[]{:S(2)}) collective-permute-start(bf16[768,256]{1,0:T(8,128)(2,1)S(1)} %constant_dynamic-update-slice_fusion.4.refs_6_), channel_id=1, source_target_pairs={{0,24},{8,0},{16,8},{24,16},{1,25},{9,1},{17,9},{25,17},{2,26},{10... | collective-permute-start | bytes 1179656 | tf_op jit(solution)/shard_map/ppermute | solution.py:25
  39.6 3.3 %collective-permute-start.20 = (bf16[768,256]{1,0:T(8,128)(2,1)S(1)}, bf16[768,256]{1,0:T(8,128)(2,1)}, u32[]{:S(2)}, u32[]{:S(2)}) collective-permute-start(bf16[768,256]{1,0:T(8,128)(2,1)S(1)} %constant_dynamic-update-slice_fusion.refs_5_), channel_id=1, source_target_pairs={{0,32},{32,64},{64,96},{96,0},{1,33},{33,65},{65,97},{97,1},{2,34}... | collective-permute-start | bytes 1179656 | tf_op jit(solution)/shard_map/ppermute | solution.py:25
  42.8 0.8 collective-permute-start.6
  43.7 0.6 collective-permute-start.2
  44.3 0.2 convert_reduce_fusion.1
  44.5 1.8 %collective-permute-done.11.refs_8_ = bf16[768,256]{1,0:T(8,128)(2,1)} collective-permute-done((bf16[768,256]{1,0:T(8,128)(2,1)S(1)}, bf16[768,256]{1,0:T(8,128)(2,1)}, u32[]{:S(2)}, u32[]{:S(2)}) %collective-permute-start.11) | collective-permute-done | bytes 393248 | tf_op jit(solution)/shard_map/ppermute | solution.py:25
  46.3 4.8 %collective-permute-start.21 = (bf16[768,256]{1,0:T(8,128)(2,1)S(1)}, bf16[768,256]{1,0:T(8,128)(2,1)S(1)}, u32[]{:S(2)}, u32[]{:S(2)}) collective-permute-start(bf16[768,256]{1,0:T(8,128)(2,1)S(1)} %pad_maximum_fusion.refs_4_), channel_id=1, source_target_pairs={{0,96},{32,0},{64,32},{96,64},{1,97},{33,1},{65,33},{97,65},{2,98}... | collective-permute-start | bytes 1179656 | tf_op jit(solution)/shard_map/ppermute | solution.py:25
  51.1 0.1 pad_add_fusion.refs_0_
  51.2 1.0 convert_reduce_fusion.refs_2_
  52.2 1.3 %collective-permute-start.16 = (bf16[768,256]{1,0:T(8,128)(2,1)S(1)}, bf16[768,256]{1,0:T(8,128)(2,1)S(1)}, u32[]{:S(2)}, u32[]{:S(2)}) collective-permute-start(bf16[768,256]{1,0:T(8,128)(2,1)S(1)} %collective-permute-done.15.refs_11_), channel_id=1, source_target_pairs={{0,24},{8,0},{16,8},{24,16},{1,25},{9,1},{17,9},{25,17},{2,26},{10... | collective-permute-start | bytes 1179656 | tf_op jit(solution)/shard_map/ppermute | solution.py:25
  53.4 0.3 collective-permute-start.12
  53.7 5.5 %collective-permute-done.2.refs_4_ = bf16[768,256]{1,0:T(8,128)(2,1)} collective-permute-done((bf16[768,256]{1,0:T(8,128)(2,1)S(1)}, bf16[768,256]{1,0:T(8,128)(2,1)}, u32[]{:S(2)}, u32[]{:S(2)}) %collective-permute-start.2) | collective-permute-done | bytes 393248 | tf_op jit(solution)/shard_map/ppermute | solution.py:25
  59.2 0.8 collective-permute-start.3
  60.0 6.5 %shard_map.64 = (bf16[8,384,256]{2,1,0:T(8,128)(2,1)S(1)}, f32[8,384,128]{2,1,0:T(8,128)S(1)}, f32[8,384,256]{2,1,0:T(8,128)S(1)}, bf16[2048,4096]{1,0:T(8,128)(2,1)S(1)}) custom-call(s32[4]{0:T(128)S(1)} %pad_add_fusion.refs_0_, s32[128]{0:T(128)S(1)} %copy-done.1, s32[8]{0:T(128)S(1)} %convert_reduce_fusion.refs_2_, s32[136]{0:T(256)S(1)} %get-tuple-element.32.refs_3_, ...), custom_call_target="tpu_custom_call" | custom-call | flops 2000000000 | bytes 2500000 | tf_op jit(solution)/shard_map/pallas_call | solution.py:229
  66.5 6.5 %shard_map.65 = (f32[8,384,128]{2,1,0:T(8,128)S(1)}, f32[8,384,256]{2,1,0:T(8,128)S(1)}) custom-call(s32[4]{0:T(128)S(1)} %pad_add_fusion.refs_0_, s32[128]{0:T(128)S(1)} %copy-done.1, s32[8]{0:T(128)S(1)} %convert_reduce_fusion.refs_2_, s32[136]{0:T(256)S(1)} %get-tuple-element.31.refs_3_, ...), custom_call_target="tpu_custom_call", output_to_operand_aliasing={{0}: (13, {}), {1}: (14, {})} | custom-call | flops 4000000000 | bytes 5000000 | tf_op jit(solution)/shard_map/pallas_call | solution.py:229
  73.0 4.4 %shard_map.66 = (f32[8,384,128]{2,1,0:T(8,128)S(1)}, f32[8,384,256]{2,1,0:T(8,128)S(1)}, bf16[96,512]{1,0:T(8,128)(2,1)S(1)}, bf16[96,512]{1,0:T(8,128)(2,1)S(1)...) custom-call(s32[4]{0:T(128)S(1)} %pad_add_fusion.refs_0_, ...), custom_call_target="tpu_custom_call", output_to_operand_aliasing={{0}: (9, {}), {1}: (10, {})} | custom-call | flops 2000000000 | bytes 2500000 | tf_op jit(solution)/shard_map/pallas_call | solution.py:229
  77.4 2.3 %collective-permute-start.25 = (bf16[192,512]{1,0:T(8,128)(2,1)S(1)}, bf16[192,512]{1,0:T(8,128)(2,1)S(1)}, u32[]{:S(2)}, u32[]{:S(2)}) collective-permute-start(bf16[192,512]{1,0:T(8,128)(2,1)S(1)} %get-tuple-element.25), channel_id=1, source_target_pairs={{0,4},{2,6},{4,0},{6,2},{1,5},{3,7},{5,1},{7,3},{8,12},{10,14},{12... | collective-permute-start | bytes 589832 | tf_op jit(solution)/shard_map/ppermute | solution.py:25
  79.7 3.4 %collective-permute-start.27 = (bf16[96,512]{1,0:T(8,128)(2,1)S(1)}, bf16[96,512]{1,0:T(8,128)(2,1)S(1)}, u32[]{:S(2)}, u32[]{:S(2)}) collective-permute-start(bf16[96,512]{1,0:T(8,128)(2,1)S(1)} %get-tuple-element.29), channel_id=1, source_target_pairs={{0,6},{2,0},{4,2},{6,4},{1,7},{3,1},{5,3},{7,5},{8,14},{10,8},{12,... | collective-permute-start | bytes 294920 | tf_op jit(solution)/shard_map/ppermute | solution.py:25
  83.2 3.6 %collective-permute-done.27.refs_2_ = bf16[96,512]{1,0:T(8,128)(2,1)S(1)} collective-permute-done((bf16[96,512]{1,0:T(8,128)(2,1)S(1)}, bf16[96,512]{1,0:T(8,128)(2,1)S(1)}, u32[]{:S(2)}, u32[]{:S(2)}) %collective-permute-start.27) | collective-permute-done | bytes 98336 | tf_op jit(solution)/shard_map/ppermute | solution.py:25
  86.7 2.3 %collective-permute-done.28.refs_4_ = bf16[96,512]{1,0:T(8,128)(2,1)S(1)} collective-permute-done((bf16[96,512]{1,0:T(8,128)(2,1)S(1)}, bf16[96,512]{1,0:T(8,128)(2,1)S(1)}, u32[]{:S(2)}, u32[]{:S(2)}) %collective-permute-start.28) | collective-permute-done | bytes 98336 | tf_op jit(solution)/shard_map/ppermute | solution.py:25
  89.0 3.4 %project.3 = bf16[96,4096]{1,0:T(8,128)(2,1)S(1)} custom-call(s32[4]{0:T(128)S(1)} %pad_add_fusion.refs_0_, bf16[96,512]{1,0:T(8,128)(2,1)S(1)} %get-tuple-element.28.refs_1_, bf16[96,512]{1,0:T(8,128)(2,1)S(1)} %collective-permute-done.27.refs_2_, bf16[192,512]{1,0:T(8,128)(2,1)S(1)} %collective-permute-done.25.refs_3_, ...), custom_call_target="tpu_custom_call" | custom-call | flops 1610612736 | bytes 16777216 | tf_op jit(solution)/shard_map/project/pallas_call | solution.py:263
  92.4 3.3 %collective-permute-start.29 = (bf16[96,4096]{1,0:T(8,128)(2,1)S(1)}, bf16[96,4096]{1,0:T(8,128)(2,1)S(1)}, u32[]{:S(2)}, u32[]{:S(2)}) collective-permute-start(bf16[96,4096]{1,0:T(8,128)(2,1)S(1)} %project.3), channel_id=1, source_target_pairs={{0,1},{1,0},{2,3},{3,2},{4,5},{5,4},{6,7},{7,6},{8,9},{9,8},{10,11... | collective-permute-start | bytes 2359304 | tf_op jit(solution)/shard_map/ppermute | solution.py:326
  95.7 0.4 collective-permute-start.24
  96.1 1.0 collective-permute-start.26
  97.2 2.8 %collective-permute-done.24.refs_2_ = bf16[96,512]{1,0:T(8,128)(2,1)S(1)} collective-permute-done((bf16[96,512]{1,0:T(8,128)(2,1)S(1)}, bf16[96,512]{1,0:T(8,128)(2,1)S(1)}, u32[]{:S(2)}, u32[]{:S(2)}) %collective-permute-start.24) | collective-permute-done | bytes 98336 | tf_op jit(solution)/shard_map/ppermute | solution.py:25
  100.0 1.4 %collective-permute-done.26.refs_4_ = bf16[96,512]{1,0:T(8,128)(2,1)S(1)} collective-permute-done((bf16[96,512]{1,0:T(8,128)(2,1)S(1)}, bf16[96,512]{1,0:T(8,128)(2,1)S(1)}, u32[]{:S(2)}, u32[]{:S(2)}) %collective-permute-start.26) | collective-permute-done | bytes 98336 | tf_op jit(solution)/shard_map/ppermute | solution.py:25
  101.3 3.4 %project.2 = f32[96,4096]{1,0:T(8,128)S(1)} custom-call(s32[4]{0:T(128)S(1)} %pad_add_fusion.refs_0_, bf16[96,512]{1,0:T(8,128)(2,1)S(1)} %get-tuple-element.23.refs_1_, bf16[96,512]{1,0:T(8,128)(2,1)S(1)} %collective-permute-done.24.refs_2_, bf16[192,512]{1,0:T(8,128)(2,1)S(1)} %collective-permute-done.25.refs_3_, ...), custom_call_target="tpu_custom_call" | custom-call | flops 1610612736 | bytes 16777216 | tf_op jit(solution)/shard_map/project/pallas_call | solution.py:263
  104.7 1.1 %add_convert_fusion = bf16[96,4096]{1,0:T(8,128)(2,1)} fusion(f32[96,4096]{1,0:T(8,128)S(1)} %project.2, bf16[96,4096]{1,0:T(8,128)(2,1)S(1)} %collective-permute-done.29), kind=kLoop, calls=%fused_computation | loop fusion | flops 1179648 | bytes 3145728 | tf_op jit(solution)/shard_map/convert_element_type | solution.py:328
  (44 shorter events, 0.3 us)
Async XLA Ops:
  0.0 0.9 copy-start
  0.0 7.3 %copy-start.2 = (bf16[192,2048]{1,0:T(8,128)(2,1)S(1)}, bf16[192,2048]{1,0:T(8,128)(2,1)}, u32[]{:S(2)}) copy-start(bf16[192,2048]{1,0:T(8,128)(2,1)} %param.6) | copy-start | bytes 2359300
  2.0 6.5 %collective-permute-start.8 = (bf16[192,256]{1,0:T(8,128)(2,1)S(1)}, bf16[192,256]{1,0:T(8,128)(2,1)S(1)}, u32[]{:S(2)}, u32[]{:S(2)}) collective-permute-start(bf16[192,256]{1,0:T(8,128)(2,1)S(1)} %get-tuple-element.41), channel_id=1, source_target_pairs={{0,4},{2,6},{4,0},{6,2},{1,5},{3,7},{5,1},{7,3},{8,12},{10,14},{12... | collective-permute-start | bytes 294920 | tf_op jit(solution)/shard_map/ppermute | solution.py:25
  5.8 4.4 %collective-permute-start.9 = (bf16[192,256]{1,0:T(8,128)(2,1)S(1)}, bf16[192,256]{1,0:T(8,128)(2,1)S(1)}, u32[]{:S(2)}, u32[]{:S(2)}) collective-permute-start(bf16[192,256]{1,0:T(8,128)(2,1)S(1)} %get-tuple-element.40), channel_id=1, source_target_pairs={{0,6},{2,0},{4,2},{6,4},{1,7},{3,1},{5,3},{7,5},{8,14},{10,8},{12,... | collective-permute-start | bytes 294920 | tf_op jit(solution)/shard_map/ppermute | solution.py:25
  6.6 8.1 %collective-permute-start = (bf16[192,256]{1,0:T(8,128)(2,1)S(1)}, bf16[192,256]{1,0:T(8,128)(2,1)S(1)}, u32[]{:S(2)}, u32[]{:S(2)}) collective-permute-start(bf16[192,256]{1,0:T(8,128)(2,1)S(1)} %get-tuple-element.42), channel_id=1, source_target_pairs={{0,2},{2,4},{4,6},{6,0},{1,3},{3,5},{5,7},{7,1},{8,10},{10,12},{12... | collective-permute-start | bytes 294920 | tf_op jit(solution)/shard_map/ppermute | solution.py:25
  8.1 21.2 %collective-permute-start.17 = (bf16[192,512]{1,0:T(8,128)(2,1)}, bf16[192,512]{1,0:T(8,128)(2,1)S(1)}, u32[]{:S(2)}, u32[]{:S(2)}) collective-permute-start(bf16[192,512]{1,0:T(8,128)(2,1)} %get-tuple-element.37), channel_id=1, source_target_pairs={{0,2},{2,4},{4,6},{6,0},{1,3},{3,5},{5,7},{7,1},{8,10},{10,12},{12... | collective-permute-start | bytes 589832 | tf_op jit(solution)/shard_map/ppermute | solution.py:25
  8.5 20.8 %copy-start.3 = (bf16[192,512]{1,0:T(8,128)(2,1)S(1)}, bf16[192,512]{1,0:T(8,128)(2,1)}, u32[]{:S(2)}) copy-start(bf16[192,512]{1,0:T(8,128)(2,1)} %get-tuple-element.39) | copy-start | bytes 589828
  10.3 8.1 %collective-permute-start.13 = (bf16[384,256]{1,0:T(8,128)(2,1)S(1)}, bf16[384,256]{1,0:T(8,128)(2,1)S(1)}, u32[]{:S(2)}, u32[]{:S(2)}) collective-permute-start(bf16[384,256]{1,0:T(8,128)(2,1)S(1)} %get-tuple-element.44), channel_id=1, source_target_pairs={{0,64},{32,96},{64,0},{96,32},{1,65},{33,97},{65,1},{97,33},{2,66}... | collective-permute-start | bytes 589832 | tf_op jit(solution)/shard_map/ppermute | solution.py:25
  13.2 8.0 %collective-permute-start.14 = (bf16[384,256]{1,0:T(8,128)(2,1)S(1)}, bf16[384,256]{1,0:T(8,128)(2,1)S(1)}, u32[]{:S(2)}, u32[]{:S(2)}) collective-permute-start(bf16[384,256]{1,0:T(8,128)(2,1)S(1)} %get-tuple-element.44), channel_id=1, source_target_pairs={{0,96},{32,0},{64,32},{96,64},{1,97},{33,1},{65,33},{97,65},{2,98}... | collective-permute-start | bytes 589832 | tf_op jit(solution)/shard_map/ppermute | solution.py:25
  14.1 17.1 %collective-permute-start.10 = (bf16[384,256]{1,0:T(8,128)(2,1)S(1)}, bf16[384,256]{1,0:T(8,128)(2,1)S(1)}, u32[]{:S(2)}, u32[]{:S(2)}) collective-permute-start(bf16[384,256]{1,0:T(8,128)(2,1)S(1)} %get-tuple-element.44), channel_id=1, source_target_pairs={{0,32},{32,64},{64,96},{96,0},{1,33},{33,65},{65,97},{97,1},{2,34}... | collective-permute-start | bytes 589832 | tf_op jit(solution)/shard_map/ppermute | solution.py:25
  14.7 29.6 %copy-start.1 = (s32[128]{0:T(128)S(1)}, s32[128]{0:T(128)}, u32[]{:S(2)}) copy-start(s32[128]{0:T(128)} %refs_1_.5) | copy-start | bytes 1540
  14.7 11.8 %collective-permute-start.4 = (bf16[384,256]{1,0:T(8,128)(2,1)S(1)}, bf16[384,256]{1,0:T(8,128)(2,1)S(1)}, u32[]{:S(2)}, u32[]{:S(2)}) collective-permute-start(bf16[384,256]{1,0:T(8,128)(2,1)S(1)} %pad_maximum_fusion.1), channel_id=1, source_target_pairs={{0,16},{8,24},{16,0},{24,8},{1,17},{9,25},{17,1},{25,9},{2,18},{10... | collective-permute-start | bytes 589832 | tf_op jit(solution)/shard_map/ppermute | solution.py:25
  18.4 8.1 %collective-permute-start.1 = (bf16[384,256]{1,0:T(8,128)(2,1)S(1)}, bf16[384,256]{1,0:T(8,128)(2,1)S(1)}, u32[]{:S(2)}, u32[]{:S(2)}) collective-permute-start(bf16[384,256]{1,0:T(8,128)(2,1)S(1)} %pad_maximum_fusion.1), channel_id=1, source_target_pairs={{0,8},{8,16},{16,24},{24,0},{1,9},{9,17},{17,25},{25,1},{2,10},{10... | collective-permute-start | bytes 589832 | tf_op jit(solution)/shard_map/ppermute | solution.py:25
  21.2 21.6 %collective-permute-start.15 = (bf16[768,256]{1,0:T(8,128)(2,1)S(1)}, bf16[768,256]{1,0:T(8,128)(2,1)S(1)}, u32[]{:S(2)}, u32[]{:S(2)}) collective-permute-start(bf16[768,256]{1,0:T(8,128)(2,1)S(1)} %constant_dynamic-update-slice_fusion.7.refs_7_), channel_id=1, source_target_pairs={{0,24},{8,0},{16,8},{24,16},{1,25},{9,1},{17,9},{25,17},{2,26},{10... | collective-permute-start | bytes 1179656 | tf_op jit(solution)/shard_map/ppermute | solution.py:25
  26.5 17.2 %collective-permute-start.22 = (bf16[768,256]{1,0:T(8,128)(2,1)S(1)}, bf16[768,256]{1,0:T(8,128)(2,1)S(1)}, u32[]{:S(2)}, u32[]{:S(2)}) collective-permute-start(bf16[768,256]{1,0:T(8,128)(2,1)S(1)} %constant_dynamic-update-slice_fusion.7.refs_7_), channel_id=1, source_target_pairs={{0,8},{8,16},{16,24},{24,0},{1,9},{9,17},{17,25},{25,1},{2,10},{10... | collective-permute-start | bytes 1179656 | tf_op jit(solution)/shard_map/ppermute | solution.py:25
  26.5 10.3 %collective-permute-start.5 = (bf16[384,256]{1,0:T(8,128)(2,1)S(1)}, bf16[384,256]{1,0:T(8,128)(2,1)S(1)}, u32[]{:S(2)}, u32[]{:S(2)}) collective-permute-start(bf16[384,256]{1,0:T(8,128)(2,1)S(1)} %pad_maximum_fusion.1), channel_id=1, source_target_pairs={{0,24},{8,0},{16,8},{24,16},{1,25},{9,1},{17,9},{25,17},{2,26},{10... | collective-permute-start | bytes 589832 | tf_op jit(solution)/shard_map/ppermute | solution.py:25
  29.3 7.5 %collective-permute-start.18 = (bf16[192,512]{1,0:T(8,128)(2,1)S(1)}, bf16[192,512]{1,0:T(8,128)(2,1)S(1)}, u32[]{:S(2)}, u32[]{:S(2)}) collective-permute-start(bf16[192,512]{1,0:T(8,128)(2,1)S(1)} %copy-done.3), channel_id=1, source_target_pairs={{0,4},{2,6},{4,0},{6,2},{1,5},{3,7},{5,1},{7,3},{8,12},{10,14},{12... | collective-permute-start | bytes 589832 | tf_op jit(solution)/shard_map/ppermute | solution.py:25
  31.2 8.4 %collective-permute-start.19 = (bf16[192,512]{1,0:T(8,128)(2,1)S(1)}, bf16[192,512]{1,0:T(8,128)(2,1)S(1)}, u32[]{:S(2)}, u32[]{:S(2)}) collective-permute-start(bf16[192,512]{1,0:T(8,128)(2,1)S(1)} %get-tuple-element.36), channel_id=1, source_target_pairs={{0,6},{2,0},{4,2},{6,4},{1,7},{3,1},{5,3},{7,5},{8,14},{10,8},{12,... | collective-permute-start | bytes 589832 | tf_op jit(solution)/shard_map/ppermute | solution.py:25
  36.8 9.5 %collective-permute-start.11 = (bf16[768,256]{1,0:T(8,128)(2,1)S(1)}, bf16[768,256]{1,0:T(8,128)(2,1)}, u32[]{:S(2)}, u32[]{:S(2)}) collective-permute-start(bf16[768,256]{1,0:T(8,128)(2,1)S(1)} %constant_dynamic-update-slice_fusion.4.refs_6_), channel_id=1, source_target_pairs={{0,8},{8,16},{16,24},{24,0},{1,9},{9,17},{17,25},{25,1},{2,10},{10... | collective-permute-start | bytes 1179656 | tf_op jit(solution)/shard_map/ppermute | solution.py:25
  36.8 15.4 %collective-permute-start.23 = (bf16[768,256]{1,0:T(8,128)(2,1)S(1)}, bf16[768,256]{1,0:T(8,128)(2,1)}, u32[]{:S(2)}, u32[]{:S(2)}) collective-permute-start(bf16[768,256]{1,0:T(8,128)(2,1)S(1)} %constant_dynamic-update-slice_fusion.4.refs_6_), channel_id=1, source_target_pairs={{0,24},{8,0},{16,8},{24,16},{1,25},{9,1},{17,9},{25,17},{2,26},{10... | collective-permute-start | bytes 1179656 | tf_op jit(solution)/shard_map/ppermute | solution.py:25
  39.6 13.9 %collective-permute-start.20 = (bf16[768,256]{1,0:T(8,128)(2,1)S(1)}, bf16[768,256]{1,0:T(8,128)(2,1)}, u32[]{:S(2)}, u32[]{:S(2)}) collective-permute-start(bf16[768,256]{1,0:T(8,128)(2,1)S(1)} %constant_dynamic-update-slice_fusion.refs_5_), channel_id=1, source_target_pairs={{0,32},{32,64},{64,96},{96,0},{1,33},{33,65},{65,97},{97,1},{2,34}... | collective-permute-start | bytes 1179656 | tf_op jit(solution)/shard_map/ppermute | solution.py:25
  42.8 10.9 %collective-permute-start.6 = (bf16[768,256]{1,0:T(8,128)(2,1)S(1)}, bf16[768,256]{1,0:T(8,128)(2,1)}, u32[]{:S(2)}, u32[]{:S(2)}) collective-permute-start(bf16[768,256]{1,0:T(8,128)(2,1)S(1)} %constant_dynamic-update-slice_fusion.refs_5_), channel_id=1, source_target_pairs={{0,96},{32,0},{64,32},{96,64},{1,97},{33,1},{65,33},{97,65},{2,98}... | collective-permute-start | bytes 1179656 | tf_op jit(solution)/shard_map/ppermute | solution.py:25
  43.7 15.5 %collective-permute-start.2 = (bf16[768,256]{1,0:T(8,128)(2,1)S(1)}, bf16[768,256]{1,0:T(8,128)(2,1)}, u32[]{:S(2)}, u32[]{:S(2)}) collective-permute-start(bf16[768,256]{1,0:T(8,128)(2,1)S(1)} %pad_maximum_fusion.refs_4_), channel_id=1, source_target_pairs={{0,32},{32,64},{64,96},{96,0},{1,33},{33,65},{65,97},{97,1},{2,34}... | collective-permute-start | bytes 1179656 | tf_op jit(solution)/shard_map/ppermute | solution.py:25
  46.3 20.2 %collective-permute-start.21 = (bf16[768,256]{1,0:T(8,128)(2,1)S(1)}, bf16[768,256]{1,0:T(8,128)(2,1)S(1)}, u32[]{:S(2)}, u32[]{:S(2)}) collective-permute-start(bf16[768,256]{1,0:T(8,128)(2,1)S(1)} %pad_maximum_fusion.refs_4_), channel_id=1, source_target_pairs={{0,96},{32,0},{64,32},{96,64},{1,97},{33,1},{65,33},{97,65},{2,98}... | collective-permute-start | bytes 1179656 | tf_op jit(solution)/shard_map/ppermute | solution.py:25
  52.2 20.8 %collective-permute-start.16 = (bf16[768,256]{1,0:T(8,128)(2,1)S(1)}, bf16[768,256]{1,0:T(8,128)(2,1)S(1)}, u32[]{:S(2)}, u32[]{:S(2)}) collective-permute-start(bf16[768,256]{1,0:T(8,128)(2,1)S(1)} %collective-permute-done.15.refs_11_), channel_id=1, source_target_pairs={{0,24},{8,0},{16,8},{24,16},{1,25},{9,1},{17,9},{25,17},{2,26},{10... | collective-permute-start | bytes 1179656 | tf_op jit(solution)/shard_map/ppermute | solution.py:25
  53.4 19.6 %collective-permute-start.12 = (bf16[768,256]{1,0:T(8,128)(2,1)}, bf16[768,256]{1,0:T(8,128)(2,1)S(1)}, u32[]{:S(2)}, u32[]{:S(2)}) collective-permute-start(bf16[768,256]{1,0:T(8,128)(2,1)} %collective-permute-done.11.refs_8_), channel_id=1, source_target_pairs={{0,8},{8,16},{16,24},{24,0},{1,9},{9,17},{17,25},{25,1},{2,10},{10... | collective-permute-start | bytes 1179656 | tf_op jit(solution)/shard_map/ppermute | solution.py:25
  53.7 19.3 %collective-permute-start.7 = (bf16[768,256]{1,0:T(8,128)(2,1)}, bf16[768,256]{1,0:T(8,128)(2,1)S(1)}, u32[]{:S(2)}, u32[]{:S(2)}) collective-permute-start(bf16[768,256]{1,0:T(8,128)(2,1)} %collective-permute-done.6.refs_7_), channel_id=1, source_target_pairs={{0,96},{32,0},{64,32},{96,64},{1,97},{33,1},{65,33},{97,65},{2,98}... | collective-permute-start | bytes 1179656 | tf_op jit(solution)/shard_map/ppermute | solution.py:25
  59.2 13.8 %collective-permute-start.3 = (bf16[768,256]{1,0:T(8,128)(2,1)}, bf16[768,256]{1,0:T(8,128)(2,1)S(1)}, u32[]{:S(2)}, u32[]{:S(2)}) collective-permute-start(bf16[768,256]{1,0:T(8,128)(2,1)} %collective-permute-done.2.refs_4_), channel_id=1, source_target_pairs={{0,32},{32,64},{64,96},{96,0},{1,33},{33,65},{65,97},{97,1},{2,34}... | collective-permute-start | bytes 1179656 | tf_op jit(solution)/shard_map/ppermute | solution.py:25
  77.4 11.6 %collective-permute-start.25 = (bf16[192,512]{1,0:T(8,128)(2,1)S(1)}, bf16[192,512]{1,0:T(8,128)(2,1)S(1)}, u32[]{:S(2)}, u32[]{:S(2)}) collective-permute-start(bf16[192,512]{1,0:T(8,128)(2,1)S(1)} %get-tuple-element.25), channel_id=1, source_target_pairs={{0,4},{2,6},{4,0},{6,2},{1,5},{3,7},{5,1},{7,3},{8,12},{10,14},{12... | collective-permute-start | bytes 589832 | tf_op jit(solution)/shard_map/ppermute | solution.py:25
  79.7 7.0 %collective-permute-start.27 = (bf16[96,512]{1,0:T(8,128)(2,1)S(1)}, bf16[96,512]{1,0:T(8,128)(2,1)S(1)}, u32[]{:S(2)}, u32[]{:S(2)}) collective-permute-start(bf16[96,512]{1,0:T(8,128)(2,1)S(1)} %get-tuple-element.29), channel_id=1, source_target_pairs={{0,6},{2,0},{4,2},{6,4},{1,7},{3,1},{5,3},{7,5},{8,14},{10,8},{12,... | collective-permute-start | bytes 294920 | tf_op jit(solution)/shard_map/ppermute | solution.py:25
  83.2 5.8 %collective-permute-start.28 = (bf16[96,512]{1,0:T(8,128)(2,1)S(1)}, bf16[96,512]{1,0:T(8,128)(2,1)S(1)}, u32[]{:S(2)}, u32[]{:S(2)}) collective-permute-start(bf16[96,512]{1,0:T(8,128)(2,1)S(1)} %get-tuple-element.30), channel_id=1, source_target_pairs={{0,2},{2,4},{4,6},{6,0},{1,3},{3,5},{5,7},{7,1},{8,10},{10,12},{12... | collective-permute-start | bytes 294920 | tf_op jit(solution)/shard_map/ppermute | solution.py:25
  92.4 12.3 %collective-permute-start.29 = (bf16[96,4096]{1,0:T(8,128)(2,1)S(1)}, bf16[96,4096]{1,0:T(8,128)(2,1)S(1)}, u32[]{:S(2)}, u32[]{:S(2)}) collective-permute-start(bf16[96,4096]{1,0:T(8,128)(2,1)S(1)} %project.3), channel_id=1, source_target_pairs={{0,1},{1,0},{2,3},{3,2},{4,5},{5,4},{6,7},{7,6},{8,9},{9,8},{10,11... | collective-permute-start | bytes 2359304 | tf_op jit(solution)/shard_map/ppermute | solution.py:326
  95.7 4.3 %collective-permute-start.24 = (bf16[96,512]{1,0:T(8,128)(2,1)S(1)}, bf16[96,512]{1,0:T(8,128)(2,1)S(1)}, u32[]{:S(2)}, u32[]{:S(2)}) collective-permute-start(bf16[96,512]{1,0:T(8,128)(2,1)S(1)} %get-tuple-element.24), channel_id=1, source_target_pairs={{0,6},{2,0},{4,2},{6,4},{1,7},{3,1},{5,3},{7,5},{8,14},{10,8},{12,... | collective-permute-start | bytes 294920 | tf_op jit(solution)/shard_map/ppermute | solution.py:25
  96.1 5.2 %collective-permute-start.26 = (bf16[96,512]{1,0:T(8,128)(2,1)S(1)}, bf16[96,512]{1,0:T(8,128)(2,1)S(1)}, u32[]{:S(2)}, u32[]{:S(2)}) collective-permute-start(bf16[96,512]{1,0:T(8,128)(2,1)S(1)} %get-tuple-element.26), channel_id=1, source_target_pairs={{0,2},{2,4},{4,6},{6,0},{1,3},{3,5},{5,7},{7,1},{8,10},{10,12},{12... | collective-permute-start | bytes 294920 | tf_op jit(solution)/shard_map/ppermute | solution.py:25

commit v5 on v4

--- a/solution.py
+++ b/solution.py
@@ -17,8 +17,8 @@
 MAX_TASKS = 160
 TILE = 16
 
-PHASES = (((0, 0), (0, 1)), ((1, 0), (1, 1), (3, 0), (3, 1)), ((2, 0), (2, 1)))
-CHUNKS = (256, 512, 256)
+PHASES = (((0, 0), (0, 1)), ((1, 0), (3, 1)), ((1, 1), (3, 0)), ((2, 0), (2, 1)))
+CHUNKS = (256, 256, 256, 256)
 
 
 def shift(value, axis, by):
@@ -27,7 +27,7 @@
 
 def phase_kernel(phase, *refs):
     chunk = CHUNKS[phase]
-    first_phase, last_phase = phase == 0, phase == 2
+    first_phase, last_phase = phase == 0, phase == 3
     order = PHASES[phase]
     refs = list(refs)
 
@@ -208,7 +208,7 @@
         outs = state + held
         first = 4 + len(pieces) + 1
         aliases = {first: 0, first + 1: 1}
-    if phase == 2:
+    if phase == 3:
         part = ((SPAN, GROUP * HEAD), jnp.bfloat16)
         outs = outs + [part] * 6 + [((2 * SPAN, GROUP * HEAD), jnp.bfloat16)]
     scratch = [
@@ -298,7 +298,7 @@
         behind_first = shift(first, far_axis, -1)
         far_first = shift(ahead_first, far_axis, 1)
         far_second = shift(behind_second, far_axis, -1)
-        return [first, second], [ahead_first, ahead_second, behind_first, behind_second], [far_first, far_second]
+        return [first, second], [ahead_first, behind_second], [ahead_second, behind_first], [far_first, far_second]
 
     pieces = [a + b for a, b in zip(gathered(low, "z", "x"), gathered(high, "x", "z"))]
 
@@ -307,15 +307,17 @@
     slot = jnp.arange(spans, dtype=jnp.int32)
     cp = slot // 2
     dx, dz, dy = (x - cp // 16) % RING, (z - (cp // 4) % 4) % RING, (y - cp % 4) % RING
-    far = jnp.where(dy < 2, dx, dz)
-    phase_of = jnp.where(far == 0, 0, jnp.where(far == 2, 2, 1))
+    far, near = jnp.where(dy < 2, dx, dz), jnp.where(dy < 2, dz, dx)
+    early = (far == 1) == (near < 2)
+    phase_of = jnp.where(far == 0, 0, jnp.where(far == 2, 3, jnp.where(early, 1, 2)))
     before = span_table[None, :] < jnp.arange(spans + 8, dtype=jnp.int32)[:, None]
-    ranks = [jnp.sum((before & (phase_of == p)[None, :]).astype(jnp.int32), axis=1) for p in range(3)]
+    ranks = [jnp.sum((before & (phase_of == p)[None, :]).astype(jnp.int32), axis=1) for p in range(4)]
 
     scalars = [coords, span_table, starts]
     q_all, best, acc, weight = run_phase(0, scalars + [ranks[0]], pieces[0], q_part, out_weight)
     best, acc = run_phase(1, scalars + [ranks[1]], pieces[1], [q_all, best, acc])
-    o_part = run_phase(2, scalars + [ranks[2]], pieces[2], [q_all, best, acc])[2:]
+    best, acc = run_phase(2, scalars + [ranks[2]], pieces[2], [q_all, best, acc])
+    o_part = run_phase(3, scalars + [ranks[3]], pieces[3], [q_all, best, acc])[2:]
 
     def returned(part):
         return [part[0], shift(part[1], "y", -1), both, shift(part[2], "y", 1)]

time: 107 us -> 117 us (1.093)
  waiting for transfers between devices: 25.9 us -> 31.8 us
  local copies, waits for them, and re-layouts: 2.91 us -> 6.96 us
  starting transfers between devices: 50.2 us -> 47.1 us
  Pallas kernels: 24.1 us -> 26.7 us
  other arithmetic: 2.44 us -> 3.72 us
    ppermute x29, waiting for transfers between devices: 25.9 us -> 31.8 us  [shift(): lax.ppermute(value, axis, [(i, (i + by) % RING) for i in range(RING)])]
    unnamed x12 -> x22, local copies, waits for them, and re-layouts: 1.01 us -> 5.8 us
    pallas_call x3 -> x4, Pallas kernels: 17.4 us -> 19.9 us  [run_phase(): pl.pallas_call(lambda *refs: phase_kernel(phase, *refs), out_shape=[jax.S...]
    ppermute x29, starting transfers between devices: 46.9 us -> 45 us  [shift(): lax.ppermute(value, axis, [(i, (i + by) % RING) for i in range(RING)])]
    ppermute x1, starting transfers between devices: 3.31 us -> 2.08 us  [layer(): sent = lax.ppermute(sent, 'hd', [(0, 1), (1, 0)])]
  transfers between devices with their start and end apart: 30 -> 30, of which waited for: 10 -> 11; matrix products, arithmetic and copies ran while one was open for 2% -> 2% of each run, Pallas kernels for 15% -> 16%
where the time goes in v5:
time: 117 us; the launch traced here: 116 us
  starting transfers between devices  47.1 us (40%)
  waiting for transfers between devices  31.8 us (27%)
  Pallas kernels  26.7 us (23%)
  local copies, waits for them, and re-layouts  6.96 us (6%)
  other arithmetic  3.72 us (3%)
    ppermute x29, starting transfers between devices, shift(): lax.ppermute(value, axis, [(i, (i + by) % RING) for i in range(RING)])  45 us
    ppermute x29, waiting for transfers between devices, shift(): lax.ppermute(value, axis, [(i, (i + by) % RING) for i in range(RING)])  31.8 us
    pallas_call x4, Pallas kernels, run_phase(): pl.pallas_call(lambda *refs: phase_kernel(phase, *refs), out_shape=[jax.S...  19.9 us
    pallas_call x2, Pallas kernels, project(): pl.pallas_call(lambda *refs: project_kernel(turn, *refs), out_shape=jax.S...  6.76 us
    unnamed x22, local copies, waits for them, and re-layouts  5.8 us
  transfers between devices with their start and end apart: 30, of which 11 were waited for; matrix products, arithmetic and copies ran while one was open for 2% of the time, Pallas kernels for 16%

profile of v5, /device:TPU:1, one launch (start us, length us, event | category | flops | bytes accessed | tf_op | source)
XLA Modules:
  0.0 116.4 jit_solution(4866449776115179853)
XLA Ops:
  0.0 0.9 copy-done
  1.0 1.0 bitcast_dynamic-update-slice_fusion
  2.0 3.8 %collective-permute-start.8 = (bf16[192,256]{1,0:T(8,128)(2,1)S(1)}, bf16[192,256]{1,0:T(8,128)(2,1)S(1)}, u32[]{:S(2)}, u32[]{:S(2)}) collective-permute-start(bf16[192,256]{1,0:T(8,128)(2,1)S(1)} %get-tuple-element.46), channel_id=1, source_target_pairs={{0,4},{2,6},{4,0},{6,2},{1,5},{3,7},{5,1},{7,3},{8,12},{10,14},{12... | collective-permute-start | bytes 294920 | tf_op jit(solution)/shard_map/ppermute | solution.py:25
  5.8 0.8 collective-permute-start.9
  6.6 0.7 collective-permute-start
  7.9 2.4 %collective-permute-done.9 = bf16[192,256]{1,0:T(8,128)(2,1)S(1)} collective-permute-done((bf16[192,256]{1,0:T(8,128)(2,1)S(1)}, bf16[192,256]{1,0:T(8,128)(2,1)S(1)}, u32[]{:S(2)}, u32[]{:S(2)}) %collective-permute-start.9) | collective-permute-done | bytes 98336 | tf_op jit(solution)/shard_map/ppermute | solution.py:25
  10.3 2.8 %collective-permute-start.13 = (bf16[384,256]{1,0:T(8,128)(2,1)S(1)}, bf16[384,256]{1,0:T(8,128)(2,1)S(1)}, u32[]{:S(2)}, u32[]{:S(2)}) collective-permute-start(bf16[384,256]{1,0:T(8,128)(2,1)S(1)} %get-tuple-element.49), channel_id=1, source_target_pairs={{0,64},{32,96},{64,0},{96,32},{1,65},{33,97},{65,1},{97,33},{2,66}... | collective-permute-start | bytes 589832 | tf_op jit(solution)/shard_map/ppermute | solution.py:25
  13.2 0.9 collective-permute-start.14
  14.1 0.6 collective-permute-start.10
  14.8 3.7 %collective-permute-start.4 = (bf16[384,256]{1,0:T(8,128)(2,1)S(1)}, bf16[384,256]{1,0:T(8,128)(2,1)S(1)}, u32[]{:S(2)}, u32[]{:S(2)}) collective-permute-start(bf16[384,256]{1,0:T(8,128)(2,1)S(1)} %pad_maximum_fusion.1), channel_id=1, source_target_pairs={{0,16},{8,24},{16,0},{24,8},{1,17},{9,25},{17,1},{25,9},{2,18},{10... | collective-permute-start | bytes 589832 | tf_op jit(solution)/shard_map/ppermute | solution.py:25
  18.9 1.0 collective-permute-start.1
  19.9 1.2 %collective-permute-done.14 = bf16[384,256]{1,0:T(8,128)(2,1)S(1)} collective-permute-done((bf16[384,256]{1,0:T(8,128)(2,1)S(1)}, bf16[384,256]{1,0:T(8,128)(2,1)S(1)}, u32[]{:S(2)}, u32[]{:S(2)}) %collective-permute-start.14) | collective-permute-done | bytes 196640 | tf_op jit(solution)/shard_map/ppermute | solution.py:25
  21.2 3.8 %collective-permute-start.15 = (bf16[768,256]{1,0:T(8,128)(2,1)S(1)}, bf16[768,256]{1,0:T(8,128)(2,1)S(1)}, u32[]{:S(2)}, u32[]{:S(2)}) collective-permute-start(bf16[768,256]{1,0:T(8,128)(2,1)S(1)} %constant_dynamic-update-slice_fusion.7.refs_7_), channel_id=1, source_target_pairs={{0,24},{8,0},{16,8},{24,16},{1,25},{9,1},{17,9},{25,17},{2,26},{10... | collective-permute-start | bytes 1179656 | tf_op jit(solution)/shard_map/ppermute | solution.py:25
  25.2 2.8 %collective-permute-start.17 = (bf16[192,512]{1,0:T(8,128)(2,1)S(1)}, bf16[192,512]{1,0:T(8,128)(2,1)S(1)}, u32[]{:S(2)}, u32[]{:S(2)}) collective-permute-start(bf16[192,512]{1,0:T(8,128)(2,1)S(1)} %get-tuple-element.42), channel_id=1, source_target_pairs={{0,2},{2,4},{4,6},{6,0},{1,3},{3,5},{5,7},{7,1},{8,10},{10,12},{12... | collective-permute-start | bytes 589832 | tf_op jit(solution)/shard_map/ppermute | solution.py:25
  28.0 2.6 %collective-permute-start.18 = (bf16[192,512]{1,0:T(8,128)(2,1)S(1)}, bf16[192,512]{1,0:T(8,128)(2,1)S(1)}, u32[]{:S(2)}, u32[]{:S(2)}) collective-permute-start(bf16[192,512]{1,0:T(8,128)(2,1)S(1)} %get-tuple-element.44), channel_id=1, source_target_pairs={{0,4},{2,6},{4,0},{6,2},{1,5},{3,7},{5,1},{7,3},{8,12},{10,14},{12... | collective-permute-start | bytes 589832 | tf_op jit(solution)/shard_map/ppermute | solution.py:25
  30.6 1.3 %collective-permute-start.19 = (bf16[192,512]{1,0:T(8,128)(2,1)S(1)}, bf16[192,512]{1,0:T(8,128)(2,1)S(1)}, u32[]{:S(2)}, u32[]{:S(2)}) collective-permute-start(bf16[192,512]{1,0:T(8,128)(2,1)S(1)} %get-tuple-element.41), channel_id=1, source_target_pairs={{0,6},{2,0},{4,2},{6,4},{1,7},{3,1},{5,3},{7,5},{8,14},{10,8},{12,... | collective-permute-start | bytes 589832 | tf_op jit(solution)/shard_map/ppermute | solution.py:25
  31.9 0.8 collective-permute-done.17.refs_9_
  32.8 0.7 copy-done.1
  33.4 4.1 %collective-permute-done.18.refs_10_ = bf16[192,512]{1,0:T(8,128)(2,1)S(1)} collective-permute-done((bf16[192,512]{1,0:T(8,128)(2,1)S(1)}, bf16[192,512]{1,0:T(8,128)(2,1)S(1)}, u32[]{:S(2)}, u32[]{:S(2)}) %collective-permute-start.18) | collective-permute-done | bytes 196640 | tf_op jit(solution)/shard_map/ppermute | solution.py:25
  37.6 0.7 copy-done.3
  38.2 2.4 %collective-permute-start.23 = (bf16[768,256]{1,0:T(8,128)(2,1)S(1)}, bf16[768,256]{1,0:T(8,128)(2,1)}, u32[]{:S(2)}, u32[]{:S(2)}) collective-permute-start(bf16[768,256]{1,0:T(8,128)(2,1)S(1)} %constant_dynamic-update-slice_fusion.4.refs_6_), channel_id=1, source_target_pairs={{0,24},{8,0},{16,8},{24,16},{1,25},{9,1},{17,9},{25,17},{2,26},{10... | collective-permute-start | bytes 1179656 | tf_op jit(solution)/shard_map/ppermute | solution.py:25
  40.6 0.7 copy-done.5
  41.3 4.8 %collective-permute-start.6 = (bf16[768,256]{1,0:T(8,128)(2,1)S(1)}, bf16[768,256]{1,0:T(8,128)(2,1)S(1)}, u32[]{:S(2)}, u32[]{:S(2)}) collective-permute-start(bf16[768,256]{1,0:T(8,128)(2,1)S(1)} %constant_dynamic-update-slice_fusion.refs_5_), channel_id=1, source_target_pairs={{0,96},{32,0},{64,32},{96,64},{1,97},{33,1},{65,33},{97,65},{2,98}... | collective-permute-start | bytes 1179656 | tf_op jit(solution)/shard_map/ppermute | solution.py:25
  46.3 0.6 broadcast_compare_fusion.2
  46.8 0.9 convert_reduce_fusion.1
  47.7 1.0 convert_reduce_fusion.refs_2_
  48.7 3.6 %collective-permute-done.6.refs_5_ = bf16[768,256]{1,0:T(8,128)(2,1)S(1)} collective-permute-done((bf16[768,256]{1,0:T(8,128)(2,1)S(1)}, bf16[768,256]{1,0:T(8,128)(2,1)S(1)}, u32[]{:S(2)}, u32[]{:S(2)}) %collective-permute-start.6) | collective-permute-done | bytes 393248 | tf_op jit(solution)/shard_map/ppermute | solution.py:25
  52.3 3.4 %collective-permute-start.21 = (bf16[768,256]{1,0:T(8,128)(2,1)S(1)}, bf16[768,256]{1,0:T(8,128)(2,1)S(1)}, u32[]{:S(2)}, u32[]{:S(2)}) collective-permute-start(bf16[768,256]{1,0:T(8,128)(2,1)S(1)} %pad_maximum_fusion.refs_4_), channel_id=1, source_target_pairs={{0,96},{32,0},{64,32},{96,64},{1,97},{33,1},{65,33},{97,65},{2,98}... | collective-permute-start | bytes 1179656 | tf_op jit(solution)/shard_map/ppermute | solution.py:25
  55.8 8.2 %collective-permute-done.2.refs_4_ = bf16[768,256]{1,0:T(8,128)(2,1)} collective-permute-done((bf16[768,256]{1,0:T(8,128)(2,1)S(1)}, bf16[768,256]{1,0:T(8,128)(2,1)}, u32[]{:S(2)}, u32[]{:S(2)}) %collective-permute-start.2) | collective-permute-done | bytes 393248 | tf_op jit(solution)/shard_map/ppermute | solution.py:25
  64.3 1.2 %collective-permute-start.12 = (bf16[768,256]{1,0:T(8,128)(2,1)S(1)}, bf16[768,256]{1,0:T(8,128)(2,1)S(1)}, u32[]{:S(2)}, u32[]{:S(2)}) collective-permute-start(bf16[768,256]{1,0:T(8,128)(2,1)S(1)} %collective-permute-done.11.refs_6_), channel_id=1, source_target_pairs={{0,8},{8,16},{16,24},{24,0},{1,9},{9,17},{17,25},{25,1},{2,10},{10... | collective-permute-start | bytes 1179656 | tf_op jit(solution)/shard_map/ppermute | solution.py:25
  65.5 1.5 %collective-permute-start.3 = (bf16[768,256]{1,0:T(8,128)(2,1)}, bf16[768,256]{1,0:T(8,128)(2,1)S(1)}, u32[]{:S(2)}, u32[]{:S(2)}) collective-permute-start(bf16[768,256]{1,0:T(8,128)(2,1)} %collective-permute-done.2.refs_4_), channel_id=1, source_target_pairs={{0,32},{32,64},{64,96},{96,0},{1,33},{33,65},{65,97},{97,1},{2,34}... | collective-permute-start | bytes 1179656 | tf_op jit(solution)/shard_map/ppermute | solution.py:25
  67.0 0.9 copy-done.2
  67.9 0.9 copy-done.4
  68.8 0.9 copy-done.6
  69.7 6.5 %shard_map.64 = (bf16[8,384,256]{2,1,0:T(8,128)(2,1)S(1)}, f32[8,384,128]{2,1,0:T(8,128)S(1)}, f32[8,384,256]{2,1,0:T(8,128)S(1)}, bf16[2048,4096]{1,0:T(8,128)(2,1)S(1)}) custom-call(s32[4]{0:T(128)S(1)} %pad_add_fusion.refs_0_, s32[128]{0:T(128)S(1)} %copy-done.7, s32[8]{0:T(128)S(1)} %convert_reduce_fusion.refs_2_, s32[136]{0:T(256)S(1)} %get-tuple-element.37.refs_3_, ...), custom_call_target="tpu_custom_call" | custom-call | flops 2000000000 | bytes 2500000 | tf_op jit(solution)/shard_map/pallas_call | solution.py:229
  76.2 4.3 %shard_map.65 = (f32[8,384,128]{2,1,0:T(8,128)S(1)}, f32[8,384,256]{2,1,0:T(8,128)S(1)}) custom-call(s32[4]{0:T(128)S(1)} %pad_add_fusion.refs_0_, s32[128]{0:T(128)S(1)} %copy-done.7, s32[8]{0:T(128)S(1)} %convert_reduce_fusion.refs_2_, s32[136]{0:T(256)S(1)} %get-tuple-element.35.refs_3_, ...), custom_call_target="tpu_custom_call", output_to_operand_aliasing={{0}: (9, {}), {1}: (10, {})} | custom-call | flops 2000000000 | bytes 2500000 | tf_op jit(solution)/shard_map/pallas_call | solution.py:229
  80.6 4.7 %shard_map.66 = (f32[8,384,128]{2,1,0:T(8,128)S(1)}, f32[8,384,256]{2,1,0:T(8,128)S(1)}) custom-call(s32[4]{0:T(128)S(1)} %pad_add_fusion.refs_0_, s32[128]{0:T(128)S(1)} %copy-done.7, s32[8]{0:T(128)S(1)} %convert_reduce_fusion.refs_2_, s32[136]{0:T(256)S(1)} %get-tuple-element.36.refs_3_, ...), custom_call_target="tpu_custom_call", output_to_operand_aliasing={{0}: (9, {}), {1}: (10, {})} | custom-call | flops 2000000000 | bytes 2500000 | tf_op jit(solution)/shard_map/pallas_call | solution.py:229
  85.3 4.4 %shard_map.67 = (f32[8,384,128]{2,1,0:T(8,128)S(1)}, f32[8,384,256]{2,1,0:T(8,128)S(1)}, bf16[96,512]{1,0:T(8,128)(2,1)S(1)}, bf16[96,512]{1,0:T(8,128)(2,1)S(1)...) custom-call(s32[4]{0:T(128)S(1)} %pad_add_fusion.refs_0_, ...), custom_call_target="tpu_custom_call", output_to_operand_aliasing={{0}: (9, {}), {1}: (10, {})} | custom-call | flops 2000000000 | bytes 2500000 | tf_op jit(solution)/shard_map/pallas_call | solution.py:229
  89.8 4.4 %collective-permute-start.27 = (bf16[96,512]{1,0:T(8,128)(2,1)S(1)}, bf16[96,512]{1,0:T(8,128)(2,1)S(1)}, u32[]{:S(2)}, u32[]{:S(2)}) collective-permute-start(bf16[96,512]{1,0:T(8,128)(2,1)S(1)} %get-tuple-element.33), channel_id=1, source_target_pairs={{0,6},{2,0},{4,2},{6,4},{1,7},{3,1},{5,3},{7,5},{8,14},{10,8},{12,... | collective-permute-start | bytes 294920 | tf_op jit(solution)/shard_map/ppermute | solution.py:25
  94.2 2.5 %collective-permute-done.27.refs_2_ = bf16[96,512]{1,0:T(8,128)(2,1)S(1)} collective-permute-done((bf16[96,512]{1,0:T(8,128)(2,1)S(1)}, bf16[96,512]{1,0:T(8,128)(2,1)S(1)}, u32[]{:S(2)}, u32[]{:S(2)}) %collective-permute-start.27) | collective-permute-done | bytes 98336 | tf_op jit(solution)/shard_map/ppermute | solution.py:25
  96.8 4.3 %collective-permute-done.28.refs_4_ = bf16[96,512]{1,0:T(8,128)(2,1)S(1)} collective-permute-done((bf16[96,512]{1,0:T(8,128)(2,1)S(1)}, bf16[96,512]{1,0:T(8,128)(2,1)S(1)}, u32[]{:S(2)}, u32[]{:S(2)}) %collective-permute-start.28) | collective-permute-done | bytes 98336 | tf_op jit(solution)/shard_map/ppermute | solution.py:25
  101.1 3.4 %project.3 = bf16[96,4096]{1,0:T(8,128)(2,1)S(1)} custom-call(s32[4]{0:T(128)S(1)} %pad_add_fusion.refs_0_, bf16[96,512]{1,0:T(8,128)(2,1)S(1)} %get-tuple-element.32.refs_1_, bf16[96,512]{1,0:T(8,128)(2,1)S(1)} %collective-permute-done.27.refs_2_, bf16[192,512]{1,0:T(8,128)(2,1)S(1)} %collective-permute-done.25.refs_3_, ...), custom_call_target="tpu_custom_call" | custom-call | flops 1610612736 | bytes 16777216 | tf_op jit(solution)/shard_map/project/pallas_call | solution.py:263
  104.5 2.1 %collective-permute-start.29 = (bf16[96,4096]{1,0:T(8,128)(2,1)S(1)}, bf16[96,4096]{1,0:T(8,128)(2,1)S(1)}, u32[]{:S(2)}, u32[]{:S(2)}) collective-permute-start(bf16[96,4096]{1,0:T(8,128)(2,1)S(1)} %project.3), channel_id=1, source_target_pairs={{0,1},{1,0},{2,3},{3,2},{4,5},{5,4},{6,7},{7,6},{8,9},{9,8},{10,11... | collective-permute-start | bytes 2359304 | tf_op jit(solution)/shard_map/ppermute | solution.py:328
  106.6 1.5 %collective-permute-start.26 = (bf16[96,512]{1,0:T(8,128)(2,1)S(1)}, bf16[96,512]{1,0:T(8,128)(2,1)S(1)}, u32[]{:S(2)}, u32[]{:S(2)}) collective-permute-start(bf16[96,512]{1,0:T(8,128)(2,1)S(1)} %get-tuple-element.30), channel_id=1, source_target_pairs={{0,2},{2,4},{4,6},{6,0},{1,3},{3,5},{5,7},{7,1},{8,10},{10,12},{12... | collective-permute-start | bytes 294920 | tf_op jit(solution)/shard_map/ppermute | solution.py:25
  108.0 2.8 %collective-permute-done.24.refs_2_ = bf16[96,512]{1,0:T(8,128)(2,1)S(1)} collective-permute-done((bf16[96,512]{1,0:T(8,128)(2,1)S(1)}, bf16[96,512]{1,0:T(8,128)(2,1)S(1)}, u32[]{:S(2)}, u32[]{:S(2)}) %collective-permute-start.24) | collective-permute-done | bytes 98336 | tf_op jit(solution)/shard_map/ppermute | solution.py:25
  110.8 1.1 collective-permute-done.26.refs_4_
  112.0 3.4 %project.2 = f32[96,4096]{1,0:T(8,128)S(1)} custom-call(s32[4]{0:T(128)S(1)} %pad_add_fusion.refs_0_, bf16[96,512]{1,0:T(8,128)(2,1)S(1)} %get-tuple-element.27.refs_1_, bf16[96,512]{1,0:T(8,128)(2,1)S(1)} %collective-permute-done.24.refs_2_, bf16[192,512]{1,0:T(8,128)(2,1)S(1)} %collective-permute-done.25.refs_3_, ...), custom_call_target="tpu_custom_call" | custom-call | flops 1610612736 | bytes 16777216 | tf_op jit(solution)/shard_map/project/pallas_call | solution.py:263
  115.3 1.1 add_convert_fusion
  (55 shorter events, 2.1 us)
Async XLA Ops:
  0.0 0.9 copy-start
  0.0 13.1 %copy-start.8 = (bf16[192,2048]{1,0:T(8,128)(2,1)S(1)}, bf16[192,2048]{1,0:T(8,128)(2,1)}, u32[]{:S(2)}) copy-start(bf16[192,2048]{1,0:T(8,128)(2,1)} %param.6) | copy-start | bytes 2359300
  2.0 5.8 %collective-permute-start.8 = (bf16[192,256]{1,0:T(8,128)(2,1)S(1)}, bf16[192,256]{1,0:T(8,128)(2,1)S(1)}, u32[]{:S(2)}, u32[]{:S(2)}) collective-permute-start(bf16[192,256]{1,0:T(8,128)(2,1)S(1)} %get-tuple-element.46), channel_id=1, source_target_pairs={{0,4},{2,6},{4,0},{6,2},{1,5},{3,7},{5,1},{7,3},{8,12},{10,14},{12... | collective-permute-start | bytes 294920 | tf_op jit(solution)/shard_map/ppermute | solution.py:25
  5.8 4.4 %collective-permute-start.9 = (bf16[192,256]{1,0:T(8,128)(2,1)S(1)}, bf16[192,256]{1,0:T(8,128)(2,1)S(1)}, u32[]{:S(2)}, u32[]{:S(2)}) collective-permute-start(bf16[192,256]{1,0:T(8,128)(2,1)S(1)} %get-tuple-element.45), channel_id=1, source_target_pairs={{0,6},{2,0},{4,2},{6,4},{1,7},{3,1},{5,3},{7,5},{8,14},{10,8},{12,... | collective-permute-start | bytes 294920 | tf_op jit(solution)/shard_map/ppermute | solution.py:25
  6.6 8.1 %collective-permute-start = (bf16[192,256]{1,0:T(8,128)(2,1)S(1)}, bf16[192,256]{1,0:T(8,128)(2,1)S(1)}, u32[]{:S(2)}, u32[]{:S(2)}) collective-permute-start(bf16[192,256]{1,0:T(8,128)(2,1)S(1)} %get-tuple-element.47), channel_id=1, source_target_pairs={{0,2},{2,4},{4,6},{6,0},{1,3},{3,5},{5,7},{7,1},{8,10},{10,12},{12... | collective-permute-start | bytes 294920 | tf_op jit(solution)/shard_map/ppermute | solution.py:25
  10.3 8.6 %collective-permute-start.13 = (bf16[384,256]{1,0:T(8,128)(2,1)S(1)}, bf16[384,256]{1,0:T(8,128)(2,1)S(1)}, u32[]{:S(2)}, u32[]{:S(2)}) collective-permute-start(bf16[384,256]{1,0:T(8,128)(2,1)S(1)} %get-tuple-element.49), channel_id=1, source_target_pairs={{0,64},{32,96},{64,0},{96,32},{1,65},{33,97},{65,1},{97,33},{2,66}... | collective-permute-start | bytes 589832 | tf_op jit(solution)/shard_map/ppermute | solution.py:25
  13.2 7.9 %collective-permute-start.14 = (bf16[384,256]{1,0:T(8,128)(2,1)S(1)}, bf16[384,256]{1,0:T(8,128)(2,1)S(1)}, u32[]{:S(2)}, u32[]{:S(2)}) collective-permute-start(bf16[384,256]{1,0:T(8,128)(2,1)S(1)} %get-tuple-element.49), channel_id=1, source_target_pairs={{0,96},{32,0},{64,32},{96,64},{1,97},{33,1},{65,33},{97,65},{2,98}... | collective-permute-start | bytes 589832 | tf_op jit(solution)/shard_map/ppermute | solution.py:25
  14.1 10.9 %collective-permute-start.10 = (bf16[384,256]{1,0:T(8,128)(2,1)S(1)}, bf16[384,256]{1,0:T(8,128)(2,1)S(1)}, u32[]{:S(2)}, u32[]{:S(2)}) collective-permute-start(bf16[384,256]{1,0:T(8,128)(2,1)S(1)} %get-tuple-element.49), channel_id=1, source_target_pairs={{0,32},{32,64},{64,96},{96,0},{1,33},{33,65},{65,97},{97,1},{2,34}... | collective-permute-start | bytes 589832 | tf_op jit(solution)/shard_map/ppermute | solution.py:25
  14.8 32.1 %copy-start.7 = (s32[128]{0:T(128)S(1)}, s32[128]{0:T(128)}, u32[]{:S(2)}) copy-start(s32[128]{0:T(128)} %refs_1_.7) | copy-start | bytes 1540
  14.8 10.4 %collective-permute-start.4 = (bf16[384,256]{1,0:T(8,128)(2,1)S(1)}, bf16[384,256]{1,0:T(8,128)(2,1)S(1)}, u32[]{:S(2)}, u32[]{:S(2)}) collective-permute-start(bf16[384,256]{1,0:T(8,128)(2,1)S(1)} %pad_maximum_fusion.1), channel_id=1, source_target_pairs={{0,16},{8,24},{16,0},{24,8},{1,17},{9,25},{17,1},{25,9},{2,18},{10... | collective-permute-start | bytes 589832 | tf_op jit(solution)/shard_map/ppermute | solution.py:25
  18.5 9.5 %collective-permute-start.5 = (bf16[384,256]{1,0:T(8,128)(2,1)S(1)}, bf16[384,256]{1,0:T(8,128)(2,1)S(1)}, u32[]{:S(2)}, u32[]{:S(2)}) collective-permute-start(bf16[384,256]{1,0:T(8,128)(2,1)S(1)} %pad_maximum_fusion.1), channel_id=1, source_target_pairs={{0,24},{8,0},{16,8},{24,16},{1,25},{9,1},{17,9},{25,17},{2,26},{10... | collective-permute-start | bytes 589832 | tf_op jit(solution)/shard_map/ppermute | solution.py:25
  18.9 11.7 %collective-permute-start.1 = (bf16[384,256]{1,0:T(8,128)(2,1)S(1)}, bf16[384,256]{1,0:T(8,128)(2,1)S(1)}, u32[]{:S(2)}, u32[]{:S(2)}) collective-permute-start(bf16[384,256]{1,0:T(8,128)(2,1)S(1)} %pad_maximum_fusion.1), channel_id=1, source_target_pairs={{0,8},{8,16},{16,24},{24,0},{1,9},{9,17},{17,25},{25,1},{2,10},{10... | collective-permute-start | bytes 589832 | tf_op jit(solution)/shard_map/ppermute | solution.py:25
  21.2 24.9 %collective-permute-start.15 = (bf16[768,256]{1,0:T(8,128)(2,1)S(1)}, bf16[768,256]{1,0:T(8,128)(2,1)S(1)}, u32[]{:S(2)}, u32[]{:S(2)}) collective-permute-start(bf16[768,256]{1,0:T(8,128)(2,1)S(1)} %constant_dynamic-update-slice_fusion.7.refs_7_), channel_id=1, source_target_pairs={{0,24},{8,0},{16,8},{24,16},{1,25},{9,1},{17,9},{25,17},{2,26},{10... | collective-permute-start | bytes 1179656 | tf_op jit(solution)/shard_map/ppermute | solution.py:25
  25.0 21.0 %collective-permute-start.11 = (bf16[768,256]{1,0:T(8,128)(2,1)S(1)}, bf16[768,256]{1,0:T(8,128)(2,1)S(1)}, u32[]{:S(2)}, u32[]{:S(2)}) collective-permute-start(bf16[768,256]{1,0:T(8,128)(2,1)S(1)} %constant_dynamic-update-slice_fusion.4.refs_6_), channel_id=1, source_target_pairs={{0,8},{8,16},{16,24},{24,0},{1,9},{9,17},{17,25},{25,1},{2,10},{10... | collective-permute-start | bytes 1179656 | tf_op jit(solution)/shard_map/ppermute | solution.py:25
  25.2 7.6 %collective-permute-start.17 = (bf16[192,512]{1,0:T(8,128)(2,1)S(1)}, bf16[192,512]{1,0:T(8,128)(2,1)S(1)}, u32[]{:S(2)}, u32[]{:S(2)}) collective-permute-start(bf16[192,512]{1,0:T(8,128)(2,1)S(1)} %get-tuple-element.42), channel_id=1, source_target_pairs={{0,2},{2,4},{4,6},{6,0},{1,3},{3,5},{5,7},{7,1},{8,10},{10,12},{12... | collective-permute-start | bytes 589832 | tf_op jit(solution)/shard_map/ppermute | solution.py:25
  28.0 9.6 %collective-permute-start.18 = (bf16[192,512]{1,0:T(8,128)(2,1)S(1)}, bf16[192,512]{1,0:T(8,128)(2,1)S(1)}, u32[]{:S(2)}, u32[]{:S(2)}) collective-permute-start(bf16[192,512]{1,0:T(8,128)(2,1)S(1)} %get-tuple-element.44), channel_id=1, source_target_pairs={{0,4},{2,6},{4,0},{6,2},{1,5},{3,7},{5,1},{7,3},{8,12},{10,14},{12... | collective-permute-start | bytes 589832 | tf_op jit(solution)/shard_map/ppermute | solution.py:25
  30.6 10.0 %collective-permute-start.19 = (bf16[192,512]{1,0:T(8,128)(2,1)S(1)}, bf16[192,512]{1,0:T(8,128)(2,1)S(1)}, u32[]{:S(2)}, u32[]{:S(2)}) collective-permute-start(bf16[192,512]{1,0:T(8,128)(2,1)S(1)} %get-tuple-element.41), channel_id=1, source_target_pairs={{0,6},{2,0},{4,2},{6,4},{1,7},{3,1},{5,3},{7,5},{8,14},{10,8},{12,... | collective-permute-start | bytes 589832 | tf_op jit(solution)/shard_map/ppermute | solution.py:25
  32.8 0.7 copy-start.1
  33.4 30.9 %collective-permute-start.22 = (bf16[768,256]{1,0:T(8,128)(2,1)S(1)}, bf16[768,256]{1,0:T(8,128)(2,1)S(1)}, u32[]{:S(2)}, u32[]{:S(2)}) collective-permute-start(bf16[768,256]{1,0:T(8,128)(2,1)S(1)} %constant_dynamic-update-slice_fusion.7.refs_7_), channel_id=1, source_target_pairs={{0,8},{8,16},{16,24},{24,0},{1,9},{9,17},{17,25},{25,1},{2,10},{10... | collective-permute-start | bytes 1179656 | tf_op jit(solution)/shard_map/ppermute | solution.py:25
  37.6 0.7 copy-start.3
  38.2 27.2 %collective-permute-start.23 = (bf16[768,256]{1,0:T(8,128)(2,1)S(1)}, bf16[768,256]{1,0:T(8,128)(2,1)}, u32[]{:S(2)}, u32[]{:S(2)}) collective-permute-start(bf16[768,256]{1,0:T(8,128)(2,1)S(1)} %constant_dynamic-update-slice_fusion.4.refs_6_), channel_id=1, source_target_pairs={{0,24},{8,0},{16,8},{24,16},{1,25},{9,1},{17,9},{25,17},{2,26},{10... | collective-permute-start | bytes 1179656 | tf_op jit(solution)/shard_map/ppermute | solution.py:25
  40.6 0.7 copy-start.5
  41.3 11.1 %collective-permute-start.6 = (bf16[768,256]{1,0:T(8,128)(2,1)S(1)}, bf16[768,256]{1,0:T(8,128)(2,1)S(1)}, u32[]{:S(2)}, u32[]{:S(2)}) collective-permute-start(bf16[768,256]{1,0:T(8,128)(2,1)S(1)} %constant_dynamic-update-slice_fusion.refs_5_), channel_id=1, source_target_pairs={{0,96},{32,0},{64,32},{96,64},{1,97},{33,1},{65,33},{97,65},{2,98}... | collective-permute-start | bytes 1179656 | tf_op jit(solution)/shard_map/ppermute | solution.py:25
  46.1 19.4 %collective-permute-start.20 = (bf16[768,256]{1,0:T(8,128)(2,1)S(1)}, bf16[768,256]{1,0:T(8,128)(2,1)}, u32[]{:S(2)}, u32[]{:S(2)}) collective-permute-start(bf16[768,256]{1,0:T(8,128)(2,1)S(1)} %constant_dynamic-update-slice_fusion.refs_5_), channel_id=1, source_target_pairs={{0,32},{32,64},{64,96},{96,0},{1,33},{33,65},{65,97},{97,1},{2,34}... | collective-permute-start | bytes 1179656 | tf_op jit(solution)/shard_map/ppermute | solution.py:25
  46.1 17.9 %collective-permute-start.2 = (bf16[768,256]{1,0:T(8,128)(2,1)S(1)}, bf16[768,256]{1,0:T(8,128)(2,1)}, u32[]{:S(2)}, u32[]{:S(2)}) collective-permute-start(bf16[768,256]{1,0:T(8,128)(2,1)S(1)} %pad_maximum_fusion.refs_4_), channel_id=1, source_target_pairs={{0,32},{32,64},{64,96},{96,0},{1,33},{33,65},{65,97},{97,1},{2,34}... | collective-permute-start | bytes 1179656 | tf_op jit(solution)/shard_map/ppermute | solution.py:25
  52.3 28.2 %collective-permute-start.21 = (bf16[768,256]{1,0:T(8,128)(2,1)S(1)}, bf16[768,256]{1,0:T(8,128)(2,1)S(1)}, u32[]{:S(2)}, u32[]{:S(2)}) collective-permute-start(bf16[768,256]{1,0:T(8,128)(2,1)S(1)} %pad_maximum_fusion.refs_4_), channel_id=1, source_target_pairs={{0,96},{32,0},{64,32},{96,64},{1,97},{33,1},{65,33},{97,65},{2,98}... | collective-permute-start | bytes 1179656 | tf_op jit(solution)/shard_map/ppermute | solution.py:25
  64.0 21.3 %collective-permute-start.16 = (bf16[768,256]{1,0:T(8,128)(2,1)S(1)}, bf16[768,256]{1,0:T(8,128)(2,1)S(1)}, u32[]{:S(2)}, u32[]{:S(2)}) collective-permute-start(bf16[768,256]{1,0:T(8,128)(2,1)S(1)} %collective-permute-done.15.refs_7_), channel_id=1, source_target_pairs={{0,24},{8,0},{16,8},{24,16},{1,25},{9,1},{17,9},{25,17},{2,26},{10... | collective-permute-start | bytes 1179656 | tf_op jit(solution)/shard_map/ppermute | solution.py:25
  64.3 21.0 %collective-permute-start.12 = (bf16[768,256]{1,0:T(8,128)(2,1)S(1)}, bf16[768,256]{1,0:T(8,128)(2,1)S(1)}, u32[]{:S(2)}, u32[]{:S(2)}) collective-permute-start(bf16[768,256]{1,0:T(8,128)(2,1)S(1)} %collective-permute-done.11.refs_6_), channel_id=1, source_target_pairs={{0,8},{8,16},{16,24},{24,0},{1,9},{9,17},{17,25},{25,1},{2,10},{10... | collective-permute-start | bytes 1179656 | tf_op jit(solution)/shard_map/ppermute | solution.py:25
  65.5 19.8 %collective-permute-start.7 = (bf16[768,256]{1,0:T(8,128)(2,1)S(1)}, bf16[768,256]{1,0:T(8,128)(2,1)S(1)}, u32[]{:S(2)}, u32[]{:S(2)}) collective-permute-start(bf16[768,256]{1,0:T(8,128)(2,1)S(1)} %collective-permute-done.6.refs_5_), channel_id=1, source_target_pairs={{0,96},{32,0},{64,32},{96,64},{1,97},{33,1},{65,33},{97,65},{2,98}... | collective-permute-start | bytes 1179656 | tf_op jit(solution)/shard_map/ppermute | solution.py:25
  65.5 19.9 %collective-permute-start.3 = (bf16[768,256]{1,0:T(8,128)(2,1)}, bf16[768,256]{1,0:T(8,128)(2,1)S(1)}, u32[]{:S(2)}, u32[]{:S(2)}) collective-permute-start(bf16[768,256]{1,0:T(8,128)(2,1)} %collective-permute-done.2.refs_4_), channel_id=1, source_target_pairs={{0,32},{32,64},{64,96},{96,0},{1,33},{33,65},{65,97},{97,1},{2,34}... | collective-permute-start | bytes 1179656 | tf_op jit(solution)/shard_map/ppermute | solution.py:25
  67.0 0.9 copy-start.2
  67.9 0.9 copy-start.4
  68.8 0.9 copy-start.6
  89.7 11.3 %collective-permute-start.25 = (bf16[192,512]{1,0:T(8,128)(2,1)S(1)}, bf16[192,512]{1,0:T(8,128)(2,1)S(1)}, u32[]{:S(2)}, u32[]{:S(2)}) collective-permute-start(bf16[192,512]{1,0:T(8,128)(2,1)S(1)} %get-tuple-element.29), channel_id=1, source_target_pairs={{0,4},{2,6},{4,0},{6,2},{1,5},{3,7},{5,1},{7,3},{8,12},{10,14},{12... | collective-permute-start | bytes 589832 | tf_op jit(solution)/shard_map/ppermute | solution.py:25
  89.8 6.9 %collective-permute-start.27 = (bf16[96,512]{1,0:T(8,128)(2,1)S(1)}, bf16[96,512]{1,0:T(8,128)(2,1)S(1)}, u32[]{:S(2)}, u32[]{:S(2)}) collective-permute-start(bf16[96,512]{1,0:T(8,128)(2,1)S(1)} %get-tuple-element.33), channel_id=1, source_target_pairs={{0,6},{2,0},{4,2},{6,4},{1,7},{3,1},{5,3},{7,5},{8,14},{10,8},{12,... | collective-permute-start | bytes 294920 | tf_op jit(solution)/shard_map/ppermute | solution.py:25
  94.2 6.9 %collective-permute-start.28 = (bf16[96,512]{1,0:T(8,128)(2,1)S(1)}, bf16[96,512]{1,0:T(8,128)(2,1)S(1)}, u32[]{:S(2)}, u32[]{:S(2)}) collective-permute-start(bf16[96,512]{1,0:T(8,128)(2,1)S(1)} %get-tuple-element.34), channel_id=1, source_target_pairs={{0,2},{2,4},{4,6},{6,0},{1,3},{3,5},{5,7},{7,1},{8,10},{10,12},{12... | collective-permute-start | bytes 294920 | tf_op jit(solution)/shard_map/ppermute | solution.py:25
  104.5 10.9 %collective-permute-start.29 = (bf16[96,4096]{1,0:T(8,128)(2,1)S(1)}, bf16[96,4096]{1,0:T(8,128)(2,1)S(1)}, u32[]{:S(2)}, u32[]{:S(2)}) collective-permute-start(bf16[96,4096]{1,0:T(8,128)(2,1)S(1)} %project.3), channel_id=1, source_target_pairs={{0,1},{1,0},{2,3},{3,2},{4,5},{5,4},{6,7},{7,6},{8,9},{9,8},{10,11... | collective-permute-start | bytes 2359304 | tf_op jit(solution)/shard_map/ppermute | solution.py:328
  106.6 4.3 %collective-permute-start.24 = (bf16[96,512]{1,0:T(8,128)(2,1)S(1)}, bf16[96,512]{1,0:T(8,128)(2,1)S(1)}, u32[]{:S(2)}, u32[]{:S(2)}) collective-permute-start(bf16[96,512]{1,0:T(8,128)(2,1)S(1)} %get-tuple-element.28), channel_id=1, source_target_pairs={{0,6},{2,0},{4,2},{6,4},{1,7},{3,1},{5,3},{7,5},{8,14},{10,8},{12,... | collective-permute-start | bytes 294920 | tf_op jit(solution)/shard_map/ppermute | solution.py:25
  106.6 5.4 %collective-permute-start.26 = (bf16[96,512]{1,0:T(8,128)(2,1)S(1)}, bf16[96,512]{1,0:T(8,128)(2,1)S(1)}, u32[]{:S(2)}, u32[]{:S(2)}) collective-permute-start(bf16[96,512]{1,0:T(8,128)(2,1)S(1)} %get-tuple-element.30), channel_id=1, source_target_pairs={{0,2},{2,4},{4,6},{6,0},{1,3},{3,5},{5,7},{7,1},{8,10},{10,12},{12... | collective-permute-start | bytes 294920 | tf_op jit(solution)/shard_map/ppermute | solution.py:25

commit v6 on v5

--- a/solution.py
+++ b/solution.py
@@ -16,6 +16,7 @@
 FACTOR = HEAD ** -0.5 * LOG2E
 MAX_TASKS = 160
 TILE = 16
+COPIES = 4
 
 PHASES = (((0, 0), (0, 1)), ((1, 0), (3, 1)), ((1, 1), (3, 0)), ((2, 0), (2, 1)))
 CHUNKS = (256, 256, 256, 256)
@@ -51,8 +52,16 @@
         outs = take(7)
     if first_phase:
         (weight_held,) = take(1)
-        weight_copy = pltpu.make_async_copy(weight, weight_held, refs.pop())
-        weight_copy.start()
+        weight_sem = refs.pop()
+        height = weight.shape[0] // COPIES
+        weight_copies = [
+            pltpu.make_async_copy(
+                weight.at[pl.ds(n * height, height)], weight_held.at[pl.ds(n * height, height)], weight_sem.at[n]
+            )
+            for n in range(COPIES)
+        ]
+        for copy in weight_copies:
+            copy.start()
     kv, low_all, high_all, s0, s1, p0, p1, f0, f1, task_span, task_first, task_upper = refs
     x, z, y, core = coords[0], coords[1], coords[2], coords[3]
 
@@ -178,7 +187,8 @@
     accumulate(2 * pairs, p1, f1)
 
     if first_phase:
-        weight_copy.wait()
+        for copy in weight_copies:
+            copy.wait()
     if last_phase:
         for turn in range(2):
             half = 1 - core if turn == 0 else core
@@ -224,7 +234,7 @@
         pltpu.SMEM((MAX_TASKS,), jnp.int32),
         pltpu.SMEM((MAX_TASKS,), jnp.int32),
         pltpu.SMEM((MAX_TASKS,), jnp.int32),
-    ] + [pltpu.SemaphoreType.DMA] * len(far)
+    ] + [pltpu.SemaphoreType.DMA((COPIES,))] * len(far)
     share = len(pieces) / 16
     return pl.pallas_call(
         lambda *refs: phase_kernel(phase, *refs),
@@ -242,35 +252,48 @@
     )(*scalars, *pieces, *others, *far)
 
 
-def project_kernel(turn, coords, o0, o1, o2, o3, w, out):
+def own_kernel(coords, theirs, ours, w, out):
+    block = 512
+    row = pl.multiple_of(coords[2] * 512, 512)
+    both = jnp.concatenate([theirs[...], ours[...]], axis=0)
+    for n in range(w.shape[1] // block):
+        cols = slice(n * block, (n + 1) * block)
+        out[:, cols] = jnp.dot(both, w[pl.ds(row, 512), cols], preferred_element_type=jnp.float32)
+
+
+def project_kernel(turn, coords, own, o1, o2, o3, w, out):
     y = coords[2]
     block = 512
+    at = slice(turn * SPAN, (turn + 1) * SPAN)
     for n in range(w.shape[1] // block):
         cols = slice(n * block, (n + 1) * block)
         acc = None
-        for s, ref in enumerate((o0, o1, o2, o3)):
+        for s, ref in ((1, o1), (2, o2), (3, o3)):
             row = pl.multiple_of(((y + s) % RING) * 512, 512)
-            rows = ref[turn * SPAN : (turn + 1) * SPAN, :] if s == 2 else ref[...]
+            rows = ref[at, :] if s == 2 else ref[...]
             part = jnp.dot(rows, w[pl.ds(row, 512), cols], preferred_element_type=jnp.float32)
             acc = part if acc is None else acc + part
-        out[:, cols] = acc.astype(out.dtype)
-
-
-def project(turn, coords, o_parts, weight, dtype):
+        out[:, cols] = (acc + own[at, cols]).astype(out.dtype)
+
+
+def dense(kernel, coords, operands, weight, height, dtype):
     smem = pl.BlockSpec(memory_space=pltpu.SMEM)
     vmem = pl.BlockSpec(memory_space=pltpu.VMEM)
     width = weight.shape[1]
     return pl.pallas_call(
-        lambda *refs: project_kernel(turn, *refs),
-        out_shape=jax.ShapeDtypeStruct((SPAN, width), dtype),
-        in_specs=[smem] + [vmem] * 5,
+        kernel,
+        out_shape=jax.ShapeDtypeStruct((height, width), dtype),
+        in_specs=[smem] + [vmem] * (len(operands) + 1),
         out_specs=vmem,
         compiler_params=pltpu.CompilerParams(vmem_limit_bytes=16 * 1024 * 1024),
         cost_estimate=pl.CostEstimate(
             flops=2 * SPAN * 2048 * width, bytes_accessed=2048 * width * 2, transcendentals=0
         ),
-        name="project",
-    )(coords, *o_parts, weight)
+    )(coords, *operands, weight)
+
+
+def project(turn, coords, operands, weight, dtype):
+    return dense(lambda *refs: project_kernel(turn, *refs), coords, operands, weight, SPAN, dtype)
 
 
 def layer(queries, keys, values, span_table, doc_ids, out_weight):
@@ -320,9 +343,10 @@
     o_part = run_phase(3, scalars + [ranks[3]], pieces[3], [q_all, best, acc])[2:]
 
     def returned(part):
-        return [part[0], shift(part[1], "y", -1), both, shift(part[2], "y", 1)]
+        return [own, shift(part[1], "y", -1), both, shift(part[2], "y", 1)]
 
     both = shift(o_part[6], "y", -2)
+    own = dense(own_kernel, coords, [o_part[0], o_part[3]], weight, 2 * SPAN, jnp.float32)
     theirs, ours = returned(o_part[:3]), returned(o_part[3:6])
     sent = project(0, coords, theirs, weight, jnp.bfloat16)
     sent = lax.ppermute(sent, "hd", [(0, 1), (1, 0)])

time: 117 us -> 117 us (level)
  waiting for transfers between devices: 31.8 us -> 30.2 us
    ppermute x29, waiting for transfers between devices: 31.8 us -> 30.2 us  [shift(): lax.ppermute(value, axis, [(i, (i + by) % RING) for i in range(RING)])]
    pallas_call x2 -> x3, Pallas kernels: 6.76 us -> 6.92 us  [dense(): pl.pallas_call(kernel, out_shape=jax.ShapeDtypeStruct((height, width), dt...]
  transfers between devices with their start and end apart: 30 -> 30, of which waited for: 11 -> 11; matrix products, arithmetic and copies ran while one was open for 2% -> 2% of each run, Pallas kernels for 16% -> 17%
where the time goes in v6:
time: 117 us; the launch traced here: 115 us
  starting transfers between devices  47 us (40%)
  waiting for transfers between devices  30.2 us (26%)
  Pallas kernels  27.4 us (23%)
  local copies, waits for them, and re-layouts  6.96 us (6%)
  other arithmetic  3.66 us (3%)
    ppermute x29, starting transfers between devices, shift(): lax.ppermute(value, axis, [(i, (i + by) % RING) for i in range(RING)])  45 us
    ppermute x29, waiting for transfers between devices, shift(): lax.ppermute(value, axis, [(i, (i + by) % RING) for i in range(RING)])  30.2 us
    pallas_call x4, Pallas kernels, run_phase(): pl.pallas_call(lambda *refs: phase_kernel(phase, *refs), out_shape=[jax.S...  20.4 us
    pallas_call x3, Pallas kernels, dense(): pl.pallas_call(kernel, out_shape=jax.ShapeDtypeStruct((height, width), dt...  6.92 us
    unnamed x22, local copies, waits for them, and re-layouts  5.8 us
  transfers between devices with their start and end apart: 30, of which 11 were waited for; matrix products, arithmetic and copies ran while one was open for 2% of the time, Pallas kernels for 17%

profile of v6, /device:TPU:1, one launch (start us, length us, event | category | flops | bytes accessed | tf_op | source)
XLA Modules:
  0.0 115.5 jit_solution(2098824899405883706)
XLA Ops:
  0.0 0.9 copy-done
  1.0 1.0 bitcast_dynamic-update-slice_fusion
  2.0 3.8 %collective-permute-start.8 = (bf16[192,256]{1,0:T(8,128)(2,1)S(1)}, bf16[192,256]{1,0:T(8,128)(2,1)S(1)}, u32[]{:S(2)}, u32[]{:S(2)}) collective-permute-start(bf16[192,256]{1,0:T(8,128)(2,1)S(1)} %get-tuple-element.46), channel_id=1, source_target_pairs={{0,4},{2,6},{4,0},{6,2},{1,5},{3,7},{5,1},{7,3},{8,12},{10,14},{12... | collective-permute-start | bytes 294920 | tf_op jit(solution)/shard_map/ppermute | solution.py:26
  5.8 0.8 collective-permute-start.9
  6.6 0.7 collective-permute-start
  7.9 2.4 %collective-permute-done.9 = bf16[192,256]{1,0:T(8,128)(2,1)S(1)} collective-permute-done((bf16[192,256]{1,0:T(8,128)(2,1)S(1)}, bf16[192,256]{1,0:T(8,128)(2,1)S(1)}, u32[]{:S(2)}, u32[]{:S(2)}) %collective-permute-start.9) | collective-permute-done | bytes 98336 | tf_op jit(solution)/shard_map/ppermute | solution.py:26
  10.3 2.8 %collective-permute-start.13 = (bf16[384,256]{1,0:T(8,128)(2,1)S(1)}, bf16[384,256]{1,0:T(8,128)(2,1)S(1)}, u32[]{:S(2)}, u32[]{:S(2)}) collective-permute-start(bf16[384,256]{1,0:T(8,128)(2,1)S(1)} %get-tuple-element.49), channel_id=1, source_target_pairs={{0,64},{32,96},{64,0},{96,32},{1,65},{33,97},{65,1},{97,33},{2,66}... | collective-permute-start | bytes 589832 | tf_op jit(solution)/shard_map/ppermute | solution.py:26
  13.2 0.9 collective-permute-start.14
  14.1 0.6 collective-permute-start.10
  14.8 3.7 %collective-permute-start.4 = (bf16[384,256]{1,0:T(8,128)(2,1)S(1)}, bf16[384,256]{1,0:T(8,128)(2,1)S(1)}, u32[]{:S(2)}, u32[]{:S(2)}) collective-permute-start(bf16[384,256]{1,0:T(8,128)(2,1)S(1)} %pad_maximum_fusion.1), channel_id=1, source_target_pairs={{0,16},{8,24},{16,0},{24,8},{1,17},{9,25},{17,1},{25,9},{2,18},{10... | collective-permute-start | bytes 589832 | tf_op jit(solution)/shard_map/ppermute | solution.py:26
  18.9 1.0 collective-permute-start.1
  19.9 1.2 %collective-permute-done.14 = bf16[384,256]{1,0:T(8,128)(2,1)S(1)} collective-permute-done((bf16[384,256]{1,0:T(8,128)(2,1)S(1)}, bf16[384,256]{1,0:T(8,128)(2,1)S(1)}, u32[]{:S(2)}, u32[]{:S(2)}) %collective-permute-start.14) | collective-permute-done | bytes 196640 | tf_op jit(solution)/shard_map/ppermute | solution.py:26
  21.2 3.8 %collective-permute-start.15 = (bf16[768,256]{1,0:T(8,128)(2,1)S(1)}, bf16[768,256]{1,0:T(8,128)(2,1)S(1)}, u32[]{:S(2)}, u32[]{:S(2)}) collective-permute-start(bf16[768,256]{1,0:T(8,128)(2,1)S(1)} %constant_dynamic-update-slice_fusion.7.refs_7_), channel_id=1, source_target_pairs={{0,24},{8,0},{16,8},{24,16},{1,25},{9,1},{17,9},{25,17},{2,26},{10... | collective-permute-start | bytes 1179656 | tf_op jit(solution)/shard_map/ppermute | solution.py:26
  25.2 2.8 %collective-permute-start.17 = (bf16[192,512]{1,0:T(8,128)(2,1)S(1)}, bf16[192,512]{1,0:T(8,128)(2,1)S(1)}, u32[]{:S(2)}, u32[]{:S(2)}) collective-permute-start(bf16[192,512]{1,0:T(8,128)(2,1)S(1)} %get-tuple-element.42), channel_id=1, source_target_pairs={{0,2},{2,4},{4,6},{6,0},{1,3},{3,5},{5,7},{7,1},{8,10},{10,12},{12... | collective-permute-start | bytes 589832 | tf_op jit(solution)/shard_map/ppermute | solution.py:26
  28.0 2.6 %collective-permute-start.18 = (bf16[192,512]{1,0:T(8,128)(2,1)S(1)}, bf16[192,512]{1,0:T(8,128)(2,1)S(1)}, u32[]{:S(2)}, u32[]{:S(2)}) collective-permute-start(bf16[192,512]{1,0:T(8,128)(2,1)S(1)} %get-tuple-element.44), channel_id=1, source_target_pairs={{0,4},{2,6},{4,0},{6,2},{1,5},{3,7},{5,1},{7,3},{8,12},{10,14},{12... | collective-permute-start | bytes 589832 | tf_op jit(solution)/shard_map/ppermute | solution.py:26
  30.6 1.3 %collective-permute-start.19 = (bf16[192,512]{1,0:T(8,128)(2,1)S(1)}, bf16[192,512]{1,0:T(8,128)(2,1)S(1)}, u32[]{:S(2)}, u32[]{:S(2)}) collective-permute-start(bf16[192,512]{1,0:T(8,128)(2,1)S(1)} %get-tuple-element.41), channel_id=1, source_target_pairs={{0,6},{2,0},{4,2},{6,4},{1,7},{3,1},{5,3},{7,5},{8,14},{10,8},{12,... | collective-permute-start | bytes 589832 | tf_op jit(solution)/shard_map/ppermute | solution.py:26
  31.9 0.8 collective-permute-done.17.refs_9_
  32.8 0.7 copy-done.1
  33.4 4.1 %collective-permute-done.18.refs_10_ = bf16[192,512]{1,0:T(8,128)(2,1)S(1)} collective-permute-done((bf16[192,512]{1,0:T(8,128)(2,1)S(1)}, bf16[192,512]{1,0:T(8,128)(2,1)S(1)}, u32[]{:S(2)}, u32[]{:S(2)}) %collective-permute-start.18) | collective-permute-done | bytes 196640 | tf_op jit(solution)/shard_map/ppermute | solution.py:26
  37.6 0.7 copy-done.3
  38.2 2.4 %collective-permute-start.23 = (bf16[768,256]{1,0:T(8,128)(2,1)S(1)}, bf16[768,256]{1,0:T(8,128)(2,1)}, u32[]{:S(2)}, u32[]{:S(2)}) collective-permute-start(bf16[768,256]{1,0:T(8,128)(2,1)S(1)} %constant_dynamic-update-slice_fusion.4.refs_6_), channel_id=1, source_target_pairs={{0,24},{8,0},{16,8},{24,16},{1,25},{9,1},{17,9},{25,17},{2,26},{10... | collective-permute-start | bytes 1179656 | tf_op jit(solution)/shard_map/ppermute | solution.py:26
  40.6 0.7 copy-done.5
  41.3 4.8 %collective-permute-start.6 = (bf16[768,256]{1,0:T(8,128)(2,1)S(1)}, bf16[768,256]{1,0:T(8,128)(2,1)S(1)}, u32[]{:S(2)}, u32[]{:S(2)}) collective-permute-start(bf16[768,256]{1,0:T(8,128)(2,1)S(1)} %constant_dynamic-update-slice_fusion.refs_5_), channel_id=1, source_target_pairs={{0,96},{32,0},{64,32},{96,64},{1,97},{33,1},{65,33},{97,65},{2,98}... | collective-permute-start | bytes 1179656 | tf_op jit(solution)/shard_map/ppermute | solution.py:26
  46.8 0.9 convert_reduce_fusion.1
  47.7 1.0 convert_reduce_fusion.refs_2_
  48.7 3.6 %collective-permute-done.6.refs_5_ = bf16[768,256]{1,0:T(8,128)(2,1)S(1)} collective-permute-done((bf16[768,256]{1,0:T(8,128)(2,1)S(1)}, bf16[768,256]{1,0:T(8,128)(2,1)S(1)}, u32[]{:S(2)}, u32[]{:S(2)}) %collective-permute-start.6) | collective-permute-done | bytes 393248 | tf_op jit(solution)/shard_map/ppermute | solution.py:26
  52.3 3.4 %collective-permute-start.21 = (bf16[768,256]{1,0:T(8,128)(2,1)S(1)}, bf16[768,256]{1,0:T(8,128)(2,1)S(1)}, u32[]{:S(2)}, u32[]{:S(2)}) collective-permute-start(bf16[768,256]{1,0:T(8,128)(2,1)S(1)} %pad_maximum_fusion.refs_4_), channel_id=1, source_target_pairs={{0,96},{32,0},{64,32},{96,64},{1,97},{33,1},{65,33},{97,65},{2,98}... | collective-permute-start | bytes 1179656 | tf_op jit(solution)/shard_map/ppermute | solution.py:26
  55.8 8.2 %collective-permute-done.2.refs_4_ = bf16[768,256]{1,0:T(8,128)(2,1)} collective-permute-done((bf16[768,256]{1,0:T(8,128)(2,1)S(1)}, bf16[768,256]{1,0:T(8,128)(2,1)}, u32[]{:S(2)}, u32[]{:S(2)}) %collective-permute-start.2) | collective-permute-done | bytes 393248 | tf_op jit(solution)/shard_map/ppermute | solution.py:26
  64.3 1.2 %collective-permute-start.12 = (bf16[768,256]{1,0:T(8,128)(2,1)S(1)}, bf16[768,256]{1,0:T(8,128)(2,1)S(1)}, u32[]{:S(2)}, u32[]{:S(2)}) collective-permute-start(bf16[768,256]{1,0:T(8,128)(2,1)S(1)} %collective-permute-done.11.refs_6_), channel_id=1, source_target_pairs={{0,8},{8,16},{16,24},{24,0},{1,9},{9,17},{17,25},{25,1},{2,10},{10... | collective-permute-start | bytes 1179656 | tf_op jit(solution)/shard_map/ppermute | solution.py:26
  65.5 1.5 %collective-permute-start.3 = (bf16[768,256]{1,0:T(8,128)(2,1)}, bf16[768,256]{1,0:T(8,128)(2,1)S(1)}, u32[]{:S(2)}, u32[]{:S(2)}) collective-permute-start(bf16[768,256]{1,0:T(8,128)(2,1)} %collective-permute-done.2.refs_4_), channel_id=1, source_target_pairs={{0,32},{32,64},{64,96},{96,0},{1,33},{33,65},{65,97},{97,1},{2,34}... | collective-permute-start | bytes 1179656 | tf_op jit(solution)/shard_map/ppermute | solution.py:26
  67.0 0.9 copy-done.2
  67.9 0.9 copy-done.4
  68.8 0.9 copy-done.6
  69.7 6.6 %shard_map.64 = (bf16[8,384,256]{2,1,0:T(8,128)(2,1)S(1)}, f32[8,384,128]{2,1,0:T(8,128)S(1)}, f32[8,384,256]{2,1,0:T(8,128)S(1)}, bf16[2048,4096]{1,0:T(8,128)(2,1)S(1)}) custom-call(s32[4]{0:T(128)S(1)} %pad_add_fusion.refs_0_.coords, s32[128]{0:T(128)S(1)} %copy-done.7, s32[8]{0:T(128)S(1)} %convert_reduce_fusion.refs_2_, ...), custom_call_target="tpu_custom_call" | custom-call | flops 2000000000 | bytes 2500000 | tf_op jit(solution)/shard_map/pallas_call | solution.py:239
  76.3 4.5 %shard_map.65 = (f32[8,384,128]{2,1,0:T(8,128)S(1)}, f32[8,384,256]{2,1,0:T(8,128)S(1)}) custom-call(s32[4]{0:T(128)S(1)} %pad_add_fusion.refs_0_.coords, s32[128]{0:T(128)S(1)} %copy-done.7, s32[8]{0:T(128)S(1)} %convert_reduce_fusion.refs_2_, s32[136]{0:T(256)S(1)} %get-tuple-element.35.refs_3_, ...), custom_call_target="tpu_custom_call", output_to_operand_aliasing={{0}: (9, {}), {1}: (10, {})} | custom-call | flops 2000000000 | bytes 2500000 | tf_op jit(solution)/shard_map/pallas_call | solution.py:239
  80.8 4.9 %shard_map.66 = (f32[8,384,128]{2,1,0:T(8,128)S(1)}, f32[8,384,256]{2,1,0:T(8,128)S(1)}) custom-call(s32[4]{0:T(128)S(1)} %pad_add_fusion.refs_0_.coords, s32[128]{0:T(128)S(1)} %copy-done.7, s32[8]{0:T(128)S(1)} %convert_reduce_fusion.refs_2_, s32[136]{0:T(256)S(1)} %get-tuple-element.36.refs_3_, ...), custom_call_target="tpu_custom_call", output_to_operand_aliasing={{0}: (9, {}), {1}: (10, {})} | custom-call | flops 2000000000 | bytes 2500000 | tf_op jit(solution)/shard_map/pallas_call | solution.py:239
  85.7 4.5 %shard_map.67 = (f32[8,384,128]{2,1,0:T(8,128)S(1)}, f32[8,384,256]{2,1,0:T(8,128)S(1)}, bf16[96,512]{1,0:T(8,128)(2,1)S(1)}, bf16[96,512]{1,0:T(8,128)(2,1)S(1)...) custom-call(s32[4]{0:T(128)S(1)} %pad_add_fusion.refs_0_.coords, ...), custom_call_target="tpu_custom_call", output_to_operand_aliasing={{0}: (9, {}), {1}: (10, {})} | custom-call | flops 2000000000 | bytes 2500000 | tf_op jit(solution)/shard_map/pallas_call | solution.py:239
  90.3 4.4 %collective-permute-start.27 = (bf16[96,512]{1,0:T(8,128)(2,1)S(1)}, bf16[96,512]{1,0:T(8,128)(2,1)S(1)}, u32[]{:S(2)}, u32[]{:S(2)}) collective-permute-start(bf16[96,512]{1,0:T(8,128)(2,1)S(1)} %get-tuple-element.33), channel_id=1, source_target_pairs={{0,6},{2,0},{4,2},{6,4},{1,7},{3,1},{5,3},{7,5},{8,14},{10,8},{12,... | collective-permute-start | bytes 294920 | tf_op jit(solution)/shard_map/ppermute | solution.py:26
  94.7 1.6 %shard_map.68.refs_1_ = f32[192,4096]{1,0:T(8,128)S(1)} custom-call(s32[4]{0:T(128)S(1)} %pad_add_fusion.refs_0_.coords, bf16[96,512]{1,0:T(8,128)(2,1)S(1)} %get-tuple-element.27.theirs, bf16[96,512]{1,0:T(8,128)(2,1)S(1)} %get-tuple-element.28.ours, bf16[2048,4096]{1,0:T(8,128)(2,1)S(1)} %get-tuple-element.29.w.refs_5_), custom_call_target="tpu_custom_call" | custom-call | flops 1610612736 | bytes 16777216 | tf_op jit(solution)/shard_map/pallas_call | solution.py:283
  96.3 0.9 collective-permute-done.27.refs_2_
  97.2 4.4 %collective-permute-done.28.refs_4_ = bf16[96,512]{1,0:T(8,128)(2,1)S(1)} collective-permute-done((bf16[96,512]{1,0:T(8,128)(2,1)S(1)}, bf16[96,512]{1,0:T(8,128)(2,1)S(1)}, u32[]{:S(2)}, u32[]{:S(2)}) %collective-permute-start.28) | collective-permute-done | bytes 98336 | tf_op jit(solution)/shard_map/ppermute | solution.py:26
  101.6 2.7 %shard_map.70 = bf16[96,4096]{1,0:T(8,128)(2,1)S(1)} custom-call(s32[4]{0:T(128)S(1)} %pad_add_fusion.refs_0_.coords, f32[192,4096]{1,0:T(8,128)S(1)} %shard_map.68.refs_1_, bf16[96,512]{1,0:T(8,128)(2,1)S(1)} %collective-permute-done.27.refs_2_, bf16[192,512]{1,0:T(8,128)(2,1)S(1)} %collective-permute-done.25.refs_3_, ...), custom_call_target="tpu_custom_call" | custom-call | flops 1610612736 | bytes 16777216 | tf_op jit(solution)/shard_map/pallas_call | solution.py:283
  104.3 2.0 %collective-permute-start.29 = (bf16[96,4096]{1,0:T(8,128)(2,1)S(1)}, bf16[96,4096]{1,0:T(8,128)(2,1)S(1)}, u32[]{:S(2)}, u32[]{:S(2)}) collective-permute-start(bf16[96,4096]{1,0:T(8,128)(2,1)S(1)} %shard_map.70), channel_id=1, source_target_pairs={{0,1},{1,0},{2,3},{3,2},{4,5},{5,4},{6,7},{7,6},{8,9},{9,8},{10,11... | collective-permute-start | bytes 2359304 | tf_op jit(solution)/shard_map/ppermute | solution.py:352
  106.3 1.5 %collective-permute-start.26 = (bf16[96,512]{1,0:T(8,128)(2,1)S(1)}, bf16[96,512]{1,0:T(8,128)(2,1)S(1)}, u32[]{:S(2)}, u32[]{:S(2)}) collective-permute-start(bf16[96,512]{1,0:T(8,128)(2,1)S(1)} %get-tuple-element.32), channel_id=1, source_target_pairs={{0,2},{2,4},{4,6},{6,0},{1,3},{3,5},{5,7},{7,1},{8,10},{10,12},{12... | collective-permute-start | bytes 294920 | tf_op jit(solution)/shard_map/ppermute | solution.py:26
  107.8 2.8 %collective-permute-done.24.refs_2_ = bf16[96,512]{1,0:T(8,128)(2,1)S(1)} collective-permute-done((bf16[96,512]{1,0:T(8,128)(2,1)S(1)}, bf16[96,512]{1,0:T(8,128)(2,1)S(1)}, u32[]{:S(2)}, u32[]{:S(2)}) %collective-permute-start.24) | collective-permute-done | bytes 98336 | tf_op jit(solution)/shard_map/ppermute | solution.py:26
  110.6 1.1 collective-permute-done.26.refs_4_
  111.7 2.7 %shard_map.69 = f32[96,4096]{1,0:T(8,128)S(1)} custom-call(s32[4]{0:T(128)S(1)} %pad_add_fusion.refs_0_.coords, f32[192,4096]{1,0:T(8,128)S(1)} %shard_map.68.refs_1_, bf16[96,512]{1,0:T(8,128)(2,1)S(1)} %collective-permute-done.24.refs_2_, bf16[192,512]{1,0:T(8,128)(2,1)S(1)} %collective-permute-done.25.refs_3_, ...), custom_call_target="tpu_custom_call" | custom-call | flops 1610612736 | bytes 16777216 | tf_op jit(solution)/shard_map/pallas_call | solution.py:283
  114.4 1.0 add_convert_fusion
  (56 shorter events, 2.7 us)
Async XLA Ops:
  0.0 0.9 copy-start
  0.0 13.1 %copy-start.8 = (bf16[192,2048]{1,0:T(8,128)(2,1)S(1)}, bf16[192,2048]{1,0:T(8,128)(2,1)}, u32[]{:S(2)}) copy-start(bf16[192,2048]{1,0:T(8,128)(2,1)} %param.6) | copy-start | bytes 2359300
  2.0 5.8 %collective-permute-start.8 = (bf16[192,256]{1,0:T(8,128)(2,1)S(1)}, bf16[192,256]{1,0:T(8,128)(2,1)S(1)}, u32[]{:S(2)}, u32[]{:S(2)}) collective-permute-start(bf16[192,256]{1,0:T(8,128)(2,1)S(1)} %get-tuple-element.46), channel_id=1, source_target_pairs={{0,4},{2,6},{4,0},{6,2},{1,5},{3,7},{5,1},{7,3},{8,12},{10,14},{12... | collective-permute-start | bytes 294920 | tf_op jit(solution)/shard_map/ppermute | solution.py:26
  5.8 4.4 %collective-permute-start.9 = (bf16[192,256]{1,0:T(8,128)(2,1)S(1)}, bf16[192,256]{1,0:T(8,128)(2,1)S(1)}, u32[]{:S(2)}, u32[]{:S(2)}) collective-permute-start(bf16[192,256]{1,0:T(8,128)(2,1)S(1)} %get-tuple-element.45), channel_id=1, source_target_pairs={{0,6},{2,0},{4,2},{6,4},{1,7},{3,1},{5,3},{7,5},{8,14},{10,8},{12,... | collective-permute-start | bytes 294920 | tf_op jit(solution)/shard_map/ppermute | solution.py:26
  6.6 8.1 %collective-permute-start = (bf16[192,256]{1,0:T(8,128)(2,1)S(1)}, bf16[192,256]{1,0:T(8,128)(2,1)S(1)}, u32[]{:S(2)}, u32[]{:S(2)}) collective-permute-start(bf16[192,256]{1,0:T(8,128)(2,1)S(1)} %get-tuple-element.47), channel_id=1, source_target_pairs={{0,2},{2,4},{4,6},{6,0},{1,3},{3,5},{5,7},{7,1},{8,10},{10,12},{12... | collective-permute-start | bytes 294920 | tf_op jit(solution)/shard_map/ppermute | solution.py:26
  10.3 8.6 %collective-permute-start.13 = (bf16[384,256]{1,0:T(8,128)(2,1)S(1)}, bf16[384,256]{1,0:T(8,128)(2,1)S(1)}, u32[]{:S(2)}, u32[]{:S(2)}) collective-permute-start(bf16[384,256]{1,0:T(8,128)(2,1)S(1)} %get-tuple-element.49), channel_id=1, source_target_pairs={{0,64},{32,96},{64,0},{96,32},{1,65},{33,97},{65,1},{97,33},{2,66}... | collective-permute-start | bytes 589832 | tf_op jit(solution)/shard_map/ppermute | solution.py:26
  13.2 7.9 %collective-permute-start.14 = (bf16[384,256]{1,0:T(8,128)(2,1)S(1)}, bf16[384,256]{1,0:T(8,128)(2,1)S(1)}, u32[]{:S(2)}, u32[]{:S(2)}) collective-permute-start(bf16[384,256]{1,0:T(8,128)(2,1)S(1)} %get-tuple-element.49), channel_id=1, source_target_pairs={{0,96},{32,0},{64,32},{96,64},{1,97},{33,1},{65,33},{97,65},{2,98}... | collective-permute-start | bytes 589832 | tf_op jit(solution)/shard_map/ppermute | solution.py:26
  14.1 10.9 %collective-permute-start.10 = (bf16[384,256]{1,0:T(8,128)(2,1)S(1)}, bf16[384,256]{1,0:T(8,128)(2,1)S(1)}, u32[]{:S(2)}, u32[]{:S(2)}) collective-permute-start(bf16[384,256]{1,0:T(8,128)(2,1)S(1)} %get-tuple-element.49), channel_id=1, source_target_pairs={{0,32},{32,64},{64,96},{96,0},{1,33},{33,65},{65,97},{97,1},{2,34}... | collective-permute-start | bytes 589832 | tf_op jit(solution)/shard_map/ppermute | solution.py:26
  14.8 32.1 %copy-start.7 = (s32[128]{0:T(128)S(1)}, s32[128]{0:T(128)}, u32[]{:S(2)}) copy-start(s32[128]{0:T(128)} %refs_1_.7) | copy-start | bytes 1540
  14.8 10.4 %collective-permute-start.4 = (bf16[384,256]{1,0:T(8,128)(2,1)S(1)}, bf16[384,256]{1,0:T(8,128)(2,1)S(1)}, u32[]{:S(2)}, u32[]{:S(2)}) collective-permute-start(bf16[384,256]{1,0:T(8,128)(2,1)S(1)} %pad_maximum_fusion.1), channel_id=1, source_target_pairs={{0,16},{8,24},{16,0},{24,8},{1,17},{9,25},{17,1},{25,9},{2,18},{10... | collective-permute-start | bytes 589832 | tf_op jit(solution)/shard_map/ppermute | solution.py:26
  18.5 9.5 %collective-permute-start.5 = (bf16[384,256]{1,0:T(8,128)(2,1)S(1)}, bf16[384,256]{1,0:T(8,128)(2,1)S(1)}, u32[]{:S(2)}, u32[]{:S(2)}) collective-permute-start(bf16[384,256]{1,0:T(8,128)(2,1)S(1)} %pad_maximum_fusion.1), channel_id=1, source_target_pairs={{0,24},{8,0},{16,8},{24,16},{1,25},{9,1},{17,9},{25,17},{2,26},{10... | collective-permute-start | bytes 589832 | tf_op jit(solution)/shard_map/ppermute | solution.py:26
  18.9 11.7 %collective-permute-start.1 = (bf16[384,256]{1,0:T(8,128)(2,1)S(1)}, bf16[384,256]{1,0:T(8,128)(2,1)S(1)}, u32[]{:S(2)}, u32[]{:S(2)}) collective-permute-start(bf16[384,256]{1,0:T(8,128)(2,1)S(1)} %pad_maximum_fusion.1), channel_id=1, source_target_pairs={{0,8},{8,16},{16,24},{24,0},{1,9},{9,17},{17,25},{25,1},{2,10},{10... | collective-permute-start | bytes 589832 | tf_op jit(solution)/shard_map/ppermute | solution.py:26
  21.2 24.9 %collective-permute-start.15 = (bf16[768,256]{1,0:T(8,128)(2,1)S(1)}, bf16[768,256]{1,0:T(8,128)(2,1)S(1)}, u32[]{:S(2)}, u32[]{:S(2)}) collective-permute-start(bf16[768,256]{1,0:T(8,128)(2,1)S(1)} %constant_dynamic-update-slice_fusion.7.refs_7_), channel_id=1, source_target_pairs={{0,24},{8,0},{16,8},{24,16},{1,25},{9,1},{17,9},{25,17},{2,26},{10... | collective-permute-start | bytes 1179656 | tf_op jit(solution)/shard_map/ppermute | solution.py:26
  25.0 21.0 %collective-permute-start.11 = (bf16[768,256]{1,0:T(8,128)(2,1)S(1)}, bf16[768,256]{1,0:T(8,128)(2,1)S(1)}, u32[]{:S(2)}, u32[]{:S(2)}) collective-permute-start(bf16[768,256]{1,0:T(8,128)(2,1)S(1)} %constant_dynamic-update-slice_fusion.4.refs_6_), channel_id=1, source_target_pairs={{0,8},{8,16},{16,24},{24,0},{1,9},{9,17},{17,25},{25,1},{2,10},{10... | collective-permute-start | bytes 1179656 | tf_op jit(solution)/shard_map/ppermute | solution.py:26
  25.2 7.6 %collective-permute-start.17 = (bf16[192,512]{1,0:T(8,128)(2,1)S(1)}, bf16[192,512]{1,0:T(8,128)(2,1)S(1)}, u32[]{:S(2)}, u32[]{:S(2)}) collective-permute-start(bf16[192,512]{1,0:T(8,128)(2,1)S(1)} %get-tuple-element.42), channel_id=1, source_target_pairs={{0,2},{2,4},{4,6},{6,0},{1,3},{3,5},{5,7},{7,1},{8,10},{10,12},{12... | collective-permute-start | bytes 589832 | tf_op jit(solution)/shard_map/ppermute | solution.py:26
  28.0 9.6 %collective-permute-start.18 = (bf16[192,512]{1,0:T(8,128)(2,1)S(1)}, bf16[192,512]{1,0:T(8,128)(2,1)S(1)}, u32[]{:S(2)}, u32[]{:S(2)}) collective-permute-start(bf16[192,512]{1,0:T(8,128)(2,1)S(1)} %get-tuple-element.44), channel_id=1, source_target_pairs={{0,4},{2,6},{4,0},{6,2},{1,5},{3,7},{5,1},{7,3},{8,12},{10,14},{12... | collective-permute-start | bytes 589832 | tf_op jit(solution)/shard_map/ppermute | solution.py:26
  30.6 10.0 %collective-permute-start.19 = (bf16[192,512]{1,0:T(8,128)(2,1)S(1)}, bf16[192,512]{1,0:T(8,128)(2,1)S(1)}, u32[]{:S(2)}, u32[]{:S(2)}) collective-permute-start(bf16[192,512]{1,0:T(8,128)(2,1)S(1)} %get-tuple-element.41), channel_id=1, source_target_pairs={{0,6},{2,0},{4,2},{6,4},{1,7},{3,1},{5,3},{7,5},{8,14},{10,8},{12,... | collective-permute-start | bytes 589832 | tf_op jit(solution)/shard_map/ppermute | solution.py:26
  32.8 0.7 copy-start.1
  33.4 30.9 %collective-permute-start.22 = (bf16[768,256]{1,0:T(8,128)(2,1)S(1)}, bf16[768,256]{1,0:T(8,128)(2,1)S(1)}, u32[]{:S(2)}, u32[]{:S(2)}) collective-permute-start(bf16[768,256]{1,0:T(8,128)(2,1)S(1)} %constant_dynamic-update-slice_fusion.7.refs_7_), channel_id=1, source_target_pairs={{0,8},{8,16},{16,24},{24,0},{1,9},{9,17},{17,25},{25,1},{2,10},{10... | collective-permute-start | bytes 1179656 | tf_op jit(solution)/shard_map/ppermute | solution.py:26
  37.6 0.7 copy-start.3
  38.2 27.2 %collective-permute-start.23 = (bf16[768,256]{1,0:T(8,128)(2,1)S(1)}, bf16[768,256]{1,0:T(8,128)(2,1)}, u32[]{:S(2)}, u32[]{:S(2)}) collective-permute-start(bf16[768,256]{1,0:T(8,128)(2,1)S(1)} %constant_dynamic-update-slice_fusion.4.refs_6_), channel_id=1, source_target_pairs={{0,24},{8,0},{16,8},{24,16},{1,25},{9,1},{17,9},{25,17},{2,26},{10... | collective-permute-start | bytes 1179656 | tf_op jit(solution)/shard_map/ppermute | solution.py:26
  40.6 0.7 copy-start.5
  41.3 11.1 %collective-permute-start.6 = (bf16[768,256]{1,0:T(8,128)(2,1)S(1)}, bf16[768,256]{1,0:T(8,128)(2,1)S(1)}, u32[]{:S(2)}, u32[]{:S(2)}) collective-permute-start(bf16[768,256]{1,0:T(8,128)(2,1)S(1)} %constant_dynamic-update-slice_fusion.refs_5_), channel_id=1, source_target_pairs={{0,96},{32,0},{64,32},{96,64},{1,97},{33,1},{65,33},{97,65},{2,98}... | collective-permute-start | bytes 1179656 | tf_op jit(solution)/shard_map/ppermute | solution.py:26
  46.1 19.4 %collective-permute-start.20 = (bf16[768,256]{1,0:T(8,128)(2,1)S(1)}, bf16[768,256]{1,0:T(8,128)(2,1)}, u32[]{:S(2)}, u32[]{:S(2)}) collective-permute-start(bf16[768,256]{1,0:T(8,128)(2,1)S(1)} %constant_dynamic-update-slice_fusion.refs_5_), channel_id=1, source_target_pairs={{0,32},{32,64},{64,96},{96,0},{1,33},{33,65},{65,97},{97,1},{2,34}... | collective-permute-start | bytes 1179656 | tf_op jit(solution)/shard_map/ppermute | solution.py:26
  46.1 17.9 %collective-permute-start.2 = (bf16[768,256]{1,0:T(8,128)(2,1)S(1)}, bf16[768,256]{1,0:T(8,128)(2,1)}, u32[]{:S(2)}, u32[]{:S(2)}) collective-permute-start(bf16[768,256]{1,0:T(8,128)(2,1)S(1)} %pad_maximum_fusion.refs_4_), channel_id=1, source_target_pairs={{0,32},{32,64},{64,96},{96,0},{1,33},{33,65},{65,97},{97,1},{2,34}... | collective-permute-start | bytes 1179656 | tf_op jit(solution)/shard_map/ppermute | solution.py:26
  52.3 28.5 %collective-permute-start.21 = (bf16[768,256]{1,0:T(8,128)(2,1)S(1)}, bf16[768,256]{1,0:T(8,128)(2,1)S(1)}, u32[]{:S(2)}, u32[]{:S(2)}) collective-permute-start(bf16[768,256]{1,0:T(8,128)(2,1)S(1)} %pad_maximum_fusion.refs_4_), channel_id=1, source_target_pairs={{0,96},{32,0},{64,32},{96,64},{1,97},{33,1},{65,33},{97,65},{2,98}... | collective-permute-start | bytes 1179656 | tf_op jit(solution)/shard_map/ppermute | solution.py:26
  64.0 21.7 %collective-permute-start.16 = (bf16[768,256]{1,0:T(8,128)(2,1)S(1)}, bf16[768,256]{1,0:T(8,128)(2,1)S(1)}, u32[]{:S(2)}, u32[]{:S(2)}) collective-permute-start(bf16[768,256]{1,0:T(8,128)(2,1)S(1)} %collective-permute-done.15.refs_7_), channel_id=1, source_target_pairs={{0,24},{8,0},{16,8},{24,16},{1,25},{9,1},{17,9},{25,17},{2,26},{10... | collective-permute-start | bytes 1179656 | tf_op jit(solution)/shard_map/ppermute | solution.py:26
  64.3 21.4 %collective-permute-start.12 = (bf16[768,256]{1,0:T(8,128)(2,1)S(1)}, bf16[768,256]{1,0:T(8,128)(2,1)S(1)}, u32[]{:S(2)}, u32[]{:S(2)}) collective-permute-start(bf16[768,256]{1,0:T(8,128)(2,1)S(1)} %collective-permute-done.11.refs_6_), channel_id=1, source_target_pairs={{0,8},{8,16},{16,24},{24,0},{1,9},{9,17},{17,25},{25,1},{2,10},{10... | collective-permute-start | bytes 1179656 | tf_op jit(solution)/shard_map/ppermute | solution.py:26
  65.5 20.2 %collective-permute-start.7 = (bf16[768,256]{1,0:T(8,128)(2,1)S(1)}, bf16[768,256]{1,0:T(8,128)(2,1)S(1)}, u32[]{:S(2)}, u32[]{:S(2)}) collective-permute-start(bf16[768,256]{1,0:T(8,128)(2,1)S(1)} %collective-permute-done.6.refs_5_), channel_id=1, source_target_pairs={{0,96},{32,0},{64,32},{96,64},{1,97},{33,1},{65,33},{97,65},{2,98}... | collective-permute-start | bytes 1179656 | tf_op jit(solution)/shard_map/ppermute | solution.py:26
  65.5 20.2 %collective-permute-start.3 = (bf16[768,256]{1,0:T(8,128)(2,1)}, bf16[768,256]{1,0:T(8,128)(2,1)S(1)}, u32[]{:S(2)}, u32[]{:S(2)}) collective-permute-start(bf16[768,256]{1,0:T(8,128)(2,1)} %collective-permute-done.2.refs_4_), channel_id=1, source_target_pairs={{0,32},{32,64},{64,96},{96,0},{1,33},{33,65},{65,97},{97,1},{2,34}... | collective-permute-start | bytes 1179656 | tf_op jit(solution)/shard_map/ppermute | solution.py:26
  67.0 0.9 copy-start.2
  67.9 0.9 copy-start.4
  68.8 0.9 copy-start.6
  90.2 11.4 %collective-permute-start.25 = (bf16[192,512]{1,0:T(8,128)(2,1)S(1)}, bf16[192,512]{1,0:T(8,128)(2,1)S(1)}, u32[]{:S(2)}, u32[]{:S(2)}) collective-permute-start(bf16[192,512]{1,0:T(8,128)(2,1)S(1)} %get-tuple-element.31), channel_id=1, source_target_pairs={{0,4},{2,6},{4,0},{6,2},{1,5},{3,7},{5,1},{7,3},{8,12},{10,14},{12... | collective-permute-start | bytes 589832 | tf_op jit(solution)/shard_map/ppermute | solution.py:26
  90.3 6.8 %collective-permute-start.27 = (bf16[96,512]{1,0:T(8,128)(2,1)S(1)}, bf16[96,512]{1,0:T(8,128)(2,1)S(1)}, u32[]{:S(2)}, u32[]{:S(2)}) collective-permute-start(bf16[96,512]{1,0:T(8,128)(2,1)S(1)} %get-tuple-element.33), channel_id=1, source_target_pairs={{0,6},{2,0},{4,2},{6,4},{1,7},{3,1},{5,3},{7,5},{8,14},{10,8},{12,... | collective-permute-start | bytes 294920 | tf_op jit(solution)/shard_map/ppermute | solution.py:26
  94.7 6.9 %collective-permute-start.28 = (bf16[96,512]{1,0:T(8,128)(2,1)S(1)}, bf16[96,512]{1,0:T(8,128)(2,1)S(1)}, u32[]{:S(2)}, u32[]{:S(2)}) collective-permute-start(bf16[96,512]{1,0:T(8,128)(2,1)S(1)} %get-tuple-element.34), channel_id=1, source_target_pairs={{0,2},{2,4},{4,6},{6,0},{1,3},{3,5},{5,7},{7,1},{8,10},{10,12},{12... | collective-permute-start | bytes 294920 | tf_op jit(solution)/shard_map/ppermute | solution.py:26
  104.3 10.1 %collective-permute-start.29 = (bf16[96,4096]{1,0:T(8,128)(2,1)S(1)}, bf16[96,4096]{1,0:T(8,128)(2,1)S(1)}, u32[]{:S(2)}, u32[]{:S(2)}) collective-permute-start(bf16[96,4096]{1,0:T(8,128)(2,1)S(1)} %shard_map.70), channel_id=1, source_target_pairs={{0,1},{1,0},{2,3},{3,2},{4,5},{5,4},{6,7},{7,6},{8,9},{9,8},{10,11... | collective-permute-start | bytes 2359304 | tf_op jit(solution)/shard_map/ppermute | solution.py:352
  106.3 4.3 %collective-permute-start.24 = (bf16[96,512]{1,0:T(8,128)(2,1)S(1)}, bf16[96,512]{1,0:T(8,128)(2,1)S(1)}, u32[]{:S(2)}, u32[]{:S(2)}) collective-permute-start(bf16[96,512]{1,0:T(8,128)(2,1)S(1)} %get-tuple-element.30), channel_id=1, source_target_pairs={{0,6},{2,0},{4,2},{6,4},{1,7},{3,1},{5,3},{7,5},{8,14},{10,8},{12,... | collective-permute-start | bytes 294920 | tf_op jit(solution)/shard_map/ppermute | solution.py:26
  106.3 5.4 %collective-permute-start.26 = (bf16[96,512]{1,0:T(8,128)(2,1)S(1)}, bf16[96,512]{1,0:T(8,128)(2,1)S(1)}, u32[]{:S(2)}, u32[]{:S(2)}) collective-permute-start(bf16[96,512]{1,0:T(8,128)(2,1)S(1)} %get-tuple-element.32), channel_id=1, source_target_pairs={{0,2},{2,4},{4,6},{6,0},{1,3},{3,5},{5,7},{7,1},{8,10},{10,12},{12... | collective-permute-start | bytes 294920 | tf_op jit(solution)/shard_map/ppermute | solution.py:26

commit v7 on v6

--- a/solution.py
+++ b/solution.py
@@ -17,6 +17,7 @@
 MAX_TASKS = 160
 TILE = 16
 COPIES = 4
+UNROLL = 4
 
 PHASES = (((0, 0), (0, 1)), ((1, 0), (3, 1)), ((1, 1), (3, 0)), ((2, 0), (2, 1)))
 CHUNKS = (256, 256, 256, 256)
@@ -120,7 +121,7 @@
     total = lax.fori_loop(0, 8, plan, 1)
     task_span[0] = 0
     task_first[0] = 0
-    for extra in range(3):
+    for extra in range(UNROLL + 1):
         task_span[total + extra] = 0
         task_first[total + extra] = 0
         task_upper[total + extra] = 0
@@ -172,19 +173,20 @@
 
     score(1, s0)
 
-    def pair(j, _):
-        t = 2 * j + 1
-        accumulate(t - 1, p1, f1)
-        score(t + 1, s1)
-        weigh(t, s0, p0, f0)
-        accumulate(t, p0, f0)
-        score(t + 2, s0)
-        weigh(t + 1, s1, p1, f1)
+    def several(j, _):
+        for u in range(0, UNROLL, 2):
+            t = UNROLL * j + 1 + u
+            accumulate(t - 1, p1, f1)
+            score(t + 1, s1)
+            weigh(t, s0, p0, f0)
+            accumulate(t, p0, f0)
+            score(t + 2, s0)
+            weigh(t + 1, s1, p1, f1)
         return 0
 
-    pairs = total // 2
-    lax.fori_loop(0, pairs, pair, 0)
-    accumulate(2 * pairs, p1, f1)
+    rounds = (total - 1 + UNROLL - 1) // UNROLL
+    lax.fori_loop(0, rounds, several, 0)
+    accumulate(UNROLL * rounds, p1, f1)
 
     if first_phase:
         for copy in weight_copies:
@@ -297,10 +299,10 @@
 
 
 def layer(queries, keys, values, span_table, doc_ids, out_weight):
-    rows = queries.shape[0]
     spans = span_table.shape[0]
     x, z, y, core = (lax.axis_index(a) for a in ("x", "z", "y", "hd"))
     coords = jnp.stack([x, z, y, core]).astype(jnp.int32)
+    rows = queries.shape[0]
     kv = jnp.concatenate([keys.reshape(rows, RING, HEAD), values.reshape(rows, RING, HEAD)], axis=2)
     kv = kv.transpose(1, 0, 2)
     part = [lax.dynamic_index_in_dim(kv, (y + s) % RING, 0, keepdims=False) for s in range(RING)]

time: 117 us -> 116 us (level)
  waiting for transfers between devices: 30.2 us -> 28 us
  starting transfers between devices: 47 us -> 48.9 us
    ppermute x29, waiting for transfers between devices: 30.2 us -> 28 us  [shift(): lax.ppermute(value, axis, [(i, (i + by) % RING) for i in range(RING)])]
    ppermute x1, starting transfers between devices: 2.04 us -> 4.25 us  [layer(): sent = lax.ppermute(sent, 'hd', [(0, 1), (1, 0)])]
where the time goes in v7:
time: 116 us; the launch traced here: 114 us
  starting transfers between devices  48.9 us (42%)
  waiting for transfers between devices  28 us (24%)
  Pallas kernels  26.6 us (23%)
  local copies, waits for them, and re-layouts  6.96 us (6%)
  other arithmetic  3.66 us (3%)
    ppermute x29, starting transfers between devices, shift(): lax.ppermute(value, axis, [(i, (i + by) % RING) for i in range(RING)])  44.7 us
    ppermute x29, waiting for transfers between devices, shift(): lax.ppermute(value, axis, [(i, (i + by) % RING) for i in range(RING)])  28 us
    pallas_call x4, Pallas kernels, run_phase(): pl.pallas_call(lambda *refs: phase_kernel(phase, *refs), out_shape=[jax.S...  19.7 us
    pallas_call x3, Pallas kernels, dense(): pl.pallas_call(kernel, out_shape=jax.ShapeDtypeStruct((height, width), dt...  6.92 us
    unnamed x22, local copies, waits for them, and re-layouts  5.8 us
    ppermute x1, starting transfers between devices, layer(): sent = lax.ppermute(sent, 'hd', [(0, 1), (1, 0)])  4.25 us
  transfers between devices with their start and end apart: 30, of which 11 were waited for; matrix products, arithmetic and copies ran while one was open for 2% of the time, Pallas kernels for 17%

profile of v7, /device:TPU:1, one launch (start us, length us, event | category | flops | bytes accessed | tf_op | source)
XLA Modules:
  0.0 114.4 jit_solution(14007073457825775850)
XLA Ops:
  0.0 0.9 copy-done
  1.0 1.0 bitcast_dynamic-update-slice_fusion
  2.0 3.8 %collective-permute-start.8 = (bf16[192,256]{1,0:T(8,128)(2,1)S(1)}, bf16[192,256]{1,0:T(8,128)(2,1)S(1)}, u32[]{:S(2)}, u32[]{:S(2)}) collective-permute-start(bf16[192,256]{1,0:T(8,128)(2,1)S(1)} %get-tuple-element.46), channel_id=1, source_target_pairs={{0,4},{2,6},{4,0},{6,2},{1,5},{3,7},{5,1},{7,3},{8,12},{10,14},{12... | collective-permute-start | bytes 294920 | tf_op jit(solution)/shard_map/ppermute | solution.py:27
  5.8 0.8 collective-permute-start.9
  6.6 0.7 collective-permute-start
  7.9 2.4 %collective-permute-done.9 = bf16[192,256]{1,0:T(8,128)(2,1)S(1)} collective-permute-done((bf16[192,256]{1,0:T(8,128)(2,1)S(1)}, bf16[192,256]{1,0:T(8,128)(2,1)S(1)}, u32[]{:S(2)}, u32[]{:S(2)}) %collective-permute-start.9) | collective-permute-done | bytes 98336 | tf_op jit(solution)/shard_map/ppermute | solution.py:27
  10.3 2.8 %collective-permute-start.13 = (bf16[384,256]{1,0:T(8,128)(2,1)S(1)}, bf16[384,256]{1,0:T(8,128)(2,1)S(1)}, u32[]{:S(2)}, u32[]{:S(2)}) collective-permute-start(bf16[384,256]{1,0:T(8,128)(2,1)S(1)} %get-tuple-element.49), channel_id=1, source_target_pairs={{0,64},{32,96},{64,0},{96,32},{1,65},{33,97},{65,1},{97,33},{2,66}... | collective-permute-start | bytes 589832 | tf_op jit(solution)/shard_map/ppermute | solution.py:27
  13.2 0.9 collective-permute-start.14
  14.1 0.6 collective-permute-start.10
  14.8 3.7 %collective-permute-start.4 = (bf16[384,256]{1,0:T(8,128)(2,1)S(1)}, bf16[384,256]{1,0:T(8,128)(2,1)S(1)}, u32[]{:S(2)}, u32[]{:S(2)}) collective-permute-start(bf16[384,256]{1,0:T(8,128)(2,1)S(1)} %pad_maximum_fusion.1), channel_id=1, source_target_pairs={{0,16},{8,24},{16,0},{24,8},{1,17},{9,25},{17,1},{25,9},{2,18},{10... | collective-permute-start | bytes 589832 | tf_op jit(solution)/shard_map/ppermute | solution.py:27
  18.9 1.0 collective-permute-start.1
  19.9 1.2 %collective-permute-done.14 = bf16[384,256]{1,0:T(8,128)(2,1)S(1)} collective-permute-done((bf16[384,256]{1,0:T(8,128)(2,1)S(1)}, bf16[384,256]{1,0:T(8,128)(2,1)S(1)}, u32[]{:S(2)}, u32[]{:S(2)}) %collective-permute-start.14) | collective-permute-done | bytes 196640 | tf_op jit(solution)/shard_map/ppermute | solution.py:27
  21.2 3.8 %collective-permute-start.15 = (bf16[768,256]{1,0:T(8,128)(2,1)S(1)}, bf16[768,256]{1,0:T(8,128)(2,1)S(1)}, u32[]{:S(2)}, u32[]{:S(2)}) collective-permute-start(bf16[768,256]{1,0:T(8,128)(2,1)S(1)} %constant_dynamic-update-slice_fusion.7.refs_7_), channel_id=1, source_target_pairs={{0,24},{8,0},{16,8},{24,16},{1,25},{9,1},{17,9},{25,17},{2,26},{10... | collective-permute-start | bytes 1179656 | tf_op jit(solution)/shard_map/ppermute | solution.py:27
  25.2 2.8 %collective-permute-start.17 = (bf16[192,512]{1,0:T(8,128)(2,1)S(1)}, bf16[192,512]{1,0:T(8,128)(2,1)S(1)}, u32[]{:S(2)}, u32[]{:S(2)}) collective-permute-start(bf16[192,512]{1,0:T(8,128)(2,1)S(1)} %get-tuple-element.42), channel_id=1, source_target_pairs={{0,2},{2,4},{4,6},{6,0},{1,3},{3,5},{5,7},{7,1},{8,10},{10,12},{12... | collective-permute-start | bytes 589832 | tf_op jit(solution)/shard_map/ppermute | solution.py:27
  28.0 2.6 %collective-permute-start.18 = (bf16[192,512]{1,0:T(8,128)(2,1)S(1)}, bf16[192,512]{1,0:T(8,128)(2,1)S(1)}, u32[]{:S(2)}, u32[]{:S(2)}) collective-permute-start(bf16[192,512]{1,0:T(8,128)(2,1)S(1)} %get-tuple-element.44), channel_id=1, source_target_pairs={{0,4},{2,6},{4,0},{6,2},{1,5},{3,7},{5,1},{7,3},{8,12},{10,14},{12... | collective-permute-start | bytes 589832 | tf_op jit(solution)/shard_map/ppermute | solution.py:27
  30.6 1.3 %collective-permute-start.19 = (bf16[192,512]{1,0:T(8,128)(2,1)S(1)}, bf16[192,512]{1,0:T(8,128)(2,1)S(1)}, u32[]{:S(2)}, u32[]{:S(2)}) collective-permute-start(bf16[192,512]{1,0:T(8,128)(2,1)S(1)} %get-tuple-element.41), channel_id=1, source_target_pairs={{0,6},{2,0},{4,2},{6,4},{1,7},{3,1},{5,3},{7,5},{8,14},{10,8},{12,... | collective-permute-start | bytes 589832 | tf_op jit(solution)/shard_map/ppermute | solution.py:27
  31.9 0.8 collective-permute-done.17.refs_9_
  32.8 0.7 copy-done.1
  33.4 4.1 %collective-permute-done.18.refs_10_ = bf16[192,512]{1,0:T(8,128)(2,1)S(1)} collective-permute-done((bf16[192,512]{1,0:T(8,128)(2,1)S(1)}, bf16[192,512]{1,0:T(8,128)(2,1)S(1)}, u32[]{:S(2)}, u32[]{:S(2)}) %collective-permute-start.18) | collective-permute-done | bytes 196640 | tf_op jit(solution)/shard_map/ppermute | solution.py:27
  37.6 0.7 copy-done.3
  38.2 2.4 %collective-permute-start.23 = (bf16[768,256]{1,0:T(8,128)(2,1)S(1)}, bf16[768,256]{1,0:T(8,128)(2,1)}, u32[]{:S(2)}, u32[]{:S(2)}) collective-permute-start(bf16[768,256]{1,0:T(8,128)(2,1)S(1)} %constant_dynamic-update-slice_fusion.4.refs_6_), channel_id=1, source_target_pairs={{0,24},{8,0},{16,8},{24,16},{1,25},{9,1},{17,9},{25,17},{2,26},{10... | collective-permute-start | bytes 1179656 | tf_op jit(solution)/shard_map/ppermute | solution.py:27
  40.6 0.7 copy-done.5
  41.3 4.8 %collective-permute-start.6 = (bf16[768,256]{1,0:T(8,128)(2,1)S(1)}, bf16[768,256]{1,0:T(8,128)(2,1)S(1)}, u32[]{:S(2)}, u32[]{:S(2)}) collective-permute-start(bf16[768,256]{1,0:T(8,128)(2,1)S(1)} %constant_dynamic-update-slice_fusion.refs_5_), channel_id=1, source_target_pairs={{0,96},{32,0},{64,32},{96,64},{1,97},{33,1},{65,33},{97,65},{2,98}... | collective-permute-start | bytes 1179656 | tf_op jit(solution)/shard_map/ppermute | solution.py:27
  46.8 0.9 convert_reduce_fusion.1
  47.7 1.0 convert_reduce_fusion.refs_2_
  48.7 3.6 %collective-permute-done.6.refs_5_ = bf16[768,256]{1,0:T(8,128)(2,1)S(1)} collective-permute-done((bf16[768,256]{1,0:T(8,128)(2,1)S(1)}, bf16[768,256]{1,0:T(8,128)(2,1)S(1)}, u32[]{:S(2)}, u32[]{:S(2)}) %collective-permute-start.6) | collective-permute-done | bytes 393248 | tf_op jit(solution)/shard_map/ppermute | solution.py:27
  52.3 3.4 %collective-permute-start.21 = (bf16[768,256]{1,0:T(8,128)(2,1)S(1)}, bf16[768,256]{1,0:T(8,128)(2,1)S(1)}, u32[]{:S(2)}, u32[]{:S(2)}) collective-permute-start(bf16[768,256]{1,0:T(8,128)(2,1)S(1)} %pad_maximum_fusion.refs_4_), channel_id=1, source_target_pairs={{0,96},{32,0},{64,32},{96,64},{1,97},{33,1},{65,33},{97,65},{2,98}... | collective-permute-start | bytes 1179656 | tf_op jit(solution)/shard_map/ppermute | solution.py:27
  55.8 8.2 %collective-permute-done.2.refs_4_ = bf16[768,256]{1,0:T(8,128)(2,1)} collective-permute-done((bf16[768,256]{1,0:T(8,128)(2,1)S(1)}, bf16[768,256]{1,0:T(8,128)(2,1)}, u32[]{:S(2)}, u32[]{:S(2)}) %collective-permute-start.2) | collective-permute-done | bytes 393248 | tf_op jit(solution)/shard_map/ppermute | solution.py:27
  64.3 1.2 %collective-permute-start.12 = (bf16[768,256]{1,0:T(8,128)(2,1)S(1)}, bf16[768,256]{1,0:T(8,128)(2,1)S(1)}, u32[]{:S(2)}, u32[]{:S(2)}) collective-permute-start(bf16[768,256]{1,0:T(8,128)(2,1)S(1)} %collective-permute-done.11.refs_6_), channel_id=1, source_target_pairs={{0,8},{8,16},{16,24},{24,0},{1,9},{9,17},{17,25},{25,1},{2,10},{10... | collective-permute-start | bytes 1179656 | tf_op jit(solution)/shard_map/ppermute | solution.py:27
  65.5 1.5 %collective-permute-start.3 = (bf16[768,256]{1,0:T(8,128)(2,1)}, bf16[768,256]{1,0:T(8,128)(2,1)S(1)}, u32[]{:S(2)}, u32[]{:S(2)}) collective-permute-start(bf16[768,256]{1,0:T(8,128)(2,1)} %collective-permute-done.2.refs_4_), channel_id=1, source_target_pairs={{0,32},{32,64},{64,96},{96,0},{1,33},{33,65},{65,97},{97,1},{2,34}... | collective-permute-start | bytes 1179656 | tf_op jit(solution)/shard_map/ppermute | solution.py:27
  67.0 0.9 copy-done.2
  67.9 0.9 copy-done.4
  68.8 0.9 copy-done.6
  69.7 6.6 %shard_map.64 = (bf16[8,384,256]{2,1,0:T(8,128)(2,1)S(1)}, f32[8,384,128]{2,1,0:T(8,128)S(1)}, f32[8,384,256]{2,1,0:T(8,128)S(1)}, bf16[2048,4096]{1,0:T(8,128)(2,1)S(1)}) custom-call(s32[4]{0:T(128)S(1)} %pad_add_fusion.refs_0_.coords, s32[128]{0:T(128)S(1)} %copy-done.7, s32[8]{0:T(128)S(1)} %convert_reduce_fusion.refs_2_, ...), custom_call_target="tpu_custom_call" | custom-call | flops 2000000000 | bytes 2500000 | tf_op jit(solution)/shard_map/pallas_call | solution.py:241
  76.3 4.5 %shard_map.65 = (f32[8,384,128]{2,1,0:T(8,128)S(1)}, f32[8,384,256]{2,1,0:T(8,128)S(1)}) custom-call(s32[4]{0:T(128)S(1)} %pad_add_fusion.refs_0_.coords, s32[128]{0:T(128)S(1)} %copy-done.7, s32[8]{0:T(128)S(1)} %convert_reduce_fusion.refs_2_, s32[136]{0:T(256)S(1)} %get-tuple-element.35.refs_3_, ...), custom_call_target="tpu_custom_call", output_to_operand_aliasing={{0}: (9, {}), {1}: (10, {})} | custom-call | flops 2000000000 | bytes 2500000 | tf_op jit(solution)/shard_map/pallas_call | solution.py:241
  80.8 4.5 %shard_map.66 = (f32[8,384,128]{2,1,0:T(8,128)S(1)}, f32[8,384,256]{2,1,0:T(8,128)S(1)}) custom-call(s32[4]{0:T(128)S(1)} %pad_add_fusion.refs_0_.coords, s32[128]{0:T(128)S(1)} %copy-done.7, s32[8]{0:T(128)S(1)} %convert_reduce_fusion.refs_2_, s32[136]{0:T(256)S(1)} %get-tuple-element.36.refs_3_, ...), custom_call_target="tpu_custom_call", output_to_operand_aliasing={{0}: (9, {}), {1}: (10, {})} | custom-call | flops 2000000000 | bytes 2500000 | tf_op jit(solution)/shard_map/pallas_call | solution.py:241
  85.4 4.1 %shard_map.67 = (f32[8,384,128]{2,1,0:T(8,128)S(1)}, f32[8,384,256]{2,1,0:T(8,128)S(1)}, bf16[96,512]{1,0:T(8,128)(2,1)S(1)}, bf16[96,512]{1,0:T(8,128)(2,1)S(1)...) custom-call(s32[4]{0:T(128)S(1)} %pad_add_fusion.refs_0_.coords, ...), custom_call_target="tpu_custom_call", output_to_operand_aliasing={{0}: (9, {}), {1}: (10, {})} | custom-call | flops 2000000000 | bytes 2500000 | tf_op jit(solution)/shard_map/pallas_call | solution.py:241
  89.8 3.9 %collective-permute-start.27 = (bf16[96,512]{1,0:T(8,128)(2,1)S(1)}, bf16[96,512]{1,0:T(8,128)(2,1)S(1)}, u32[]{:S(2)}, u32[]{:S(2)}) collective-permute-start(bf16[96,512]{1,0:T(8,128)(2,1)S(1)} %get-tuple-element.33), channel_id=1, source_target_pairs={{0,6},{2,0},{4,2},{6,4},{1,7},{3,1},{5,3},{7,5},{8,14},{10,8},{12,... | collective-permute-start | bytes 294920 | tf_op jit(solution)/shard_map/ppermute | solution.py:27
  93.7 1.6 %shard_map.68.refs_1_ = f32[192,4096]{1,0:T(8,128)S(1)} custom-call(s32[4]{0:T(128)S(1)} %pad_add_fusion.refs_0_.coords, bf16[96,512]{1,0:T(8,128)(2,1)S(1)} %get-tuple-element.27.theirs, bf16[96,512]{1,0:T(8,128)(2,1)S(1)} %get-tuple-element.28.ours, bf16[2048,4096]{1,0:T(8,128)(2,1)S(1)} %get-tuple-element.29.w.refs_5_), custom_call_target="tpu_custom_call" | custom-call | flops 1610612736 | bytes 16777216 | tf_op jit(solution)/shard_map/pallas_call | solution.py:285
  95.3 1.4 %collective-permute-done.27.refs_2_ = bf16[96,512]{1,0:T(8,128)(2,1)S(1)} collective-permute-done((bf16[96,512]{1,0:T(8,128)(2,1)S(1)}, bf16[96,512]{1,0:T(8,128)(2,1)S(1)}, u32[]{:S(2)}, u32[]{:S(2)}) %collective-permute-start.27) | collective-permute-done | bytes 98336 | tf_op jit(solution)/shard_map/ppermute | solution.py:27
  96.7 1.6 %collective-permute-done.28.refs_4_ = bf16[96,512]{1,0:T(8,128)(2,1)S(1)} collective-permute-done((bf16[96,512]{1,0:T(8,128)(2,1)S(1)}, bf16[96,512]{1,0:T(8,128)(2,1)S(1)}, u32[]{:S(2)}, u32[]{:S(2)}) %collective-permute-start.28) | collective-permute-done | bytes 98336 | tf_op jit(solution)/shard_map/ppermute | solution.py:27
  98.4 2.7 %shard_map.70 = bf16[96,4096]{1,0:T(8,128)(2,1)S(1)} custom-call(s32[4]{0:T(128)S(1)} %pad_add_fusion.refs_0_.coords, f32[192,4096]{1,0:T(8,128)S(1)} %shard_map.68.refs_1_, bf16[96,512]{1,0:T(8,128)(2,1)S(1)} %collective-permute-done.27.refs_2_, bf16[192,512]{1,0:T(8,128)(2,1)S(1)} %collective-permute-done.25.refs_3_, ...), custom_call_target="tpu_custom_call" | custom-call | flops 1610612736 | bytes 16777216 | tf_op jit(solution)/shard_map/pallas_call | solution.py:285
  101.0 4.3 %collective-permute-start.29 = (bf16[96,4096]{1,0:T(8,128)(2,1)S(1)}, bf16[96,4096]{1,0:T(8,128)(2,1)S(1)}, u32[]{:S(2)}, u32[]{:S(2)}) collective-permute-start(bf16[96,4096]{1,0:T(8,128)(2,1)S(1)} %shard_map.70), channel_id=1, source_target_pairs={{0,1},{1,0},{2,3},{3,2},{4,5},{5,4},{6,7},{7,6},{8,9},{9,8},{10,11... | collective-permute-start | bytes 2359304 | tf_op jit(solution)/shard_map/ppermute | solution.py:354
  105.5 1.3 %collective-permute-start.26 = (bf16[96,512]{1,0:T(8,128)(2,1)S(1)}, bf16[96,512]{1,0:T(8,128)(2,1)S(1)}, u32[]{:S(2)}, u32[]{:S(2)}) collective-permute-start(bf16[96,512]{1,0:T(8,128)(2,1)S(1)} %get-tuple-element.32), channel_id=1, source_target_pairs={{0,2},{2,4},{4,6},{6,0},{1,3},{3,5},{5,7},{7,1},{8,10},{10,12},{12... | collective-permute-start | bytes 294920 | tf_op jit(solution)/shard_map/ppermute | solution.py:27
  106.8 2.8 %collective-permute-done.24.refs_2_ = bf16[96,512]{1,0:T(8,128)(2,1)S(1)} collective-permute-done((bf16[96,512]{1,0:T(8,128)(2,1)S(1)}, bf16[96,512]{1,0:T(8,128)(2,1)S(1)}, u32[]{:S(2)}, u32[]{:S(2)}) %collective-permute-start.24) | collective-permute-done | bytes 98336 | tf_op jit(solution)/shard_map/ppermute | solution.py:27
  109.6 1.1 collective-permute-done.26.refs_4_
  110.7 2.7 %shard_map.69 = f32[96,4096]{1,0:T(8,128)S(1)} custom-call(s32[4]{0:T(128)S(1)} %pad_add_fusion.refs_0_.coords, f32[192,4096]{1,0:T(8,128)S(1)} %shard_map.68.refs_1_, bf16[96,512]{1,0:T(8,128)(2,1)S(1)} %collective-permute-done.24.refs_2_, bf16[192,512]{1,0:T(8,128)(2,1)S(1)} %collective-permute-done.25.refs_3_, ...), custom_call_target="tpu_custom_call" | custom-call | flops 1610612736 | bytes 16777216 | tf_op jit(solution)/shard_map/pallas_call | solution.py:285
  113.4 1.0 add_convert_fusion
  (56 shorter events, 3.0 us)
Async XLA Ops:
  0.0 0.9 copy-start
  0.0 13.1 %copy-start.8 = (bf16[192,2048]{1,0:T(8,128)(2,1)S(1)}, bf16[192,2048]{1,0:T(8,128)(2,1)}, u32[]{:S(2)}) copy-start(bf16[192,2048]{1,0:T(8,128)(2,1)} %param.6) | copy-start | bytes 2359300
  2.0 5.8 %collective-permute-start.8 = (bf16[192,256]{1,0:T(8,128)(2,1)S(1)}, bf16[192,256]{1,0:T(8,128)(2,1)S(1)}, u32[]{:S(2)}, u32[]{:S(2)}) collective-permute-start(bf16[192,256]{1,0:T(8,128)(2,1)S(1)} %get-tuple-element.46), channel_id=1, source_target_pairs={{0,4},{2,6},{4,0},{6,2},{1,5},{3,7},{5,1},{7,3},{8,12},{10,14},{12... | collective-permute-start | bytes 294920 | tf_op jit(solution)/shard_map/ppermute | solution.py:27
  5.8 4.4 %collective-permute-start.9 = (bf16[192,256]{1,0:T(8,128)(2,1)S(1)}, bf16[192,256]{1,0:T(8,128)(2,1)S(1)}, u32[]{:S(2)}, u32[]{:S(2)}) collective-permute-start(bf16[192,256]{1,0:T(8,128)(2,1)S(1)} %get-tuple-element.45), channel_id=1, source_target_pairs={{0,6},{2,0},{4,2},{6,4},{1,7},{3,1},{5,3},{7,5},{8,14},{10,8},{12,... | collective-permute-start | bytes 294920 | tf_op jit(solution)/shard_map/ppermute | solution.py:27
  6.6 8.1 %collective-permute-start = (bf16[192,256]{1,0:T(8,128)(2,1)S(1)}, bf16[192,256]{1,0:T(8,128)(2,1)S(1)}, u32[]{:S(2)}, u32[]{:S(2)}) collective-permute-start(bf16[192,256]{1,0:T(8,128)(2,1)S(1)} %get-tuple-element.47), channel_id=1, source_target_pairs={{0,2},{2,4},{4,6},{6,0},{1,3},{3,5},{5,7},{7,1},{8,10},{10,12},{12... | collective-permute-start | bytes 294920 | tf_op jit(solution)/shard_map/ppermute | solution.py:27
  10.3 8.6 %collective-permute-start.13 = (bf16[384,256]{1,0:T(8,128)(2,1)S(1)}, bf16[384,256]{1,0:T(8,128)(2,1)S(1)}, u32[]{:S(2)}, u32[]{:S(2)}) collective-permute-start(bf16[384,256]{1,0:T(8,128)(2,1)S(1)} %get-tuple-element.49), channel_id=1, source_target_pairs={{0,64},{32,96},{64,0},{96,32},{1,65},{33,97},{65,1},{97,33},{2,66}... | collective-permute-start | bytes 589832 | tf_op jit(solution)/shard_map/ppermute | solution.py:27
  13.2 7.9 %collective-permute-start.14 = (bf16[384,256]{1,0:T(8,128)(2,1)S(1)}, bf16[384,256]{1,0:T(8,128)(2,1)S(1)}, u32[]{:S(2)}, u32[]{:S(2)}) collective-permute-start(bf16[384,256]{1,0:T(8,128)(2,1)S(1)} %get-tuple-element.49), channel_id=1, source_target_pairs={{0,96},{32,0},{64,32},{96,64},{1,97},{33,1},{65,33},{97,65},{2,98}... | collective-permute-start | bytes 589832 | tf_op jit(solution)/shard_map/ppermute | solution.py:27
  14.1 10.9 %collective-permute-start.10 = (bf16[384,256]{1,0:T(8,128)(2,1)S(1)}, bf16[384,256]{1,0:T(8,128)(2,1)S(1)}, u32[]{:S(2)}, u32[]{:S(2)}) collective-permute-start(bf16[384,256]{1,0:T(8,128)(2,1)S(1)} %get-tuple-element.49), channel_id=1, source_target_pairs={{0,32},{32,64},{64,96},{96,0},{1,33},{33,65},{65,97},{97,1},{2,34}... | collective-permute-start | bytes 589832 | tf_op jit(solution)/shard_map/ppermute | solution.py:27
  14.8 32.1 %copy-start.7 = (s32[128]{0:T(128)S(1)}, s32[128]{0:T(128)}, u32[]{:S(2)}) copy-start(s32[128]{0:T(128)} %refs_1_.7) | copy-start | bytes 1540
  14.8 10.4 %collective-permute-start.4 = (bf16[384,256]{1,0:T(8,128)(2,1)S(1)}, bf16[384,256]{1,0:T(8,128)(2,1)S(1)}, u32[]{:S(2)}, u32[]{:S(2)}) collective-permute-start(bf16[384,256]{1,0:T(8,128)(2,1)S(1)} %pad_maximum_fusion.1), channel_id=1, source_target_pairs={{0,16},{8,24},{16,0},{24,8},{1,17},{9,25},{17,1},{25,9},{2,18},{10... | collective-permute-start | bytes 589832 | tf_op jit(solution)/shard_map/ppermute | solution.py:27
  18.5 9.5 %collective-permute-start.5 = (bf16[384,256]{1,0:T(8,128)(2,1)S(1)}, bf16[384,256]{1,0:T(8,128)(2,1)S(1)}, u32[]{:S(2)}, u32[]{:S(2)}) collective-permute-start(bf16[384,256]{1,0:T(8,128)(2,1)S(1)} %pad_maximum_fusion.1), channel_id=1, source_target_pairs={{0,24},{8,0},{16,8},{24,16},{1,25},{9,1},{17,9},{25,17},{2,26},{10... | collective-permute-start | bytes 589832 | tf_op jit(solution)/shard_map/ppermute | solution.py:27
  18.9 11.7 %collective-permute-start.1 = (bf16[384,256]{1,0:T(8,128)(2,1)S(1)}, bf16[384,256]{1,0:T(8,128)(2,1)S(1)}, u32[]{:S(2)}, u32[]{:S(2)}) collective-permute-start(bf16[384,256]{1,0:T(8,128)(2,1)S(1)} %pad_maximum_fusion.1), channel_id=1, source_target_pairs={{0,8},{8,16},{16,24},{24,0},{1,9},{9,17},{17,25},{25,1},{2,10},{10... | collective-permute-start | bytes 589832 | tf_op jit(solution)/shard_map/ppermute | solution.py:27
  21.2 24.9 %collective-permute-start.15 = (bf16[768,256]{1,0:T(8,128)(2,1)S(1)}, bf16[768,256]{1,0:T(8,128)(2,1)S(1)}, u32[]{:S(2)}, u32[]{:S(2)}) collective-permute-start(bf16[768,256]{1,0:T(8,128)(2,1)S(1)} %constant_dynamic-update-slice_fusion.7.refs_7_), channel_id=1, source_target_pairs={{0,24},{8,0},{16,8},{24,16},{1,25},{9,1},{17,9},{25,17},{2,26},{10... | collective-permute-start | bytes 1179656 | tf_op jit(solution)/shard_map/ppermute | solution.py:27
  25.0 21.0 %collective-permute-start.11 = (bf16[768,256]{1,0:T(8,128)(2,1)S(1)}, bf16[768,256]{1,0:T(8,128)(2,1)S(1)}, u32[]{:S(2)}, u32[]{:S(2)}) collective-permute-start(bf16[768,256]{1,0:T(8,128)(2,1)S(1)} %constant_dynamic-update-slice_fusion.4.refs_6_), channel_id=1, source_target_pairs={{0,8},{8,16},{16,24},{24,0},{1,9},{9,17},{17,25},{25,1},{2,10},{10... | collective-permute-start | bytes 1179656 | tf_op jit(solution)/shard_map/ppermute | solution.py:27
  25.2 7.6 %collective-permute-start.17 = (bf16[192,512]{1,0:T(8,128)(2,1)S(1)}, bf16[192,512]{1,0:T(8,128)(2,1)S(1)}, u32[]{:S(2)}, u32[]{:S(2)}) collective-permute-start(bf16[192,512]{1,0:T(8,128)(2,1)S(1)} %get-tuple-element.42), channel_id=1, source_target_pairs={{0,2},{2,4},{4,6},{6,0},{1,3},{3,5},{5,7},{7,1},{8,10},{10,12},{12... | collective-permute-start | bytes 589832 | tf_op jit(solution)/shard_map/ppermute | solution.py:27
  28.0 9.6 %collective-permute-start.18 = (bf16[192,512]{1,0:T(8,128)(2,1)S(1)}, bf16[192,512]{1,0:T(8,128)(2,1)S(1)}, u32[]{:S(2)}, u32[]{:S(2)}) collective-permute-start(bf16[192,512]{1,0:T(8,128)(2,1)S(1)} %get-tuple-element.44), channel_id=1, source_target_pairs={{0,4},{2,6},{4,0},{6,2},{1,5},{3,7},{5,1},{7,3},{8,12},{10,14},{12... | collective-permute-start | bytes 589832 | tf_op jit(solution)/shard_map/ppermute | solution.py:27
  30.6 10.0 %collective-permute-start.19 = (bf16[192,512]{1,0:T(8,128)(2,1)S(1)}, bf16[192,512]{1,0:T(8,128)(2,1)S(1)}, u32[]{:S(2)}, u32[]{:S(2)}) collective-permute-start(bf16[192,512]{1,0:T(8,128)(2,1)S(1)} %get-tuple-element.41), channel_id=1, source_target_pairs={{0,6},{2,0},{4,2},{6,4},{1,7},{3,1},{5,3},{7,5},{8,14},{10,8},{12,... | collective-permute-start | bytes 589832 | tf_op jit(solution)/shard_map/ppermute | solution.py:27
  32.8 0.7 copy-start.1
  33.4 30.9 %collective-permute-start.22 = (bf16[768,256]{1,0:T(8,128)(2,1)S(1)}, bf16[768,256]{1,0:T(8,128)(2,1)S(1)}, u32[]{:S(2)}, u32[]{:S(2)}) collective-permute-start(bf16[768,256]{1,0:T(8,128)(2,1)S(1)} %constant_dynamic-update-slice_fusion.7.refs_7_), channel_id=1, source_target_pairs={{0,8},{8,16},{16,24},{24,0},{1,9},{9,17},{17,25},{25,1},{2,10},{10... | collective-permute-start | bytes 1179656 | tf_op jit(solution)/shard_map/ppermute | solution.py:27
  37.6 0.7 copy-start.3
  38.2 27.2 %collective-permute-start.23 = (bf16[768,256]{1,0:T(8,128)(2,1)S(1)}, bf16[768,256]{1,0:T(8,128)(2,1)}, u32[]{:S(2)}, u32[]{:S(2)}) collective-permute-start(bf16[768,256]{1,0:T(8,128)(2,1)S(1)} %constant_dynamic-update-slice_fusion.4.refs_6_), channel_id=1, source_target_pairs={{0,24},{8,0},{16,8},{24,16},{1,25},{9,1},{17,9},{25,17},{2,26},{10... | collective-permute-start | bytes 1179656 | tf_op jit(solution)/shard_map/ppermute | solution.py:27
  40.6 0.7 copy-start.5
  41.3 11.1 %collective-permute-start.6 = (bf16[768,256]{1,0:T(8,128)(2,1)S(1)}, bf16[768,256]{1,0:T(8,128)(2,1)S(1)}, u32[]{:S(2)}, u32[]{:S(2)}) collective-permute-start(bf16[768,256]{1,0:T(8,128)(2,1)S(1)} %constant_dynamic-update-slice_fusion.refs_5_), channel_id=1, source_target_pairs={{0,96},{32,0},{64,32},{96,64},{1,97},{33,1},{65,33},{97,65},{2,98}... | collective-permute-start | bytes 1179656 | tf_op jit(solution)/shard_map/ppermute | solution.py:27
  46.1 19.4 %collective-permute-start.20 = (bf16[768,256]{1,0:T(8,128)(2,1)S(1)}, bf16[768,256]{1,0:T(8,128)(2,1)}, u32[]{:S(2)}, u32[]{:S(2)}) collective-permute-start(bf16[768,256]{1,0:T(8,128)(2,1)S(1)} %constant_dynamic-update-slice_fusion.refs_5_), channel_id=1, source_target_pairs={{0,32},{32,64},{64,96},{96,0},{1,33},{33,65},{65,97},{97,1},{2,34}... | collective-permute-start | bytes 1179656 | tf_op jit(solution)/shard_map/ppermute | solution.py:27
  46.1 17.9 %collective-permute-start.2 = (bf16[768,256]{1,0:T(8,128)(2,1)S(1)}, bf16[768,256]{1,0:T(8,128)(2,1)}, u32[]{:S(2)}, u32[]{:S(2)}) collective-permute-start(bf16[768,256]{1,0:T(8,128)(2,1)S(1)} %pad_maximum_fusion.refs_4_), channel_id=1, source_target_pairs={{0,32},{32,64},{64,96},{96,0},{1,33},{33,65},{65,97},{97,1},{2,34}... | collective-permute-start | bytes 1179656 | tf_op jit(solution)/shard_map/ppermute | solution.py:27
  52.3 28.5 %collective-permute-start.21 = (bf16[768,256]{1,0:T(8,128)(2,1)S(1)}, bf16[768,256]{1,0:T(8,128)(2,1)S(1)}, u32[]{:S(2)}, u32[]{:S(2)}) collective-permute-start(bf16[768,256]{1,0:T(8,128)(2,1)S(1)} %pad_maximum_fusion.refs_4_), channel_id=1, source_target_pairs={{0,96},{32,0},{64,32},{96,64},{1,97},{33,1},{65,33},{97,65},{2,98}... | collective-permute-start | bytes 1179656 | tf_op jit(solution)/shard_map/ppermute | solution.py:27
  64.0 21.3 %collective-permute-start.16 = (bf16[768,256]{1,0:T(8,128)(2,1)S(1)}, bf16[768,256]{1,0:T(8,128)(2,1)S(1)}, u32[]{:S(2)}, u32[]{:S(2)}) collective-permute-start(bf16[768,256]{1,0:T(8,128)(2,1)S(1)} %collective-permute-done.15.refs_7_), channel_id=1, source_target_pairs={{0,24},{8,0},{16,8},{24,16},{1,25},{9,1},{17,9},{25,17},{2,26},{10... | collective-permute-start | bytes 1179656 | tf_op jit(solution)/shard_map/ppermute | solution.py:27
  64.3 21.0 %collective-permute-start.12 = (bf16[768,256]{1,0:T(8,128)(2,1)S(1)}, bf16[768,256]{1,0:T(8,128)(2,1)S(1)}, u32[]{:S(2)}, u32[]{:S(2)}) collective-permute-start(bf16[768,256]{1,0:T(8,128)(2,1)S(1)} %collective-permute-done.11.refs_6_), channel_id=1, source_target_pairs={{0,8},{8,16},{16,24},{24,0},{1,9},{9,17},{17,25},{25,1},{2,10},{10... | collective-permute-start | bytes 1179656 | tf_op jit(solution)/shard_map/ppermute | solution.py:27
  65.5 19.9 %collective-permute-start.7 = (bf16[768,256]{1,0:T(8,128)(2,1)S(1)}, bf16[768,256]{1,0:T(8,128)(2,1)S(1)}, u32[]{:S(2)}, u32[]{:S(2)}) collective-permute-start(bf16[768,256]{1,0:T(8,128)(2,1)S(1)} %collective-permute-done.6.refs_5_), channel_id=1, source_target_pairs={{0,96},{32,0},{64,32},{96,64},{1,97},{33,1},{65,33},{97,65},{2,98}... | collective-permute-start | bytes 1179656 | tf_op jit(solution)/shard_map/ppermute | solution.py:27
  65.5 19.9 %collective-permute-start.3 = (bf16[768,256]{1,0:T(8,128)(2,1)}, bf16[768,256]{1,0:T(8,128)(2,1)S(1)}, u32[]{:S(2)}, u32[]{:S(2)}) collective-permute-start(bf16[768,256]{1,0:T(8,128)(2,1)} %collective-permute-done.2.refs_4_), channel_id=1, source_target_pairs={{0,32},{32,64},{64,96},{96,0},{1,33},{33,65},{65,97},{97,1},{2,34}... | collective-permute-start | bytes 1179656 | tf_op jit(solution)/shard_map/ppermute | solution.py:27
  67.0 0.9 copy-start.2
  67.9 0.9 copy-start.4
  68.8 0.9 copy-start.6
  89.5 8.8 %collective-permute-start.25 = (bf16[192,512]{1,0:T(8,128)(2,1)S(1)}, bf16[192,512]{1,0:T(8,128)(2,1)S(1)}, u32[]{:S(2)}, u32[]{:S(2)}) collective-permute-start(bf16[192,512]{1,0:T(8,128)(2,1)S(1)} %get-tuple-element.31), channel_id=1, source_target_pairs={{0,4},{2,6},{4,0},{6,2},{1,5},{3,7},{5,1},{7,3},{8,12},{10,14},{12... | collective-permute-start | bytes 589832 | tf_op jit(solution)/shard_map/ppermute | solution.py:27
  89.8 6.9 %collective-permute-start.27 = (bf16[96,512]{1,0:T(8,128)(2,1)S(1)}, bf16[96,512]{1,0:T(8,128)(2,1)S(1)}, u32[]{:S(2)}, u32[]{:S(2)}) collective-permute-start(bf16[96,512]{1,0:T(8,128)(2,1)S(1)} %get-tuple-element.33), channel_id=1, source_target_pairs={{0,6},{2,0},{4,2},{6,4},{1,7},{3,1},{5,3},{7,5},{8,14},{10,8},{12,... | collective-permute-start | bytes 294920 | tf_op jit(solution)/shard_map/ppermute | solution.py:27
  93.7 4.7 %collective-permute-start.28 = (bf16[96,512]{1,0:T(8,128)(2,1)S(1)}, bf16[96,512]{1,0:T(8,128)(2,1)S(1)}, u32[]{:S(2)}, u32[]{:S(2)}) collective-permute-start(bf16[96,512]{1,0:T(8,128)(2,1)S(1)} %get-tuple-element.34), channel_id=1, source_target_pairs={{0,2},{2,4},{4,6},{6,0},{1,3},{3,5},{5,7},{7,1},{8,10},{10,12},{12... | collective-permute-start | bytes 294920 | tf_op jit(solution)/shard_map/ppermute | solution.py:27
  101.0 12.3 %collective-permute-start.29 = (bf16[96,4096]{1,0:T(8,128)(2,1)S(1)}, bf16[96,4096]{1,0:T(8,128)(2,1)S(1)}, u32[]{:S(2)}, u32[]{:S(2)}) collective-permute-start(bf16[96,4096]{1,0:T(8,128)(2,1)S(1)} %shard_map.70), channel_id=1, source_target_pairs={{0,1},{1,0},{2,3},{3,2},{4,5},{5,4},{6,7},{7,6},{8,9},{9,8},{10,11... | collective-permute-start | bytes 2359304 | tf_op jit(solution)/shard_map/ppermute | solution.py:354
  105.3 4.3 %collective-permute-start.24 = (bf16[96,512]{1,0:T(8,128)(2,1)S(1)}, bf16[96,512]{1,0:T(8,128)(2,1)S(1)}, u32[]{:S(2)}, u32[]{:S(2)}) collective-permute-start(bf16[96,512]{1,0:T(8,128)(2,1)S(1)} %get-tuple-element.30), channel_id=1, source_target_pairs={{0,6},{2,0},{4,2},{6,4},{1,7},{3,1},{5,3},{7,5},{8,14},{10,8},{12,... | collective-permute-start | bytes 294920 | tf_op jit(solution)/shard_map/ppermute | solution.py:27
  105.5 5.2 %collective-permute-start.26 = (bf16[96,512]{1,0:T(8,128)(2,1)S(1)}, bf16[96,512]{1,0:T(8,128)(2,1)S(1)}, u32[]{:S(2)}, u32[]{:S(2)}) collective-permute-start(bf16[96,512]{1,0:T(8,128)(2,1)S(1)} %get-tuple-element.32), channel_id=1, source_target_pairs={{0,2},{2,4},{4,6},{6,0},{1,3},{3,5},{5,7},{7,1},{8,10},{10,12},{12... | collective-permute-start | bytes 294920 | tf_op jit(solution)/shard_map/ppermute | solution.py:27
